TPU v7x, 256 devices: a whole 4x4x8 slice. The times are simulated.
256 devices in a mesh: row: 32 (over y, x, core), col: 8 (over z).
Axes of the slice: x: 4, y: 4, z: 8, core: 2. Of those that a mesh axis runs over, the one named last changes fastest.
Arguments:
- item_factors: bfloat16 [32768, 128], P(('row', 'col')), may hold values from -0.5 to 0.5
- item_index: int32 [2048, 8192], P('col', 'row'), may hold values from 0 to 1023
- ratings: bfloat16 [2048, 8192], P('col', 'row'), may hold values from -4 to 4
- counts: int32 [2048, 32], P('col', 'row'), may hold values from 1 to 256, as said below
Outputs:
- user_factors: float32 [8, 256, 128], P('col', 'row')
Inputs may be any that keep to these rules, and one draw needn't show every extreme that they name: `counts`: for each user block and item block, some user has exactly 256 live slots.
All inputs are finite; a program needn't handle non-finite values.
Results may differ from a plain program's by a relative error of at most 0.0004.
Values may be sent and summed in bfloat16 or wider, within the bound.
No kernel may reach another device: no remote copies, remote signals or barrier semaphores. Data moves between devices by JAX's collectives and lax.ppermute only.
A program may use at most 192 MiB of HBM per device.

v0:
```python
import jax
import jax.numpy as jnp
from jax import lax
from jax.sharding import PartitionSpec as P


def laid_out(tiles, dim):
    dims = list(tiles.shape[1:])
    dims[dim] *= tiles.shape[0]
    return jnp.moveaxis(tiles, 0, dim).reshape(dims)


def copy_for_each(shard, axis):
    copies = jnp.broadcast_to(shard, (lax.axis_size(axis), *shard.shape))
    return lax.all_to_all(copies, axis, split_axis=0, concat_axis=0, tiled=True)


def collect(shard, axis, dim):
    return laid_out(copy_for_each(shard, axis), dim)


def split_up(shard, dim, count):
    before, after = (shard.shape[:dim], shard.shape[dim + 1 :])
    return jnp.moveaxis(shard.reshape(*before, count, -1, *after), dim, 0)


def sum_packed(arrays, axis, dims):
    count = lax.axis_size(axis)
    tiles = [split_up(a, dim, count) for a, dim in zip(arrays, dims)]
    lines = jnp.concatenate([b.reshape(count, -1) for b in tiles], axis=1)
    span = max(16, -(-lines.shape[1] // 1024) * 8)
    lines = jnp.pad(lines, ((0, 0), (0, span * 128 - lines.shape[1]))).reshape(-1, 128)
    flat, at, gathered = (lax.psum_scatter(lines, axis, tiled=True).reshape(-1), 0, [])
    for b in tiles:
        part = b[0]
        gathered.append(flat[at : at + part.size].reshape(part.shape))
        at += part.size
    return tuple(gathered)


def solve_users(normal_sum, right_side, number):
    width_rank = normal_sum.shape[-1]
    shifted = normal_sum + (0.1 * number / width_rank)[:, None, None] * jnp.eye(
        width_rank, dtype=jnp.float32
    )
    factor_low = jnp.linalg.cholesky(shifted)
    middle = jax.scipy.linalg.solve_triangular(factor_low, right_side[:, :, None], lower=True)
    answer = jax.scipy.linalg.solve_triangular(factor_low, middle, lower=True, trans=1)
    return answer[:, :, 0]


def per_device(item_factors, item_index, ratings, counts):
    item_block = collect(item_factors, "col", 0)
    position = lax.broadcasted_iota(jnp.int32, item_index.shape, 1)
    live_slot = (position < counts).astype(jnp.bfloat16)
    chosen = jnp.take(item_block, item_index, axis=0)
    weighted = chosen * live_slot[:, :, None]
    scaled = ratings * live_slot
    normal_part = jnp.einsum("usa,usb->uab", weighted, weighted, preferred_element_type=jnp.float32)
    right_part = jnp.einsum("us,usa->ua", scaled, weighted, preferred_element_type=jnp.float32)
    number_part = counts[:, 0].astype(jnp.float32)
    normal_sum, right_side, number = sum_packed(
        (normal_part, right_part, number_part), "row", (0, 0, 0)
    )
    answer = solve_users(normal_sum, right_side, number)
    return answer[None]


def solution(mesh):
    return jax.shard_map(
        per_device,
        mesh=mesh,
        in_specs=(P(("row", "col"), None), P("col", "row"), P("col", "row"), P("col", "row")),
        out_specs=P("col", "row", None),
        check_vma=False,
    )
```

profile of v0, /device:TPU:2, one launch (start us, length us, event | category | flops | bytes accessed | tf_op | source)
XLA Modules:
  0.0 660.2 jit_solution(11361669655385659169)
XLA Ops:
  6.5 1.5 broadcast_in_dim.23
  8.0 8.5 %all-to-all-start = ((bf16[8,128,128]{2,1,0:T(8,128)(2,1)}), bf16[8,128,128]{2,1,0:T(8,128)(2,1)S(1)}, u32[]{:S(2)}, u32[]{:S(2)}) async-start(bf16[8,128,128]{2,1,0:T(8,128)(2,1)} %broadcast_in_dim.23), calls=%async_computation | async-start | bytes 524288 | tf_op jit(solution)/shard_map/all_to_all | solution.py:15
  16.5 0.0 reduce-scatter.2.cloned.1.call-start
  16.5 1.0 fusion.13
  17.5 0.1 copy.26
  17.7 0.7 convert_reduce_fusion
  18.4 0.1 convert_element_type.25
  18.5 1.0 fusion.14
  19.5 1.1 fusion.12
  20.6 7.8 %all-to-all-done = bf16[8,128,128]{2,1,0:T(8,128)(2,1)S(1)} async-done(((bf16[8,128,128]{2,1,0:T(8,128)(2,1)}), bf16[8,128,128]{2,1,0:T(8,128)(2,1)S(1)}, u32[]{:S(2)}, u32[]{:S(2)}) %all-to-all-start) | async-done | bytes 262176 | tf_op jit(solution)/shard_map/all_to_all | solution.py:15
  28.4 227.3 %gather_fusion = bf16[65536,128]{1,0:T(8,128)(2,1)} fusion(bf16[1024,128]{1,0:T(8,128)(2,1)S(1)} %bitcast.37, s32[65536]{0:T(1024)S(1)} %broadcast_clamp_fusion), kind=kCustom, calls=%fused_computation | custom fusion | bytes 33816576 | tf_op jit(solution)/shard_map/jit(_take)/gather | solution.py:56
  255.7 22.4 %copy.14 = bf16[256,256,128]{1,2,0:T(8,128)(2,1)} copy(bf16[256,256,128]{2,1,0:T(8,128)(2,1)} %bitcast.38) | data formatting | bytes 33554432 | tf_op jit(solution)/shard_map/jit(_take)/gather | solution.py:56
  278.1 21.2 %fusion.1 = f32[256,128,128]{2,1,0:T(8,128)} fusion(bf16[256,256,128]{1,2,0:T(8,128)(2,1)} %copy.14, pred[256,256]{1,0:T(8,128)(4,1)S(1)} %get-tuple-element.6, bf16[256,256]{1,0:T(8,128)(2,1)S(1)} %get-tuple-element.5), kind=kOutput, calls=%fused_computation.6 | convolution fusion | flops 2164260864 | bytes 33751040 | tf_op jit(solution)/shard_map/usa,usb->uab/dot_general | solution.py:59
  299.3 10.2 %fusion = f32[256,1,128]{2,1,0:T(1,128)S(1)} fusion(bf16[256,256,128]{1,2,0:T(8,128)(2,1)} %copy.14, pred[256,256]{1,0:T(8,128)(4,1)S(1)} %get-tuple-element.6, bf16[256,256]{1,0:T(8,128)(2,1)S(1)} %get-tuple-element.5, bf16[256,256,1]{1,0,2:T(8,128)(2,1)S(1)} %fusion.14), kind=kOutput, calls=%fused_computation.5 | convolution fusion | flops 33554432 | bytes 17235968 | tf_op jit(solution)/shard_map/us,usa->ua/dot_general | solution.py:60
  309.6 12.1 %reshape_reshape.6 = f32[32,131072]{1,0:T(8,128)} reshape(f32[256,128,128]{2,1,0:T(8,128)} %fusion.1) | data formatting | bytes 33554432 | tf_op jit(solution)/shard_map/reshape;reshape | solution.py:30
  321.6 13.6 %select_maximum_fusion = f32[32,133120]{1,0:T(8,128)} fusion(f32[32,8]{1,0:T(8,128)S(1)} %convert_element_type.25, f32[32,1024]{1,0:T(8,128)S(1)} %reshape_reshape.7, f32[32,131072]{1,0:T(8,128)} %reshape_reshape.6), kind=kLoop, calls=%fused_computation.1 | loop fusion | flops 25559040 | bytes 33948672 | tf_op jit(solution)/shard_map/concatenate | solution.py:30
  335.2 19.3 %reshape.76 = f32[33280,128]{1,0:T(8,128)} reshape(f32[32,133120]{1,0:T(8,128)} %select_maximum_fusion) | data formatting | bytes 34078720 | tf_op jit(solution)/shard_map/reshape | solution.py:32
  354.5 0.0 reduce-scatter.2.cloned.1.call-update
  354.5 0.1 copy.16
  354.7 120.6 %reduce-scatter.2.cloned.1.call-done = f32[1040,128]{1,0:T(8,128)} async-done(((f32[33280,128]{1,0:T(8,128)}), f32[1040,128]{1,0:T(8,128)}) %reduce-scatter.2.cloned.1.call-update) | async-done | bytes 532496 | tf_op jit(solution)/shard_map/reduce_scatter | solution.py:33
  475.3 1.1 slice.34
  476.4 0.2 copy.17
  476.6 0.7 slice_multiply_fusion
  477.3 0.1 multiply_add_fusion
  477.4 0.2 copy.18
  477.6 0.1 fusion.9
  477.7 94.0 %custom-call.11 = f32[8,128,128]{2,1,0:T(8,128)S(1)} custom-call(f32[8,128,128]{2,1,0:T(8,128)S(1)} %fusion.9), custom_call_target="Cholesky" | custom-call | tf_op jit(solution)/shard_map/jit(cholesky)/cholesky | solution.py:46
  571.7 0.1 select_reduce_fusion
  571.7 0.1 compare_reduce_fusion
  571.9 0.1 select_bitcast_fusion
  572.0 78.6 %custom-call.12 = f32[8,1,128,128]{2,3,1,0:T(8,128)S(1)} custom-call(f32[8,1,128,128]{3,2,1,0:T(8,128)S(1)} %select_bitcast_fusion), custom_call_target="InvertDiagBlocksLowerTriangular" | custom-call | tf_op jit(solution)/shard_map/jit(_solve_triangular)/vmap()/triangular_solve | solution.py:48
  650.6 0.7 slice.36
  651.3 0.6 convolution_bitcast_fusion
  651.8 1.5 fusion.6
  (5 shorter events, 0.1 us)
Async XLA Ops:
  8.0 20.3 %all-to-all-start = ((bf16[8,128,128]{2,1,0:T(8,128)(2,1)}), bf16[8,128,128]{2,1,0:T(8,128)(2,1)S(1)}, u32[]{:S(2)}, u32[]{:S(2)}) async-start(bf16[8,128,128]{2,1,0:T(8,128)(2,1)} %broadcast_in_dim.23), calls=%async_computation | async-start | bytes 524288 | tf_op jit(solution)/shard_map/all_to_all | solution.py:15
  16.5 458.8 %reduce-scatter.2.cloned.1.call-start = ((), (), s32[]{:S(2)}) async-start(), calls=%async_computation.2 | async-start | bytes 17571840 | tf_op jit(solution)/shard_map/reduce_scatter | solution.py:33
Sparse Core Ops, SparseCore 0:
  354.6 120.6 reduce-scatter.1
where the time goes:
time: 661 us; the launch traced here: 660 us
  local copies, waits for them, and re-layouts  285 us (43%)
  other arithmetic  191 us (29%)
  waiting for transfers between devices  128 us (19%)
  matrix products  33.5 us (5%)
  between operations  13.5 us (2%)
  starting transfers between devices  8.5 us (1%)
    gather x2, local copies, waits for them, and re-layouts, per_device(): chosen = jnp.take(item_block, item_index, axis=0)  250 us
    reduce_scatter x1, waiting for transfers between devices, sum_packed(): lax.psum_scatter(lines, axis, tiled=True).reshape(-1)  121 us
    another operation x4, other arithmetic, solve_users(): factor_low = jnp.linalg.cholesky(shifted)  94.1 us
    another operation x3, other arithmetic, solve_users(): jax.scipy.linalg.solve_triangular(factor_low, middle, lower=True, trans=1)  78.7 us
    dot_general x1, matrix products, per_device(): jnp.einsum('usa,usb->uab', weighted, weighted, preferred_element_type=jnp...  21.2 us
    reshape x1, local copies, waits for them, and re-layouts, sum_packed(): jnp.pad(lines, ((0, 0), (0, span * 128 - lines.shape[1]))).reshape(-1, 128)  19.3 us
    concatenate x1, other arithmetic, sum_packed(): lines = jnp.concatenate([b.reshape(count, -1) for b in tiles], axis=1)  13.6 us
  transfers between devices with their start and end apart: 2, of which 2 were waited for; matrix products, arithmetic and copies ran while one was open for 1% of the time, Pallas kernels for 0%

commit v1 on v0

v1 whole, which is shorter than its diff:
```python
import functools

import jax
import jax.numpy as jnp
from jax import lax
from jax.experimental import pallas as pl
from jax.experimental.pallas import tpu as pltpu
from jax.sharding import PartitionSpec as P

F32, BF16 = jnp.float32, jnp.bfloat16
LOW = 256
PANEL = 8
ROWS_TO_ROWS = (((1,), (1,)), ((), ()))


def gram_kernel(code_ref, table_ref, gram_ref, code_s, rows_s, *, slots, rank):
    users = code_s.shape[0]
    shards = table_ref.shape[1]
    per = LOW // table_ref.shape[3]
    parts = shards // per

    @pl.when(pl.program_id(0) == 0)
    def _():
        gram_ref[...] = jnp.zeros(gram_ref.shape, F32)

    code_s[...] = code_ref[0].astype(F32)
    table = jnp.concatenate(
        [jnp.concatenate([table_ref[0, per * h + q] for q in range(per)], axis=1) for h in range(parts)], axis=0
    )
    row_ids = lax.broadcasted_iota(jnp.int32, (LOW, slots), 0).astype(F32).astype(BF16)
    one, zero = jnp.ones((), BF16), jnp.zeros((), BF16)
    for u in range(users):
        row = code_s[u : u + 1, :]
        low = jnp.broadcast_to(row[:, :slots], (16, slots)).astype(BF16)
        low = jnp.concatenate([low] * (LOW // 16), axis=0)
        found = jnp.dot(table, jnp.where(row_ids == low, one, zero), preferred_element_type=F32)
        high = jnp.broadcast_to(row[:, slots : 2 * slots], (rank, slots))
        rows = jnp.zeros((rank, slots), F32)
        for h in range(parts):
            rows = jnp.where(high == h, found[h * rank : (h + 1) * rank], rows)
        rows_s[u, :rank] = rows.astype(BF16)
        rows_s[u, rank:] = jnp.broadcast_to(row[:, 2 * slots :], (16, slots)).astype(BF16)
    for u in range(users):
        both = rows_s[u]
        out = lax.dot_general(both, both[:rank], ROWS_TO_ROWS, preferred_element_type=F32)
        gram_ref[u] += out[: rank + 8]


def gram(code, table, slots):
    blocks, users, _ = code.shape
    _, shards, rank, items = table.shape
    return pl.pallas_call(
        functools.partial(gram_kernel, slots=slots, rank=rank),
        grid=(blocks,),
        in_specs=[
            pl.BlockSpec((1, users, 3 * slots), lambda k: (k, 0, 0)),
            pl.BlockSpec((1, shards, rank, items), lambda k: (k, 0, 0, 0)),
        ],
        out_specs=pl.BlockSpec((users, rank + 8, rank), lambda k: (0, 0, 0)),
        out_shape=jax.ShapeDtypeStruct((users, rank + 8, rank), F32),
        scratch_shapes=[pltpu.VMEM((users, 3 * slots), F32), pltpu.VMEM((users, rank + 16, slots), BF16)],
        name="gram",
    )(code, table)


def solve_kernel(gram_ref, number_ref, out_ref, rows_s):
    users, rank = out_ref.shape
    lane = lax.broadcasted_iota(jnp.int32, (users, rank), 1)
    shift = 0.1 * number_ref[...] / rank
    for i in range(rank):
        row = gram_ref[:, i, :]
        rows_s[i] = jnp.where(lane == i, row + shift, row)
    right = gram_ref[:, rank, :]

    def lane_of(value, i):
        return jnp.broadcast_to(value[:, i : i + 1], (users, rank))

    answer = jnp.zeros((users, rank), F32)
    for start in range(0, rank, PANEL):
        steps = range(PANEL)
        rows = [rows_s[start + t] for t in steps]
        corner = {(t, s): lane_of(rows[s], start + t) for t in steps for s in range(t + 1)}
        middle = [lane_of(right, start + t) for t in steps]
        inside = (lane >= start) & (lane < start + PANEL)
        rows = [jnp.where(inside, jnp.where(lane == start + t, 1.0, 0.0), rows[t]) for t in steps]
        inverse = []
        for s in steps:
            inverse.append(1.0 / corner[s, s])
            for t in range(s + 1, PANEL):
                factor = corner[t, s] * inverse[s]
                for q in range(s + 1, t + 1):
                    corner[t, q] = corner[t, q] - factor * corner[q, s]
                rows[t] = rows[t] - factor * rows[s]
                middle[t] = middle[t] - factor * middle[s]
        for t in steps:
            scaled = middle[t] * inverse[t]
            answer = answer + jnp.where(lane < start + PANEL, scaled * rows[t], 0.0)
            right = right - scaled * rows[t]
        below = [rows[t] * inverse[t] for t in steps]
        for i in range(start + PANEL, rank):
            row = jnp.where(inside, 0.0, rows_s[i])
            for t in steps:
                row = row - lane_of(below[t], i) * rows[t]
            rows_s[i] = row
    out_ref[...] = answer


def solve(gram_sum, number):
    users, rank = number.shape
    return pl.pallas_call(
        solve_kernel,
        out_shape=jax.ShapeDtypeStruct((users, rank), F32),
        scratch_shapes=[pltpu.VMEM((rank, users, rank), F32)],
        name="solve",
    )(gram_sum, number)


def coded(item_index, ratings, counts):
    position = lax.broadcasted_iota(jnp.int32, item_index.shape, 1)
    dead = LOW
    high = jnp.where(position < counts, item_index // LOW, dead)
    return jnp.concatenate([(item_index % LOW).astype(BF16), high.astype(BF16), ratings], axis=1)


def per_device(item_factors, item_index, ratings, counts):
    slots, rank = item_index.shape[1], item_factors.shape[1]
    n_row, n_col = lax.axis_size("row"), lax.axis_size("col")
    code = coded(item_index, ratings, counts).reshape(n_row, -1, 3 * slots)
    code = lax.all_to_all(code, "row", 0, 0, tiled=True)
    table = lax.all_gather(lax.optimization_barrier(item_factors.T), ("row", "col"))
    table = table.reshape(n_row, n_col, rank, -1)
    number = jnp.sum((code[:, :, slots : 2 * slots] < LOW).astype(F32), axis=(0, 2))
    number = jnp.broadcast_to(number[:, None], (number.shape[0], rank))
    return solve(gram(code, table, slots), number)[None]


def solution(mesh):
    return jax.shard_map(
        per_device,
        mesh=mesh,
        in_specs=(P(("row", "col"), None), P("col", "row"), P("col", "row"), P("col", "row")),
        out_specs=P("col", "row", None),
        check_vma=False,
    )
```

time: 661 us -> 193 us (0.29)
  local copies, waits for them, and re-layouts: 285 us -> 12.6 us
  other arithmetic: 191 us -> 2.33 us
  Pallas kernels: 0 us -> 47.6 us
  matrix products: 33.5 us -> 0 us
  waiting for transfers between devices: 128 us -> 98 us
  blocking collectives: 0 us -> 16.4 us
  starting transfers between devices: 8.5 us -> 0.01 us
    gather x2 -> x0, local copies, waits for them, and re-layouts: 250 us -> none  [per_device(): chosen = jnp.take(item_block, item_index, axis=0)]
    another operation x7 -> x0, other arithmetic: 173 us -> none  [the longest x4 94.1 us: solve_users(): factor_low = jnp.linalg.cholesky(shifted)]
    reduce_scatter x1 -> x0, waiting for transfers between devices: 121 us -> none  [sum_packed(): lax.psum_scatter(lines, axis, tiled=True).reshape(-1)]
    all_gather x0 -> x1, waiting for transfers between devices: none -> 97.3 us  [per_device(): lax.all_gather(lax.optimization_barrier(item_factors.T), ('row', 'col'))]
    pallas_call x0 -> x2, Pallas kernels: none -> 47.6 us  [the longest x1 31.5 us: gram(): pl.pallas_call(functools.partial(gram_kernel, slots=slots, rank=rank), gr...]
    dot_general x2 -> x0, matrix products: 31.4 us -> none  [the longest x1 21.2 us: per_device(): jnp.einsum('usa,usb->uab', weighted, weighted, preferred_element_type=jnp...]
    reshape x2 -> x0, local copies, waits for them, and re-layouts: 19.5 us -> none  [the longest x1 19.3 us: sum_packed(): jnp.pad(lines, ((0, 0), (0, span * 128 - lines.shape[1]))).reshape(-1, 128)]
    all_to_all x0 -> x1, blocking collectives: none -> 16.4 us  [per_device(): code = lax.all_to_all(code, 'row', 0, 0, tiled=True)]
  transfers between devices with their start and end apart: 2 -> 1, of which waited for: 2 -> 1; matrix products, arithmetic and copies ran while one was open for 1% -> 1% of each run, Pallas kernels for 0% -> 0%
where the time goes in v1:
time: 193 us; the launch traced here: 190 us
  waiting for transfers between devices  98 us (51%)
  Pallas kernels  47.6 us (25%)
  blocking collectives  16.4 us (8%)
  between operations  13.4 us (7%)
  local copies, waits for them, and re-layouts  12.6 us (7%)
  other arithmetic  2.33 us (1%)
    all_gather x1, waiting for transfers between devices, per_device(): lax.all_gather(lax.optimization_barrier(item_factors.T), ('row', 'col'))  97.3 us
    pallas_call x1, Pallas kernels, gram(): pl.pallas_call(functools.partial(gram_kernel, slots=slots, rank=rank), gr...  31.5 us
    all_to_all x1, blocking collectives, per_device(): code = lax.all_to_all(code, 'row', 0, 0, tiled=True)  16.4 us
    pallas_call x1, Pallas kernels, solve(): pl.pallas_call(solve_kernel, out_shape=jax.ShapeDtypeStruct((users, rank)...  16.1 us
    all_gather x1, local copies, waits for them, and re-layouts, per_device(): lax.all_gather(lax.optimization_barrier(item_factors.T), ('row', 'col'))  11.9 us
  transfers between devices with their start and end apart: 1, of which 1 were waited for; matrix products, arithmetic and copies ran while one was open for 1% of the time, Pallas kernels for 0%

profile of v1, /device:TPU:2, one launch (start us, length us, event | category | flops | bytes accessed | tf_op | source)
XLA Modules:
  0.0 190.3 jit_solution(17268743135475179513)
XLA Ops:
  6.5 0.0 all-gather.3.cloned.1.call-start
  6.5 0.7 all-gather.3.cloned.1.call-update
  7.3 1.2 fusion
  8.5 0.9 maximum_bitcast_fusion
  9.4 16.4 %all_to_all.5.code_ref = bf16[32,8,768]{2,1,0:T(8,128)(2,1)S(1)} all-to-all(bf16[32,8,768]{2,1,0:T(8,128)(2,1)S(1)} %maximum_bitcast_fusion), channel_id=1, replica_groups=mesh['row'=32,'col'=8] {'row'}, dimensions={0} | all-to-all | bytes 786432 | tf_op jit(solution)/shard_map/all_to_all | solution.py:129
  25.8 0.0 copy-start
  25.8 0.2 convert_reduce_fusion
  26.0 97.3 %all-gather.3.cloned.1.call-done = bf16[32768,128]{0,1:T(8,128)(2,1)} async-done(((bf16[128,128]{0,1:T(8,128)(2,1)}), bf16[32768,128]{0,1:T(8,128)(2,1)}) %all-gather.3.cloned.1.call-update) | async-done | bytes 8388624 | tf_op jit(solution)/shard_map/all_gather | solution.py:130
  123.3 11.9 %copy.5 = bf16[32768,128]{1,0:T(8,128)(2,1)} copy(bf16[32768,128]{0,1:T(8,128)(2,1)} %all-gather.3.cloned.1.call-done) | data formatting | bytes 16777216 | tf_op jit(solution)/shard_map/all_gather | solution.py:130
  135.2 0.0 copy-done
  135.2 31.5 %gram.1.gram_ref = f32[8,136,128]{2,1,0:T(8,128)} custom-call(bf16[32,8,768]{2,1,0:T(8,128)(2,1)} %copy-done, bf16[32,8,128,128]{3,2,1,0:T(8,128)(2,1)} %bitcast.6), custom_call_target="tpu_custom_call" | custom-call | tf_op jit(solution)/shard_map/gram/pallas_call | solution.py:52
  166.8 0.7 broadcast_in_dim.6.number_ref
  167.4 16.1 %solve.1 = f32[8,128]{1,0:T(8,128)} custom-call(f32[8,136,128]{2,1,0:T(8,128)} %gram.1.gram_ref, f32[8,128]{1,0:T(8,128)} %broadcast_in_dim.6.number_ref), custom_call_target="tpu_custom_call" | custom-call | tf_op jit(solution)/shard_map/solve/pallas_call | solution.py:110
Async XLA Ops:
  6.5 116.8 %all-gather.3.cloned.1.call-start = ((), (), s32[]{:S(2)}) async-start(), calls=%async_computation.1 | async-start | bytes 8421376 | tf_op jit(solution)/shard_map/all_gather | solution.py:130
  25.8 109.4 %copy-start = (bf16[32,8,768]{2,1,0:T(8,128)(2,1)}, bf16[32,8,768]{2,1,0:T(8,128)(2,1)S(1)}, u32[]{:S(2)}) copy-start(bf16[32,8,768]{2,1,0:T(8,128)(2,1)S(1)} %all_to_all.5.code_ref) | copy-start | bytes 1179652
Sparse Core Ops, SparseCore 0:
  11.1 112.1 all-gather.2

commit v2 on v1

v2 whole, which is shorter than its diff:
```python
import functools

import jax
import jax.numpy as jnp
import numpy as np
from jax import lax
from jax.experimental import pallas as pl
from jax.experimental.pallas import tpu as pltpu
from jax.sharding import PartitionSpec as P


F32, BF16 = jnp.float32, jnp.bfloat16
LOW = 256
HALF = 128
SIDE = 4
CORES = 2
PANEL = 8
ROWS_TO_ROWS = (((1,), (1,)), ((), ()))


def gram_kernel(source_ref, code_ref, *refs, counts, first, offset):
    tables = refs[: len(counts)]
    before = refs[len(counts) : -8]
    own_ref, other_ref, table_s, low_s, high_s, rate_s, live_s, rows_s = refs[-8:]
    sums = (own_ref, other_ref)
    users, slots = low_s.shape
    rank = own_ref.shape[2]
    step = pl.program_id(0)

    @pl.when(step == 0)
    def _():
        for n, sum_ref in enumerate(sums):
            sum_ref[...] = jnp.zeros(sum_ref.shape, F32) if first else before[n][...]

    begin = 0
    for table_ref, count in zip(tables, counts):

        @pl.when((step >= begin) & (step < begin + count))
        def _(table_ref=table_ref, begin=begin):
            per = LOW // table_ref.shape[3]
            for z in range(table_ref.shape[1]):
                h, q = z // per, z % per
                table_s[h * rank : (h + 1) * rank, q * 128 : (q + 1) * 128] = table_ref[step - begin, z]

        begin += count

    code = code_ref[source_ref[offset + step]].astype(F32)
    index = code[:, :slots]
    size = jnp.abs(index)
    above = [jnp.where(size >= LOW * 2**e, 1.0, 0.0) for e in range(3)]
    low_s[...] = index * (1.0 - 0.5 * above[0] - 0.25 * above[1] - 0.125 * above[2])
    high_s[...] = above[0] + above[1] + above[2]
    rate_s[...] = code[:, slots:]
    live = jnp.where(size > 0.0, 1.0, 0.0)
    live_s[...] = live[:, : slots // 2] + live[:, slots // 2 :]

    place = lax.broadcasted_iota(jnp.int32, (LOW, slots), 0)
    row_ids = jnp.where(place < HALF, place + HALF, -place).astype(F32).astype(BF16)
    one, zero = jnp.ones((), BF16), jnp.zeros((), BF16)
    table = table_s[...]
    parts = table.shape[0] // rank
    for u in range(users):
        low = jnp.broadcast_to(low_s[u : u + 1], (16, slots)).astype(BF16)
        low = jnp.concatenate([low] * (LOW // 16), axis=0)
        found = jnp.dot(table, jnp.where(row_ids == low, one, zero), preferred_element_type=F32)
        high = jnp.broadcast_to(high_s[u : u + 1], (rank, slots))
        rows = found[:rank]
        for h in range(1, parts):
            rows = jnp.where(high == h, found[h * rank : (h + 1) * rank], rows)
        rows_s[u, :rank] = rows.astype(BF16)
        rows_s[u, rank:] = jnp.broadcast_to(rate_s[u : u + 1], (16, slots)).astype(BF16)
    tail_row = lax.broadcasted_iota(jnp.int32, (8, rank), 0)
    for u in range(users):
        both = rows_s[u]
        out = lax.dot_general(both, both[:rank], ROWS_TO_ROWS, preferred_element_type=F32)
        sum_ref, v = sums[u // (users // CORES)], u % (users // CORES)
        sum_ref[v, :rank] += out[:rank]
        tail = jnp.where(tail_row == 1, jnp.broadcast_to(live_s[u : u + 1], (8, rank)), out[rank : rank + 8])
        sum_ref[v, rank:] += tail


def gram(source, offset, code, tables, before=()):
    _, users, width = code.shape
    slots = width // 2
    rank = tables[0].shape[2]
    counts = [t.shape[0] for t in tables]
    out = jax.ShapeDtypeStruct((users // CORES, rank + 8, rank), F32)
    whole = pl.BlockSpec(memory_space=pltpu.VMEM)
    operands = [code, *tables, *before]
    pairs = users * sum(counts)
    return pl.pallas_call(
        functools.partial(gram_kernel, counts=counts, first=not before, offset=offset),
        grid_spec=pltpu.PrefetchScalarGridSpec(
            num_scalar_prefetch=1,
            grid=(sum(counts),),
            in_specs=[whole for x in operands],
            out_specs=[whole, whole],
            scratch_shapes=[
                pltpu.VMEM((4 * rank, LOW), BF16),
                pltpu.VMEM((users, slots), F32),
                pltpu.VMEM((users, slots), F32),
                pltpu.VMEM((users, slots), F32),
                pltpu.VMEM((users, slots // 2), F32),
                pltpu.VMEM((users, rank + 16, slots), BF16),
            ],
        ),
        out_shape=[out, out],
        cost_estimate=pl.CostEstimate(
            flops=pairs * 2 * slots * (4 * LOW + rank) * rank, transcendentals=0, bytes_accessed=4 * pairs * slots
        ),
        name="gram",
    )(source, *operands)


def solve_kernel(own_ref, other_ref, out_ref, rows_s):
    users, rank = out_ref.shape
    lane = lax.broadcasted_iota(jnp.int32, (users, rank), 1)
    number = jnp.sum(own_ref[:, rank + 1, :] + other_ref[:, rank + 1, :], axis=1, keepdims=True)
    shift = jnp.broadcast_to(0.1 * number / rank, (users, rank))
    for i in range(rank):
        row = own_ref[:, i, :] + other_ref[:, i, :]
        rows_s[i] = jnp.where(lane == i, row + shift, row)
    right = own_ref[:, rank, :] + other_ref[:, rank, :]

    def lane_of(value, i):
        return jnp.broadcast_to(value[:, i : i + 1], (users, rank))

    answer = jnp.zeros((users, rank), F32)
    for start in range(0, rank, PANEL):
        steps = range(PANEL)
        rows = [rows_s[start + t] for t in steps]
        corner = {(t, s): lane_of(rows[s], start + t) for t in steps for s in range(t + 1)}
        middle = [lane_of(right, start + t) for t in steps]
        inside = (lane >= start) & (lane < start + PANEL)
        rows = [jnp.where(inside, jnp.where(lane == start + t, 1.0, 0.0), rows[t]) for t in steps]
        inverse = []
        for s in steps:
            inverse.append(1.0 / corner[s, s])
            for t in range(s + 1, PANEL):
                factor = corner[t, s] * inverse[s]
                for q in range(s + 1, t + 1):
                    corner[t, q] = corner[t, q] - factor * corner[q, s]
                rows[t] = rows[t] - factor * rows[s]
                middle[t] = middle[t] - factor * middle[s]
        for t in steps:
            scaled = middle[t] * inverse[t]
            answer = answer + jnp.where(lane < start + PANEL, scaled * rows[t], 0.0)
            right = right - scaled * rows[t]
        below = [rows[t] * inverse[t] for t in steps]
        for i in range(start + PANEL, rank):
            row = jnp.where(inside, 0.0, rows_s[i])
            for t in steps:
                row = row - lane_of(below[t], i) * rows[t]
            rows_s[i] = row
    out_ref[...] = answer


def solve(own, other):
    users, _, rank = own.shape
    return pl.pallas_call(
        solve_kernel,
        out_shape=jax.ShapeDtypeStruct((users, rank), F32),
        scratch_shapes=[pltpu.VMEM((rank, users, rank), F32)],
        name="solve",
    )(own, other)


def coded(item_index, counts):
    low = item_index % LOW
    value = jnp.where(low < HALF, low + HALF, -low) * (1 << (item_index // LOW))
    position = lax.broadcasted_iota(jnp.int32, item_index.shape, 1)
    return jnp.where(position < counts, value, 0).astype(BF16)


def row_at(y, x, core):
    return (y % SIDE * SIDE + x % SIDE) * CORES + core


def shifted(value, first, by):
    pairs = []
    for y in range(SIDE):
        for x in range(SIDE):
            for core in range(CORES):
                along_x = first == (core == 0)
                to = row_at(y, x + by, core) if along_x else row_at(y + by, x, core)
                pairs.append((row_at(y, x, core), to))
    return lax.ppermute(value, "row", pairs)


def ring(value, first):
    half = value.shape[0] // 2
    behind, ahead = shifted(value, first, 1), shifted(value, first, -1)
    return behind, ahead, shifted(behind[:half], first, 1), shifted(ahead[half:], first, -1)


def half_sweep(item_factors, item_index, ratings, counts):
    n_row, n_col = lax.axis_size("row"), lax.axis_size("col")
    chips = n_row // CORES
    slots = item_index.shape[1]
    me = lax.axis_index("row")
    core = me % CORES

    code = jnp.concatenate([coded(item_index, counts), ratings], axis=1).reshape(chips, CORES, -1, 2 * slots)
    code = jnp.where(core == 0, code, code[:, ::-1]).reshape(chips, -1, 2 * slots)
    same_core = [[chip * CORES + c for chip in range(chips)] for c in range(CORES)]
    code = lax.all_to_all(code, "row", 0, 0, tiled=True, axis_index_groups=same_core)

    copies = jnp.broadcast_to(item_factors.T, (n_col, *item_factors.T.shape))
    block = lax.all_to_all(copies, "col", 0, 0, tiled=True)

    source = jnp.asarray(SOURCES)[me]
    behind, ahead, far_low, far_high = ring(block, True)
    near = jnp.stack([block, behind, ahead, jnp.concatenate([far_low, far_high])])
    own, other = gram(source, 0, code, [near])
    behind, ahead, far_low, far_high = ring(near, False)
    own, other = gram(source, 4, code, [behind, ahead], (own, other))
    own, other = gram(source, 12, code, [far_low, far_high], (own, other))
    other = lax.ppermute(other, "row", [(i, i ^ 1) for i in range(n_row)])
    return solve(own, other)[None]


def sources():
    table = np.zeros((SIDE * SIDE * CORES, SIDE * SIDE), np.int32)
    for y in range(SIDE):
        for x in range(SIDE):
            for core in range(CORES):
                for k, (second, first) in enumerate((b, a) for b in (0, -1, 1, 2) for a in (0, -1, 1, 2)):
                    dx, dy = (first, second) if core == 0 else (second, first)
                    table[row_at(y, x, core), k] = (y + dy) % SIDE * SIDE + (x + dx) % SIDE
    return table


SOURCES = sources()


def solution(mesh):
    return jax.shard_map(
        half_sweep,
        mesh=mesh,
        in_specs=(P(("row", "col"), None), P("col", "row"), P("col", "row"), P("col", "row")),
        out_specs=P("col", "row", None),
        check_vma=False,
    )
```

time: 193 us -> 119 us (0.62)
  the two profiles are of different devices: /device:TPU:2 before, /device:TPU:1 now
where the time goes in v2:
time: 119 us
  Pallas kernels  52.7 us (44%)
  starting transfers between devices  22 us (18%)
  blocking collectives  19.3 us (16%)
  waiting for transfers between devices  17.5 us (15%)
  local copies, waits for them, and re-layouts  5.77 us (5%)
  other arithmetic  1.26 us (1%)
    pallas_call x3, Pallas kernels, gram(): pl.pallas_call(functools.partial(gram_kernel, counts=counts, first=not be...  36.4 us
    all_to_all x1, blocking collectives, half_sweep(): block = lax.all_to_all(copies, 'col', 0, 0, tiled=True)  19.3 us
    pallas_call x1, Pallas kernels, solve(): pl.pallas_call(solve_kernel, out_shape=jax.ShapeDtypeStruct((users, rank)...  16.3 us
    ppermute x8, starting transfers between devices, shifted(): return lax.ppermute(value, 'row', pairs)  11.3 us
    all_to_all x1, waiting for transfers between devices, half_sweep(): lax.all_to_all(code, 'row', 0, 0, tiled=True, axis_index_groups=same_core)  9.74 us
    ppermute x8, waiting for transfers between devices, shifted(): return lax.ppermute(value, 'row', pairs)  5.99 us
    ppermute x1, starting transfers between devices, half_sweep(): other = lax.ppermute(other, 'row', [(i, i ^ 1) for i in range(n_row)])  5.56 us
    all_to_all x1, starting transfers between devices, half_sweep(): lax.all_to_all(code, 'row', 0, 0, tiled=True, axis_index_groups=same_core)  5.11 us
  transfers between devices with their start and end apart: 10, of which 4 were waited for; matrix products, arithmetic and copies ran while one was open for 3% of the time, Pallas kernels for 22%

profile of v2, /device:TPU:1, one launch (start us, length us, event | category | flops | bytes accessed | tf_op | source)
XLA Modules:
  0.0 118.6 jit_solution(1408910252031783515)
XLA Ops:
  0.0 0.9 copy.6
  0.9 19.3 %all_to_all.10 = bf16[8,128,128]{2,1,0:T(8,128)(2,1)S(1)} all-to-all(bf16[8,128,128]{2,1,0:T(8,128)(2,1)S(1)} %broadcast_in_dim.8), channel_id=1, replica_groups=mesh['row'=32,'col'=8] {'col'}, dimensions={0} | all-to-all | bytes 524288 | tf_op jit(solution)/shard_map/all_to_all | solution.py:209
  20.2 1.3 %collective-permute-start = (bf16[8,128,128]{2,1,0:T(8,128)(2,1)S(1)}, bf16[8,128,128]{2,1,0:T(8,128)(2,1)S(1)}, u32[]{:S(2)}, u32[]{:S(2)}) collective-permute-start(bf16[8,128,128]{2,1,0:T(8,128)(2,1)S(1)} %all_to_all.10), channel_id=1, source_target_pairs={{0,16},{8,72},{16,32},{24,88},{32,48},{40,104},{48,0},{56,120},{64... | collective-permute-start | bytes 786440 | tf_op jit(solution)/shard_map/ppermute | solution.py:187
  21.5 1.4 %collective-permute-start.1 = (bf16[8,128,128]{2,1,0:T(8,128)(2,1)S(1)}, bf16[8,128,128]{2,1,0:T(8,128)(2,1)S(1)}, u32[]{:S(2)}, u32[]{:S(2)}) collective-permute-start(bf16[8,128,128]{2,1,0:T(8,128)(2,1)S(1)} %all_to_all.10), channel_id=1, source_target_pairs={{0,48},{8,200},{16,0},{24,216},{32,16},{40,232},{48,32},{56,248},{... | collective-permute-start | bytes 786440 | tf_op jit(solution)/shard_map/ppermute | solution.py:187
  23.0 0.0 copy-start.2
  23.0 4.0 %collective-permute-done = bf16[8,128,128]{2,1,0:T(8,128)(2,1)S(1)} collective-permute-done((bf16[8,128,128]{2,1,0:T(8,128)(2,1)S(1)}, bf16[8,128,128]{2,1,0:T(8,128)(2,1)S(1)}, u32[]{:S(2)}, u32[]{:S(2)}) %collective-permute-start) | collective-permute-done | bytes 262176 | tf_op jit(solution)/shard_map/ppermute | solution.py:187
  27.0 0.1 collective-permute-start.2
  27.1 0.0 collective-permute-done.1
  27.1 0.0 copy-start.6
  27.1 2.7 %collective-permute-start.3 = (bf16[4,128,128]{2,1,0:T(8,128)(2,1)S(1)}, bf16[4,128,128]{2,1,0:T(8,128)(2,1)S(1)}, u32[]{:S(2)}, u32[]{:S(2)}) collective-permute-start(bf16[4,128,128]{2,1,0:T(8,128)(2,1)S(1)} %slice.17), channel_id=1, source_target_pairs={{0,48},{8,200},{16,0},{24,216},{32,16},{40,232},{48,32},{56,248},{... | collective-permute-start | bytes 393224 | tf_op jit(solution)/shard_map/ppermute | solution.py:187
  29.9 0.0 copy-done.2
  29.9 0.0 copy-done.6
  29.9 0.3 fusion.3
  30.2 1.9 %collective-permute-done.2 = bf16[4,128,128]{2,1,0:T(8,128)(2,1)S(1)} collective-permute-done((bf16[4,128,128]{2,1,0:T(8,128)(2,1)S(1)}, bf16[4,128,128]{2,1,0:T(8,128)(2,1)S(1)}, u32[]{:S(2)}, u32[]{:S(2)}) %collective-permute-start.2) | collective-permute-done | bytes 131104 | tf_op jit(solution)/shard_map/ppermute | solution.py:187
  32.1 0.0 collective-permute-done.3
  32.2 0.0 copy-start.5
  32.2 0.1 pad_maximum_fusion.refs_0_
  32.3 0.0 copy-start
  32.3 1.0 collective-permute-start.4
  33.3 1.8 %collective-permute-start.6 = (bf16[4,8,128,128]{3,2,1,0:T(8,128)(2,1)S(1)}, bf16[4,8,128,128]{3,2,1,0:T(8,128)(2,1)}, u32[]{:S(2)}, u32[]{:S(2)}) collective-permute-start(bf16[4,8,128,128]{3,2,1,0:T(8,128)(2,1)S(1)} %pad_maximum_fusion.refs_0_), channel_id=1, source_target_pairs={{0,192},{8,56},{16,208},{24,8},{32,224},{40,24},{48,240},{56,40},{... | collective-permute-start | bytes 3145736 | tf_op jit(solution)/shard_map/ppermute | solution.py:187
  35.1 0.0 copy-done.5
  35.1 0.8 fusion.4
  35.9 5.1 %all-to-all-start = ((bf16[16,16,512]{2,1,0:T(8,128)(2,1)}), bf16[16,16,512]{2,1,0:T(8,128)(2,1)S(1)}, u32[]{:S(2)}, u32[]{:S(2)}) async-start(bf16[16,16,512]{2,1,0:T(8,128)(2,1)} %fusion.4), calls=%async_computation | async-start | bytes 524288 | tf_op jit(solution)/shard_map/all_to_all | solution.py:206
  41.0 1.2 %dynamic-slice_bitcast_fusion.source_ref = s32[16]{0:T(128)} fusion(s32[32,16]{1,0:T(8,128)} %constant.53.clone, s32[]{:T(128)S(6)} %select_n.36), kind=kLoop, calls=%fused_computation.18 | loop fusion | bytes 132 | tf_op jit(solution)/shard_map/squeeze | solution.py:211
  42.2 9.7 %all-to-all-done.code_ref = bf16[16,16,512]{2,1,0:T(8,128)(2,1)S(1)} async-done(((bf16[16,16,512]{2,1,0:T(8,128)(2,1)}), bf16[16,16,512]{2,1,0:T(8,128)(2,1)S(1)}, u32[]{:S(2)}, u32[]{:S(2)}) %all-to-all-start) | async-done | bytes 262176 | tf_op jit(solution)/shard_map/all_to_all | solution.py:206
  51.9 0.0 copy-done
  51.9 0.0 copy-start.4
  52.0 0.7 copy-done.4
  52.7 9.5 %gram.3 = (f32[8,136,128]{2,1,0:T(8,128)}, f32[8,136,128]{2,1,0:T(8,128)}) custom-call(s32[16]{0:T(128)} %dynamic-slice_bitcast_fusion.source_ref, bf16[16,16,512]{2,1,0:T(8,128)(2,1)} %copy-done.4, bf16[4,8,128,128]{3,2,1,0:T(8,128)(2,1)} %copy-done), custom_call_target="tpu_custom_call" | custom-call | flops 4831838208 | bytes 65536 | tf_op jit(solution)/shard_map/gram/pallas_call | solution.py:91
  62.2 0.0 collective-permute-done.4.refs_0_
  62.2 0.0 copy-start.3
  62.2 0.9 collective-permute-start.5
  63.2 0.0 collective-permute-done.6.refs_1_
  63.2 1.1 slice.19
  64.3 0.0 copy-done.3
  64.3 2.1 %collective-permute-start.7 = (bf16[2,8,128,128]{3,2,1,0:T(8,128)(2,1)S(1)}, bf16[2,8,128,128]{3,2,1,0:T(8,128)(2,1)S(1)}, u32[]{:S(2)}, u32[]{:S(2)}) collective-permute-start(bf16[2,8,128,128]{3,2,1,0:T(8,128)(2,1)S(1)} %slice.19), channel_id=1, source_target_pairs={{0,192},{8,56},{16,208},{24,8},{32,224},{40,24},{48,240},{56,40},{... | collective-permute-start | bytes 1572872 | tf_op jit(solution)/shard_map/ppermute | solution.py:187
  66.4 16.9 %gram.4 = (f32[8,136,128]{2,1,0:T(8,128)}, f32[8,136,128]{2,1,0:T(8,128)}) custom-call(s32[16]{0:T(128)} %dynamic-slice_bitcast_fusion.source_ref, bf16[16,16,512]{2,1,0:T(8,128)(2,1)} %copy-done.4, bf16[4,8,128,128]{3,2,1,0:T(8,128)(2,1)} %copy-done.3, bf16[4,8,128,128]{3,2,1,0:T(8,128)(2,1)} %collective-permute-done.6.refs_1_, ...), custom_call_target="tpu_custom_call" | custom-call | flops 9663676416 | bytes 131072 | tf_op jit(solution)/shard_map/gram/pallas_call | solution.py:91
  83.3 0.0 collective-permute-done.5.refs_0_
  83.3 0.0 copy-start.7
  83.3 0.0 collective-permute-done.7.refs_1_
  83.3 0.0 copy-start.8
  83.3 0.8 copy-done.7
  84.1 0.2 copy-done.8
  84.3 9.9 %gram.5 = (f32[8,136,128]{2,1,0:T(8,128)}, f32[8,136,128]{2,1,0:T(8,128)}) custom-call(s32[16]{0:T(128)} %dynamic-slice_bitcast_fusion.source_ref, bf16[16,16,512]{2,1,0:T(8,128)(2,1)} %copy-done.4, bf16[2,8,128,128]{3,2,1,0:T(8,128)(2,1)} %copy-done.7, bf16[2,8,128,128]{3,2,1,0:T(8,128)(2,1)} %copy-done.8, f32[8,136,128]{2,1,0:T(8,128)} %get-tuple-element.13.refs_2_, ...), custom_call_target="tpu_custom_call" | custom-call | flops 4831838208 | bytes 65536 | tf_op jit(solution)/shard_map/gram/pallas_call | solution.py:91
  94.2 5.6 %collective-permute-start.8 = (f32[8,136,128]{2,1,0:T(8,128)}, f32[8,136,128]{2,1,0:T(8,128)S(1)}, u32[]{:S(2)}, u32[]{:S(2)}) collective-permute-start(f32[8,136,128]{2,1,0:T(8,128)} %get-tuple-element.16), channel_id=1, source_target_pairs={{0,8},{8,0},{16,24},{24,16},{32,40},{40,32},{48,56},{56,48},{64,72... | collective-permute-start | bytes 1671176 | tf_op jit(solution)/shard_map/ppermute | solution.py:218
  99.8 1.8 %collective-permute-done.8.other_ref = f32[8,136,128]{2,1,0:T(8,128)S(1)} collective-permute-done((f32[8,136,128]{2,1,0:T(8,128)}, f32[8,136,128]{2,1,0:T(8,128)S(1)}, u32[]{:S(2)}, u32[]{:S(2)}) %collective-permute-start.8) | collective-permute-done | bytes 557088 | tf_op jit(solution)/shard_map/ppermute | solution.py:218
  101.5 0.0 copy-start.1
  101.5 0.8 copy-done.1
  102.4 16.3 %solve.1 = f32[8,128]{1,0:T(8,128)} custom-call(f32[8,136,128]{2,1,0:T(8,128)} %get-tuple-element.15.own_ref, f32[8,136,128]{2,1,0:T(8,128)} %copy-done.1), custom_call_target="tpu_custom_call" | custom-call | tf_op jit(solution)/shard_map/solve/pallas_call | solution.py:160
  (6 shorter events, 0.1 us)
Async XLA Ops:
  20.2 6.8 %collective-permute-start = (bf16[8,128,128]{2,1,0:T(8,128)(2,1)S(1)}, bf16[8,128,128]{2,1,0:T(8,128)(2,1)S(1)}, u32[]{:S(2)}, u32[]{:S(2)}) collective-permute-start(bf16[8,128,128]{2,1,0:T(8,128)(2,1)S(1)} %all_to_all.10), channel_id=1, source_target_pairs={{0,16},{8,72},{16,32},{24,88},{32,48},{40,104},{48,0},{56,120},{64... | collective-permute-start | bytes 786440 | tf_op jit(solution)/shard_map/ppermute | solution.py:187
  21.5 5.6 %collective-permute-start.1 = (bf16[8,128,128]{2,1,0:T(8,128)(2,1)S(1)}, bf16[8,128,128]{2,1,0:T(8,128)(2,1)S(1)}, u32[]{:S(2)}, u32[]{:S(2)}) collective-permute-start(bf16[8,128,128]{2,1,0:T(8,128)(2,1)S(1)} %all_to_all.10), channel_id=1, source_target_pairs={{0,48},{8,200},{16,0},{24,216},{32,16},{40,232},{48,32},{56,248},{... | collective-permute-start | bytes 786440 | tf_op jit(solution)/shard_map/ppermute | solution.py:187
  23.0 6.9 %copy-start.2 = (s32[256,256]{1,0:T(8,128)S(1)}, s32[256,256]{1,0:T(8,128)}, u32[]{:S(2)}) copy-start(s32[256,256]{1,0:T(8,128)} %param.6) | copy-start | bytes 786436
  27.0 5.1 %collective-permute-start.2 = (bf16[4,128,128]{2,1,0:T(8,128)(2,1)S(1)}, bf16[4,128,128]{2,1,0:T(8,128)(2,1)S(1)}, u32[]{:S(2)}, u32[]{:S(2)}) collective-permute-start(bf16[4,128,128]{2,1,0:T(8,128)(2,1)S(1)} %slice.16), channel_id=1, source_target_pairs={{0,16},{8,72},{16,32},{24,88},{32,48},{40,104},{48,0},{56,120},{64... | collective-permute-start | bytes 393224 | tf_op jit(solution)/shard_map/ppermute | solution.py:187
  27.1 2.7 %copy-start.6 = (s32[256,1]{0,1:T(1,128)S(1)}, s32[256,1]{0,1:T(1,128)}, u32[]{:S(2)}) copy-start(s32[256,1]{0,1:T(1,128)} %param.8) | copy-start | bytes 3076
  27.1 5.0 %collective-permute-start.3 = (bf16[4,128,128]{2,1,0:T(8,128)(2,1)S(1)}, bf16[4,128,128]{2,1,0:T(8,128)(2,1)S(1)}, u32[]{:S(2)}, u32[]{:S(2)}) collective-permute-start(bf16[4,128,128]{2,1,0:T(8,128)(2,1)S(1)} %slice.17), channel_id=1, source_target_pairs={{0,48},{8,200},{16,0},{24,216},{32,16},{40,232},{48,32},{56,248},{... | collective-permute-start | bytes 393224 | tf_op jit(solution)/shard_map/ppermute | solution.py:187
  32.2 2.9 %copy-start.5 = (bf16[256,256]{1,0:T(8,128)(2,1)S(1)}, bf16[256,256]{1,0:T(8,128)(2,1)}, u32[]{:S(2)}) copy-start(bf16[256,256]{1,0:T(8,128)(2,1)} %param.7) | copy-start | bytes 393220
  32.3 19.6 %copy-start = (bf16[4,8,128,128]{3,2,1,0:T(8,128)(2,1)}, bf16[4,8,128,128]{3,2,1,0:T(8,128)(2,1)S(1)}, u32[]{:S(2)}) copy-start(bf16[4,8,128,128]{3,2,1,0:T(8,128)(2,1)S(1)} %pad_maximum_fusion.refs_0_) | copy-start | bytes 3145732
  32.3 29.9 %collective-permute-start.4 = (bf16[4,8,128,128]{3,2,1,0:T(8,128)(2,1)S(1)}, bf16[4,8,128,128]{3,2,1,0:T(8,128)(2,1)S(1)}, u32[]{:S(2)}, u32[]{:S(2)}) collective-permute-start(bf16[4,8,128,128]{3,2,1,0:T(8,128)(2,1)S(1)} %pad_maximum_fusion.refs_0_), channel_id=1, source_target_pairs={{0,64},{8,24},{16,80},{24,40},{32,96},{40,56},{48,112},{56,8},{64,... | collective-permute-start | bytes 3145736 | tf_op jit(solution)/shard_map/ppermute | solution.py:187
  33.3 29.9 %collective-permute-start.6 = (bf16[4,8,128,128]{3,2,1,0:T(8,128)(2,1)S(1)}, bf16[4,8,128,128]{3,2,1,0:T(8,128)(2,1)}, u32[]{:S(2)}, u32[]{:S(2)}) collective-permute-start(bf16[4,8,128,128]{3,2,1,0:T(8,128)(2,1)S(1)} %pad_maximum_fusion.refs_0_), channel_id=1, source_target_pairs={{0,192},{8,56},{16,208},{24,8},{32,224},{40,24},{48,240},{56,40},{... | collective-permute-start | bytes 3145736 | tf_op jit(solution)/shard_map/ppermute | solution.py:187
  35.9 16.1 %all-to-all-start = ((bf16[16,16,512]{2,1,0:T(8,128)(2,1)}), bf16[16,16,512]{2,1,0:T(8,128)(2,1)S(1)}, u32[]{:S(2)}, u32[]{:S(2)}) async-start(bf16[16,16,512]{2,1,0:T(8,128)(2,1)} %fusion.4), calls=%async_computation | async-start | bytes 524288 | tf_op jit(solution)/shard_map/all_to_all | solution.py:206
  51.9 0.7 copy-start.4
  62.2 2.1 %copy-start.3 = (bf16[4,8,128,128]{3,2,1,0:T(8,128)(2,1)}, bf16[4,8,128,128]{3,2,1,0:T(8,128)(2,1)S(1)}, u32[]{:S(2)}) copy-start(bf16[4,8,128,128]{3,2,1,0:T(8,128)(2,1)S(1)} %collective-permute-done.4.refs_0_) | copy-start | bytes 3145732
  62.2 21.0 %collective-permute-start.5 = (bf16[2,8,128,128]{3,2,1,0:T(8,128)(2,1)S(1)}, bf16[2,8,128,128]{3,2,1,0:T(8,128)(2,1)S(1)}, u32[]{:S(2)}, u32[]{:S(2)}) collective-permute-start(bf16[2,8,128,128]{3,2,1,0:T(8,128)(2,1)S(1)} %slice.18), channel_id=1, source_target_pairs={{0,64},{8,24},{16,80},{24,40},{32,96},{40,56},{48,112},{56,8},{64,... | collective-permute-start | bytes 1572872 | tf_op jit(solution)/shard_map/ppermute | solution.py:187
  64.3 19.0 %collective-permute-start.7 = (bf16[2,8,128,128]{3,2,1,0:T(8,128)(2,1)S(1)}, bf16[2,8,128,128]{3,2,1,0:T(8,128)(2,1)S(1)}, u32[]{:S(2)}, u32[]{:S(2)}) collective-permute-start(bf16[2,8,128,128]{3,2,1,0:T(8,128)(2,1)S(1)} %slice.19), channel_id=1, source_target_pairs={{0,192},{8,56},{16,208},{24,8},{32,224},{40,24},{48,240},{56,40},{... | collective-permute-start | bytes 1572872 | tf_op jit(solution)/shard_map/ppermute | solution.py:187
  83.3 0.8 copy-start.7
  83.3 1.0 copy-start.8
  94.2 7.4 %collective-permute-start.8 = (f32[8,136,128]{2,1,0:T(8,128)}, f32[8,136,128]{2,1,0:T(8,128)S(1)}, u32[]{:S(2)}, u32[]{:S(2)}) collective-permute-start(f32[8,136,128]{2,1,0:T(8,128)} %get-tuple-element.16), channel_id=1, source_target_pairs={{0,8},{8,0},{16,24},{24,16},{32,40},{40,32},{48,56},{56,48},{64,72... | collective-permute-start | bytes 1671176 | tf_op jit(solution)/shard_map/ppermute | solution.py:218
  101.5 0.8 copy-start.1

commit v3 on v2

v3 whole, which is shorter than its diff:
```python
import functools

import jax
import jax.numpy as jnp
from jax import lax
from jax.experimental import pallas as pl
from jax.experimental.pallas import tpu as pltpu
from jax.sharding import PartitionSpec as P


F32, BF16 = jnp.float32, jnp.bfloat16
LOW = 256
HALF = 128
SIDE = 4
CORES = 2
PANEL = 8
BLOCK = 32
VMEM_BYTES = 16 << 20
ROWS_TO_ROWS = (((1,), (1,)), ((), ()))
COLS_TO_COLS = (((0,), (0,)), ((), ()))


def in_vmem(value):
    return pltpu.with_memory_space_constraint(value, pltpu.VMEM)


def chip_of(me, k):
    core, x, y = me & 1, (me >> 1) & (SIDE - 1), me >> 3

    def away(n):
        return jnp.where(n == 1, -1, jnp.where(n == 2, 1, jnp.where(n == 3, 2, 0)))

    first, second = away(k & 3), away(k >> 2)
    dx, dy = jnp.where(core == 0, first, second), jnp.where(core == 0, second, first)
    return ((y + dy) & (SIDE - 1)) * SIDE + ((x + dx) & (SIDE - 1))


def gram_kernel(me_ref, code_ref, *refs, counts, groups, first, offset):
    tables = refs[: len(counts)]
    before = refs[len(counts) : -6 - len(groups)]
    sums = refs[-6 - len(groups) : -6]
    table_s, low_s, high_s, rate_s, live_s, rows_s = refs[-6:]
    users, slots = low_s.shape
    share = users // len(groups)
    rank = sums[0].shape[2]
    step = pl.program_id(0)

    @pl.when(step == 0)
    def _():
        for n, sum_ref in enumerate(sums):
            sum_ref[...] = jnp.zeros(sum_ref.shape, F32) if first else before[n][...]

    begin = 0
    for table_ref, count in zip(tables, counts):

        @pl.when((step >= begin) & (step < begin + count))
        def _(table_ref=table_ref, begin=begin):
            per = LOW // table_ref.shape[3]
            for z in range(table_ref.shape[1]):
                h, q = z // per, z % per
                table_s[h * rank : (h + 1) * rank, q * 128 : (q + 1) * 128] = table_ref[step - begin, z]

        begin += count

    code = code_ref[chip_of(me_ref[0], offset + step)].astype(F32)
    code = jnp.concatenate([code[n * share : (n + 1) * share] for n in groups], axis=0)
    index = code[:, :slots]
    size = jnp.abs(index)
    above = [jnp.where(size >= LOW * 2**e, 1.0, 0.0) for e in range(3)]
    low_s[...] = index * (1.0 - 0.5 * above[0] - 0.25 * above[1] - 0.125 * above[2])
    high_s[...] = above[0] + above[1] + above[2]
    rate_s[...] = code[:, slots:]
    live = jnp.where(size > 0.0, 1.0, 0.0)
    live_s[...] = live[:, : slots // 2] + live[:, slots // 2 :]

    place = lax.broadcasted_iota(jnp.int32, (LOW, slots), 0)
    row_ids = jnp.where(place < HALF, place + HALF, -place).astype(F32).astype(BF16)
    one, zero = jnp.ones((), BF16), jnp.zeros((), BF16)
    table = table_s[...]
    parts = table.shape[0] // rank
    for u in range(users):
        low = jnp.broadcast_to(low_s[u : u + 1], (16, slots)).astype(BF16)
        low = jnp.concatenate([low] * (LOW // 16), axis=0)
        found = jnp.dot(table, jnp.where(row_ids == low, one, zero), preferred_element_type=F32)
        high = jnp.broadcast_to(high_s[u : u + 1], (rank, slots))
        rows = found[:rank]
        for h in range(1, parts):
            rows = jnp.where(high == h, found[h * rank : (h + 1) * rank], rows)
        rows_s[u, :rank] = rows.astype(BF16)
        rows_s[u, rank:] = jnp.broadcast_to(rate_s[u : u + 1], (16, slots)).astype(BF16)
    tail_row = lax.broadcasted_iota(jnp.int32, (8, rank), 0)
    for u in range(users):
        both = rows_s[u]
        out = lax.dot_general(both, both[:rank], ROWS_TO_ROWS, preferred_element_type=F32)
        sum_ref, v = sums[u // share], u % share
        sum_ref[v, :rank] += out[:rank]
        tail = jnp.where(tail_row == 1, jnp.broadcast_to(live_s[u : u + 1], (8, rank)), out[rank : rank + 8])
        sum_ref[v, rank:] += tail


def gram(me, offset, code, tables, groups, before=()):
    _, users, width = code.shape
    slots, share = width // 2, users // CORES
    rank = tables[0].shape[2]
    counts = [t.shape[0] for t in tables]
    users = share * len(groups)
    out = pltpu.VMEM((share, rank + 8, rank), F32)
    whole = pl.BlockSpec(memory_space=pltpu.VMEM)
    operands = [code, *tables, *before]
    pairs = users * sum(counts)
    return pl.pallas_call(
        functools.partial(gram_kernel, counts=counts, groups=groups, first=not before, offset=offset),
        grid_spec=pltpu.PrefetchScalarGridSpec(
            num_scalar_prefetch=1,
            grid=(sum(counts),),
            in_specs=[whole for x in operands],
            out_specs=[whole for n in groups],
            scratch_shapes=[
                pltpu.VMEM((4 * rank, LOW), BF16),
                pltpu.VMEM((users, slots), F32),
                pltpu.VMEM((users, slots), F32),
                pltpu.VMEM((users, slots), F32),
                pltpu.VMEM((users, slots // 2), F32),
                pltpu.VMEM((users, rank + 16, slots), BF16),
            ],
        ),
        out_shape=[out for n in groups],
        cost_estimate=pl.CostEstimate(
            flops=pairs * 2 * slots * (4 * LOW + rank) * rank, transcendentals=0, bytes_accessed=4 * pairs * slots
        ),
        compiler_params=pltpu.CompilerParams(vmem_limit_bytes=VMEM_BYTES),
        name="gram",
    )(me, *[in_vmem(x) for x in operands])


def solve_kernel(own_ref, other_ref, out_ref, rows_s, below_s):
    users, rank = out_ref.shape
    lane = lax.broadcasted_iota(jnp.int32, (users, rank), 1)
    number = jnp.sum(own_ref[:, rank + 1, :] + other_ref[:, rank + 1, :], axis=1, keepdims=True)
    shift = jnp.broadcast_to(0.1 * number / rank, (users, rank))
    for i in range(rank):
        row = own_ref[:, i, :] + other_ref[:, i, :]
        rows_s[i * users : (i + 1) * users] = jnp.where(lane == i, row + shift, row)
    right = own_ref[:, rank, :] + other_ref[:, rank, :]

    def lane_of(value, i):
        return jnp.broadcast_to(value[:, i : i + 1], (users, rank))

    def row_of(i):
        return slice(i * users, (i + 1) * users)

    answer = jnp.zeros((users, rank), F32)
    steps = range(PANEL)
    for top in range(0, rank, BLOCK):
        end = top + BLOCK
        for start in range(top, end, PANEL):
            rows = [rows_s[row_of(start + t)] for t in steps]
            corner = {(t, s): lane_of(rows[s], start + t) for t in steps for s in range(t + 1)}
            middle = [lane_of(right, start + t) for t in steps]
            inside = (lane >= start) & (lane < start + PANEL)
            rows = [jnp.where(inside, jnp.where(lane == start + t, 1.0, 0.0), rows[t]) for t in steps]
            inverse = []
            for s in steps:
                inverse.append(1.0 / corner[s, s])
                for t in range(s + 1, PANEL):
                    factor = corner[t, s] * inverse[s]
                    for q in range(s + 1, t + 1):
                        corner[t, q] = corner[t, q] - factor * corner[q, s]
                    rows[t] = rows[t] - factor * rows[s]
                    middle[t] = middle[t] - factor * middle[s]
            for t in steps:
                scaled = middle[t] * inverse[t]
                answer = answer + jnp.where(lane < start + PANEL, scaled * rows[t], 0.0)
                right = right - scaled * rows[t]
            below = [rows[t] * inverse[t] for t in steps]
            for i in range(start + PANEL, end):
                row = jnp.where(inside, 0.0, rows_s[row_of(i)])
                for t in steps:
                    row = row - lane_of(below[t], i) * rows[t]
                rows_s[row_of(i)] = row
            if end < rank:
                pending = (lane >= start + PANEL) & (lane < end)
                for t in steps:
                    rows_s[row_of(start + t)] = jnp.where(pending, 0.0, rows[t])
                    below_s[row_of(start + t - top)] = below[t]
        if end < rank:
            wide = lax.broadcasted_iota(jnp.int32, (rank - end, rank), 1)
            within = (wide >= top) & (wide < end)
            for u in range(users):
                factors = below_s[pl.ds(u, BLOCK, stride=users), :]
                upper = rows_s[pl.ds(top * users + u, BLOCK, stride=users), :]
                change = lax.dot_general(
                    factors[:, end:],
                    upper,
                    COLS_TO_COLS,
                    precision=lax.Precision.HIGHEST,
                    preferred_element_type=F32,
                )
                rest = pl.ds(end * users + u, rank - end, stride=users)
                rows_s[rest, :] = jnp.where(within, 0.0, rows_s[rest, :]) - change
    out_ref[...] = answer


def solve(own, other):
    users, _, rank = own.shape
    return pl.pallas_call(
        solve_kernel,
        out_shape=jax.ShapeDtypeStruct((users, rank), F32),
        scratch_shapes=[pltpu.VMEM((rank * users, rank), F32), pltpu.VMEM((BLOCK * users, rank), F32)],
        compiler_params=pltpu.CompilerParams(vmem_limit_bytes=VMEM_BYTES),
        name="solve",
    )(in_vmem(own), in_vmem(other))


def coded(item_index, counts, begin, items):
    item_index = (item_index + (items - begin)) % items
    low = item_index % LOW
    value = jnp.where(low < HALF, low + HALF, -low) * (1 << (item_index // LOW))
    position = lax.broadcasted_iota(jnp.int32, item_index.shape, 1)
    return jnp.where(position < counts, value, 0).astype(BF16)


def row_at(y, x, core):
    return (y % SIDE * SIDE + x % SIDE) * CORES + core


def along_col(value, by):
    size = lax.axis_size("col")
    return lax.ppermute(value, "col", [(i, (i + by) % size) for i in range(size)])


def shifted(value, first, by):
    pairs = []
    for y in range(SIDE):
        for x in range(SIDE):
            for core in range(CORES):
                along_x = first == (core == 0)
                to = row_at(y, x + by, core) if along_x else row_at(y + by, x, core)
                pairs.append((row_at(y, x, core), to))
    return lax.ppermute(value, "row", pairs)


def ring(value, first):
    half = value.shape[0] // 2
    behind, ahead = shifted(value, first, 1), shifted(value, first, -1)
    return behind, ahead, shifted(behind[:half], first, 1), shifted(ahead[half:], first, -1)


def half_sweep(item_factors, item_index, ratings, counts):
    n_row, n_col = lax.axis_size("row"), lax.axis_size("col")
    chips = n_row // CORES
    slots, held = item_index.shape[1], item_factors.shape[0]
    me, z = lax.axis_index("row"), lax.axis_index("col")
    core = me % CORES

    code = coded(item_index, counts, (z + n_col // 2) % n_col * held, n_col * held)
    code = jnp.concatenate([code, ratings], axis=1).reshape(chips, CORES, -1, 2 * slots)
    code = jnp.where(core == 0, code, code[:, ::-1]).reshape(chips, -1, 2 * slots)
    same_core = [[chip * CORES + c for chip in range(chips)] for c in range(CORES)]
    code = lax.all_to_all(code, "row", 0, 0, tiled=True, axis_index_groups=same_core)

    mine = item_factors.T
    three = jnp.stack([along_col(mine, 1), mine, along_col(mine, -1)])
    block = jnp.concatenate([along_col(three, 3), three, along_col(three[:2], -3)])

    who = jnp.full((1,), me, jnp.int32)
    both, own_users, other_users = (0, 1), (0,), (1,)
    behind, ahead, far_low, far_high = ring(block, True)
    near = jnp.stack([block, behind, ahead, jnp.concatenate([far_low, far_high])])
    own, other = gram(who, 0, code, [near], both)
    behind, ahead, far_low, far_high = ring(near, False)
    own, other = gram(who, 4, code, [behind, ahead], both, (own, other))
    (other,) = gram(who, 12, code, [far_low, far_high], other_users, (other,))
    other = lax.ppermute(other, "row", [(i, i ^ 1) for i in range(n_row)])
    (own,) = gram(who, 12, code, [far_low, far_high], own_users, (own,))
    return solve(own, other)[None]


def solution(mesh):
    return jax.shard_map(
        half_sweep,
        mesh=mesh,
        in_specs=(P(("row", "col"), None), P("col", "row"), P("col", "row"), P("col", "row")),
        out_specs=P("col", "row", None),
        check_vma=False,
    )
```

time: 119 us -> 97.1 us (0.82)
  the two profiles are of different devices: /device:TPU:1 before, /device:TPU:7 now
where the time goes in v3:
time: 97.1 us; the launch traced here: 96.9 us
  Pallas kernels  35 us (36%)
  starting transfers between devices  31.2 us (32%)
  blocking collectives  17 us (18%)
  waiting for transfers between devices  11.9 us (12%)
  local copies, waits for them, and re-layouts  1.03 us (1%)
    pallas_call x4, Pallas kernels, gram(): pl.pallas_call(functools.partial(gram_kernel, counts=counts, groups=group...  27.9 us
    all_to_all x1, blocking collectives, half_sweep(): lax.all_to_all(code, 'row', 0, 0, tiled=True, axis_index_groups=same_core)  17 us
    ppermute x8, starting transfers between devices, shifted(): return lax.ppermute(value, 'row', pairs)  11.5 us
    ppermute x4, starting transfers between devices, along_col(): lax.ppermute(value, 'col', [(i, (i + by) % size) for i in range(size)])  10.4 us
    ppermute x1, starting transfers between devices, half_sweep(): other = lax.ppermute(other, 'row', [(i, i ^ 1) for i in range(n_row)])  9.32 us
    pallas_call x1, Pallas kernels, solve(): pl.pallas_call(solve_kernel, out_shape=jax.ShapeDtypeStruct((users, rank)...  7.05 us
    ppermute x4, waiting for transfers between devices, along_col(): lax.ppermute(value, 'col', [(i, (i + by) % size) for i in range(size)])  6.18 us
    ppermute x8, waiting for transfers between devices, shifted(): return lax.ppermute(value, 'row', pairs)  5.7 us
  transfers between devices with their start and end apart: 13, of which 5 were waited for; matrix products, arithmetic and copies ran while one was open for 1% of the time, Pallas kernels for 25%

profile of v3, /device:TPU:7, one launch (start us, length us, event | category | flops | bytes accessed | tf_op | source)
XLA Modules:
  0.0 96.9 jit_solution(17133503406350922528)
XLA Ops:
  0.0 0.9 copy.5
  0.9 1.7 %collective-permute-start = (bf16[128,128]{1,0:T(8,128)(2,1)S(1)}, bf16[128,128]{1,0:T(8,128)(2,1)S(1)}, u32[]{:S(2)}, u32[]{:S(2)}) collective-permute-start(bf16[128,128]{1,0:T(8,128)(2,1)S(1)} %bitcast.22), channel_id=1, source_target_pairs={{0,1},{1,2},{2,3},{3,4},{4,5},{5,6},{6,7},{7,0},{8,9},{9,10},{10,1... | collective-permute-start | bytes 98312 | tf_op jit(solution)/shard_map/ppermute | solution.py:229
  2.6 4.0 %collective-permute-start.1 = (bf16[128,128]{1,0:T(8,128)(2,1)S(1)}, bf16[128,128]{1,0:T(8,128)(2,1)S(1)}, u32[]{:S(2)}, u32[]{:S(2)}) collective-permute-start(bf16[128,128]{1,0:T(8,128)(2,1)S(1)} %bitcast.23), channel_id=1, source_target_pairs={{0,7},{1,0},{2,1},{3,2},{4,3},{5,4},{6,5},{7,6},{8,15},{9,8},{10,9... | collective-permute-start | bytes 98312 | tf_op jit(solution)/shard_map/ppermute | solution.py:229
  6.6 1.2 %collective-permute-done = bf16[128,128]{1,0:T(8,128)(2,1)S(1)} collective-permute-done((bf16[128,128]{1,0:T(8,128)(2,1)S(1)}, bf16[128,128]{1,0:T(8,128)(2,1)S(1)}, u32[]{:S(2)}, u32[]{:S(2)}) %collective-permute-start) | collective-permute-done | bytes 32800 | tf_op jit(solution)/shard_map/ppermute | solution.py:229
  7.8 0.0 collective-permute-done.1
  7.8 4.4 %collective-permute-start.2 = (bf16[3,128,128]{2,1,0:T(8,128)(2,1)S(1)}, bf16[3,128,128]{2,1,0:T(8,128)(2,1)S(1)}, u32[]{:S(2)}, u32[]{:S(2)}) collective-permute-start(bf16[3,128,128]{2,1,0:T(8,128)(2,1)S(1)} %pad_maximum_fusion.2), channel_id=1, source_target_pairs={{0,3},{1,4},{2,5},{3,6},{4,7},{5,0},{6,1},{7,2},{8,11},{9,12},{10,... | collective-permute-start | bytes 294920 | tf_op jit(solution)/shard_map/ppermute | solution.py:229
  12.2 0.3 collective-permute-start.3
  12.5 2.1 %collective-permute-done.2 = bf16[3,128,128]{2,1,0:T(8,128)(2,1)S(1)} collective-permute-done((bf16[3,128,128]{2,1,0:T(8,128)(2,1)S(1)}, bf16[3,128,128]{2,1,0:T(8,128)(2,1)S(1)}, u32[]{:S(2)}, u32[]{:S(2)}) %collective-permute-start.2) | collective-permute-done | bytes 98336 | tf_op jit(solution)/shard_map/ppermute | solution.py:229
  14.6 2.9 %collective-permute-done.3 = bf16[2,128,128]{2,1,0:T(8,128)(2,1)S(1)} collective-permute-done((bf16[2,128,128]{2,1,0:T(8,128)(2,1)S(1)}, bf16[2,128,128]{2,1,0:T(8,128)(2,1)S(1)}, u32[]{:S(2)}, u32[]{:S(2)}) %collective-permute-start.3) | collective-permute-done | bytes 65568 | tf_op jit(solution)/shard_map/ppermute | solution.py:229
  17.5 1.4 %collective-permute-start.4 = (bf16[8,128,128]{2,1,0:T(8,128)(2,1)S(1)}, bf16[8,128,128]{2,1,0:T(8,128)(2,1)S(1)}, u32[]{:S(2)}, u32[]{:S(2)}) collective-permute-start(bf16[8,128,128]{2,1,0:T(8,128)(2,1)S(1)} %constant_dynamic-update-slice_fusion), channel_id=1, source_target_pairs={{0,16},{8,72},{16,32},{24,88},{32,48},{40,104},{48,0},{56,120},{64... | collective-permute-start | bytes 786440 | tf_op jit(solution)/shard_map/ppermute | solution.py:240
  18.9 1.5 %collective-permute-start.5 = (bf16[8,128,128]{2,1,0:T(8,128)(2,1)S(1)}, bf16[8,128,128]{2,1,0:T(8,128)(2,1)S(1)}, u32[]{:S(2)}, u32[]{:S(2)}) collective-permute-start(bf16[8,128,128]{2,1,0:T(8,128)(2,1)S(1)} %constant_dynamic-update-slice_fusion), channel_id=1, source_target_pairs={{0,48},{8,200},{16,0},{24,216},{32,16},{40,232},{48,32},{56,248},{... | collective-permute-start | bytes 786440 | tf_op jit(solution)/shard_map/ppermute | solution.py:240
  20.4 0.0 copy-start
  20.4 3.7 %collective-permute-done.4 = bf16[8,128,128]{2,1,0:T(8,128)(2,1)S(1)} collective-permute-done((bf16[8,128,128]{2,1,0:T(8,128)(2,1)S(1)}, bf16[8,128,128]{2,1,0:T(8,128)(2,1)S(1)}, u32[]{:S(2)}, u32[]{:S(2)}) %collective-permute-start.4) | collective-permute-done | bytes 262176 | tf_op jit(solution)/shard_map/ppermute | solution.py:240
  24.1 0.1 collective-permute-start.6
  24.2 0.0 collective-permute-done.5
  24.2 0.0 copy-start.2
  24.2 2.7 %collective-permute-start.7 = (bf16[4,128,128]{2,1,0:T(8,128)(2,1)S(1)}, bf16[4,128,128]{2,1,0:T(8,128)(2,1)S(1)}, u32[]{:S(2)}, u32[]{:S(2)}) collective-permute-start(bf16[4,128,128]{2,1,0:T(8,128)(2,1)S(1)} %slice.19), channel_id=1, source_target_pairs={{0,48},{8,200},{16,0},{24,216},{32,16},{40,232},{48,32},{56,248},{... | collective-permute-start | bytes 393224 | tf_op jit(solution)/shard_map/ppermute | solution.py:240
  27.0 0.0 copy-done
  27.0 0.0 copy-done.2
  27.0 0.4 fusion.4
  27.4 2.0 %collective-permute-done.6 = bf16[4,128,128]{2,1,0:T(8,128)(2,1)S(1)} collective-permute-done((bf16[4,128,128]{2,1,0:T(8,128)(2,1)S(1)}, bf16[4,128,128]{2,1,0:T(8,128)(2,1)S(1)}, u32[]{:S(2)}, u32[]{:S(2)}) %collective-permute-start.6) | collective-permute-done | bytes 131104 | tf_op jit(solution)/shard_map/ppermute | solution.py:240
  29.4 0.0 collective-permute-done.7
  29.4 0.0 copy-start.1
  29.4 0.1 pad_maximum_fusion.refs_0_
  29.6 0.4 collective-permute-start.10
  30.0 2.3 %collective-permute-start.8 = (bf16[4,8,128,128]{3,2,1,0:T(8,128)(2,1)S(1)}, bf16[4,8,128,128]{3,2,1,0:T(8,128)(2,1)S(1)}, u32[]{:S(2)}, u32[]{:S(2)}) collective-permute-start(bf16[4,8,128,128]{3,2,1,0:T(8,128)(2,1)S(1)} %pad_maximum_fusion.refs_0_), channel_id=1, source_target_pairs={{0,64},{8,24},{16,80},{24,40},{32,96},{40,56},{48,112},{56,8},{64,... | collective-permute-start | bytes 3145736 | tf_op jit(solution)/shard_map/ppermute | solution.py:240
  32.3 0.0 copy-done.1
  32.4 0.1 fusion.5
  32.4 17.0 %all_to_all.5.code_ref = bf16[16,16,512]{2,1,0:T(8,128)(2,1)S(1)} all-to-all(bf16[16,16,512]{2,1,0:T(8,128)(2,1)S(1)} %fusion.5), channel_id=1, replica_groups={{0,16,32,48,64,80,96,112,128,144,160,176,192,208,224,240},{8,24,40,56,7..., dimensions={0} | all-to-all | bytes 524288 | tf_op jit(solution)/shard_map/all_to_all | solution.py:260
  49.4 6.7 %gram.4 = (f32[8,136,128]{2,1,0:T(8,128)S(1)}, f32[8,136,128]{2,1,0:T(8,128)S(1)}) custom-call(s32[1]{0:T(128)} %bitcast.me_ref, bf16[16,16,512]{2,1,0:T(8,128)(2,1)S(1)} %all_to_all.5.code_ref, bf16[4,8,128,128]{3,2,1,0:T(8,128)(2,1)S(1)} %pad_maximum_fusion.refs_0_), custom_call_target="tpu_custom_call" | custom-call | flops 4831838208 | bytes 65536 | tf_op jit(solution)/shard_map/gram/pallas_call | solution.py:111
  56.2 0.0 collective-permute-done.10.refs_1_
  56.2 0.1 collective-permute-start.11
  56.3 0.0 collective-permute-done.8.refs_0_
  56.4 2.9 %collective-permute-start.9 = (bf16[2,8,128,128]{3,2,1,0:T(8,128)(2,1)S(1)}, bf16[2,8,128,128]{3,2,1,0:T(8,128)(2,1)S(1)}, u32[]{:S(2)}, u32[]{:S(2)}) collective-permute-start(bf16[2,8,128,128]{3,2,1,0:T(8,128)(2,1)S(1)} %slice.20), channel_id=1, source_target_pairs={{0,64},{8,24},{16,80},{24,40},{32,96},{40,56},{48,112},{56,8},{64,... | collective-permute-start | bytes 1572872 | tf_op jit(solution)/shard_map/ppermute | solution.py:240
  59.3 13.4 %gram.5 = (f32[8,136,128]{2,1,0:T(8,128)S(1)}, f32[8,136,128]{2,1,0:T(8,128)S(1)}) custom-call(s32[1]{0:T(128)} %bitcast.me_ref, bf16[16,16,512]{2,1,0:T(8,128)(2,1)S(1)} %all_to_all.5.code_ref, bf16[4,8,128,128]{3,2,1,0:T(8,128)(2,1)S(1)} %collective-permute-done.8.refs_0_, bf16[4,8,128,128]{3,2,1,0:T(8,128)(2,1)S(1)} %collective-permute-done.10.refs_1_, ...), custom_call_target="tpu_custom_call" | custom-call | flops 9663676416 | bytes 131072 | tf_op jit(solution)/shard_map/gram/pallas_call | solution.py:111
  72.7 0.0 collective-permute-done.11.refs_1_
  72.7 0.0 collective-permute-done.9.refs_0_
  72.8 3.9 %gram.7 = f32[8,136,128]{2,1,0:T(8,128)S(1)} custom-call(s32[1]{0:T(128)} %bitcast.me_ref, bf16[16,16,512]{2,1,0:T(8,128)(2,1)S(1)} %all_to_all.5.code_ref, bf16[2,8,128,128]{3,2,1,0:T(8,128)(2,1)S(1)} %collective-permute-done.9.refs_0_, bf16[2,8,128,128]{3,2,1,0:T(8,128)(2,1)S(1)} %collective-permute-done.11.refs_1_, ...), custom_call_target="tpu_custom_call" | custom-call | flops 2415919104 | bytes 32768 | tf_op jit(solution)/shard_map/gram/pallas_call | solution.py:111
  76.7 9.3 %collective-permute-start.12 = (f32[8,136,128]{2,1,0:T(8,128)S(1)}, f32[8,136,128]{2,1,0:T(8,128)S(1)}, u32[]{:S(2)}, u32[]{:S(2)}) collective-permute-start(f32[8,136,128]{2,1,0:T(8,128)S(1)} %gram.7), channel_id=1, source_target_pairs={{0,8},{8,0},{16,24},{24,16},{32,40},{40,32},{48,56},{56,48},{64,72... | collective-permute-start | bytes 1671176 | tf_op jit(solution)/shard_map/ppermute | solution.py:274
  86.0 3.9 %gram.6.own_ref = f32[8,136,128]{2,1,0:T(8,128)S(1)} custom-call(s32[1]{0:T(128)} %bitcast.me_ref, bf16[16,16,512]{2,1,0:T(8,128)(2,1)S(1)} %all_to_all.5.code_ref, bf16[2,8,128,128]{3,2,1,0:T(8,128)(2,1)S(1)} %collective-permute-done.9.refs_0_, bf16[2,8,128,128]{3,2,1,0:T(8,128)(2,1)S(1)} %collective-permute-done.11.refs_1_, ...), custom_call_target="tpu_custom_call" | custom-call | flops 2415919104 | bytes 32768 | tf_op jit(solution)/shard_map/gram/pallas_call | solution.py:111
  89.9 0.0 collective-permute-done.12.other_ref
  89.9 7.0 %solve.1 = f32[8,128]{1,0:T(8,128)} custom-call(f32[8,136,128]{2,1,0:T(8,128)S(1)} %gram.6.own_ref, f32[8,136,128]{2,1,0:T(8,128)S(1)} %collective-permute-done.12.other_ref), custom_call_target="tpu_custom_call" | custom-call | tf_op jit(solution)/shard_map/solve/pallas_call | solution.py:206
  (13 shorter events, 0.2 us)
Async XLA Ops:
  0.9 7.0 %collective-permute-start = (bf16[128,128]{1,0:T(8,128)(2,1)S(1)}, bf16[128,128]{1,0:T(8,128)(2,1)S(1)}, u32[]{:S(2)}, u32[]{:S(2)}) collective-permute-start(bf16[128,128]{1,0:T(8,128)(2,1)S(1)} %bitcast.22), channel_id=1, source_target_pairs={{0,1},{1,2},{2,3},{3,4},{4,5},{5,6},{6,7},{7,0},{8,9},{9,10},{10,1... | collective-permute-start | bytes 98312 | tf_op jit(solution)/shard_map/ppermute | solution.py:229
  2.6 5.2 %collective-permute-start.1 = (bf16[128,128]{1,0:T(8,128)(2,1)S(1)}, bf16[128,128]{1,0:T(8,128)(2,1)S(1)}, u32[]{:S(2)}, u32[]{:S(2)}) collective-permute-start(bf16[128,128]{1,0:T(8,128)(2,1)S(1)} %bitcast.23), channel_id=1, source_target_pairs={{0,7},{1,0},{2,1},{3,2},{4,3},{5,4},{6,5},{7,6},{8,15},{9,8},{10,9... | collective-permute-start | bytes 98312 | tf_op jit(solution)/shard_map/ppermute | solution.py:229
  7.8 6.7 %collective-permute-start.2 = (bf16[3,128,128]{2,1,0:T(8,128)(2,1)S(1)}, bf16[3,128,128]{2,1,0:T(8,128)(2,1)S(1)}, u32[]{:S(2)}, u32[]{:S(2)}) collective-permute-start(bf16[3,128,128]{2,1,0:T(8,128)(2,1)S(1)} %pad_maximum_fusion.2), channel_id=1, source_target_pairs={{0,3},{1,4},{2,5},{3,6},{4,7},{5,0},{6,1},{7,2},{8,11},{9,12},{10,... | collective-permute-start | bytes 294920 | tf_op jit(solution)/shard_map/ppermute | solution.py:229
  12.2 5.3 %collective-permute-start.3 = (bf16[2,128,128]{2,1,0:T(8,128)(2,1)S(1)}, bf16[2,128,128]{2,1,0:T(8,128)(2,1)S(1)}, u32[]{:S(2)}, u32[]{:S(2)}) collective-permute-start(bf16[2,128,128]{2,1,0:T(8,128)(2,1)S(1)} %pad_maximum_fusion.3), channel_id=1, source_target_pairs={{0,5},{1,6},{2,7},{3,0},{4,1},{5,2},{6,3},{7,4},{8,13},{9,14},{10,... | collective-permute-start | bytes 196616 | tf_op jit(solution)/shard_map/ppermute | solution.py:229
  17.5 6.6 %collective-permute-start.4 = (bf16[8,128,128]{2,1,0:T(8,128)(2,1)S(1)}, bf16[8,128,128]{2,1,0:T(8,128)(2,1)S(1)}, u32[]{:S(2)}, u32[]{:S(2)}) collective-permute-start(bf16[8,128,128]{2,1,0:T(8,128)(2,1)S(1)} %constant_dynamic-update-slice_fusion), channel_id=1, source_target_pairs={{0,16},{8,72},{16,32},{24,88},{32,48},{40,104},{48,0},{56,120},{64... | collective-permute-start | bytes 786440 | tf_op jit(solution)/shard_map/ppermute | solution.py:240
  18.9 5.3 %collective-permute-start.5 = (bf16[8,128,128]{2,1,0:T(8,128)(2,1)S(1)}, bf16[8,128,128]{2,1,0:T(8,128)(2,1)S(1)}, u32[]{:S(2)}, u32[]{:S(2)}) collective-permute-start(bf16[8,128,128]{2,1,0:T(8,128)(2,1)S(1)} %constant_dynamic-update-slice_fusion), channel_id=1, source_target_pairs={{0,48},{8,200},{16,0},{24,216},{32,16},{40,232},{48,32},{56,248},{... | collective-permute-start | bytes 786440 | tf_op jit(solution)/shard_map/ppermute | solution.py:240
  20.4 6.5 %copy-start = (s32[256,256]{1,0:T(8,128)S(1)}, s32[256,256]{1,0:T(8,128)}, u32[]{:S(2)}) copy-start(s32[256,256]{1,0:T(8,128)} %param.5) | copy-start | bytes 786436
  24.1 5.3 %collective-permute-start.6 = (bf16[4,128,128]{2,1,0:T(8,128)(2,1)S(1)}, bf16[4,128,128]{2,1,0:T(8,128)(2,1)S(1)}, u32[]{:S(2)}, u32[]{:S(2)}) collective-permute-start(bf16[4,128,128]{2,1,0:T(8,128)(2,1)S(1)} %slice.18), channel_id=1, source_target_pairs={{0,16},{8,72},{16,32},{24,88},{32,48},{40,104},{48,0},{56,120},{64... | collective-permute-start | bytes 393224 | tf_op jit(solution)/shard_map/ppermute | solution.py:240
  24.2 2.7 %copy-start.2 = (s32[256,1]{0,1:T(1,128)S(1)}, s32[256,1]{0,1:T(1,128)}, u32[]{:S(2)}) copy-start(s32[256,1]{0,1:T(1,128)} %param.7) | copy-start | bytes 3076
  24.2 5.2 %collective-permute-start.7 = (bf16[4,128,128]{2,1,0:T(8,128)(2,1)S(1)}, bf16[4,128,128]{2,1,0:T(8,128)(2,1)S(1)}, u32[]{:S(2)}, u32[]{:S(2)}) collective-permute-start(bf16[4,128,128]{2,1,0:T(8,128)(2,1)S(1)} %slice.19), channel_id=1, source_target_pairs={{0,48},{8,200},{16,0},{24,216},{32,16},{40,232},{48,32},{56,248},{... | collective-permute-start | bytes 393224 | tf_op jit(solution)/shard_map/ppermute | solution.py:240
  29.4 2.9 %copy-start.1 = (bf16[256,256]{1,0:T(8,128)(2,1)S(1)}, bf16[256,256]{1,0:T(8,128)(2,1)}, u32[]{:S(2)}) copy-start(bf16[256,256]{1,0:T(8,128)(2,1)} %param.6) | copy-start | bytes 393220
  29.6 26.6 %collective-permute-start.10 = (bf16[4,8,128,128]{3,2,1,0:T(8,128)(2,1)S(1)}, bf16[4,8,128,128]{3,2,1,0:T(8,128)(2,1)S(1)}, u32[]{:S(2)}, u32[]{:S(2)}) collective-permute-start(bf16[4,8,128,128]{3,2,1,0:T(8,128)(2,1)S(1)} %pad_maximum_fusion.refs_0_), channel_id=1, source_target_pairs={{0,192},{8,56},{16,208},{24,8},{32,224},{40,24},{48,240},{56,40},{... | collective-permute-start | bytes 3145736 | tf_op jit(solution)/shard_map/ppermute | solution.py:240
  30.0 26.3 %collective-permute-start.8 = (bf16[4,8,128,128]{3,2,1,0:T(8,128)(2,1)S(1)}, bf16[4,8,128,128]{3,2,1,0:T(8,128)(2,1)S(1)}, u32[]{:S(2)}, u32[]{:S(2)}) collective-permute-start(bf16[4,8,128,128]{3,2,1,0:T(8,128)(2,1)S(1)} %pad_maximum_fusion.refs_0_), channel_id=1, source_target_pairs={{0,64},{8,24},{16,80},{24,40},{32,96},{40,56},{48,112},{56,8},{64,... | collective-permute-start | bytes 3145736 | tf_op jit(solution)/shard_map/ppermute | solution.py:240
  56.2 16.5 %collective-permute-start.11 = (bf16[2,8,128,128]{3,2,1,0:T(8,128)(2,1)S(1)}, bf16[2,8,128,128]{3,2,1,0:T(8,128)(2,1)S(1)}, u32[]{:S(2)}, u32[]{:S(2)}) collective-permute-start(bf16[2,8,128,128]{3,2,1,0:T(8,128)(2,1)S(1)} %slice.21), channel_id=1, source_target_pairs={{0,192},{8,56},{16,208},{24,8},{32,224},{40,24},{48,240},{56,40},{... | collective-permute-start | bytes 1572872 | tf_op jit(solution)/shard_map/ppermute | solution.py:240
  56.4 16.4 %collective-permute-start.9 = (bf16[2,8,128,128]{3,2,1,0:T(8,128)(2,1)S(1)}, bf16[2,8,128,128]{3,2,1,0:T(8,128)(2,1)S(1)}, u32[]{:S(2)}, u32[]{:S(2)}) collective-permute-start(bf16[2,8,128,128]{3,2,1,0:T(8,128)(2,1)S(1)} %slice.20), channel_id=1, source_target_pairs={{0,64},{8,24},{16,80},{24,40},{32,96},{40,56},{48,112},{56,8},{64,... | collective-permute-start | bytes 1572872 | tf_op jit(solution)/shard_map/ppermute | solution.py:240
  76.7 13.2 %collective-permute-start.12 = (f32[8,136,128]{2,1,0:T(8,128)S(1)}, f32[8,136,128]{2,1,0:T(8,128)S(1)}, u32[]{:S(2)}, u32[]{:S(2)}) collective-permute-start(f32[8,136,128]{2,1,0:T(8,128)S(1)} %gram.7), channel_id=1, source_target_pairs={{0,8},{8,0},{16,24},{24,16},{32,40},{40,32},{48,56},{56,48},{64,72... | collective-permute-start | bytes 1671176 | tf_op jit(solution)/shard_map/ppermute | solution.py:274

commit v4 on v3

--- a/solution.py
+++ b/solution.py
@@ -240,10 +240,12 @@
     return lax.ppermute(value, "row", pairs)
 
 
-def ring(value, first):
-    half = value.shape[0] // 2
-    behind, ahead = shifted(value, first, 1), shifted(value, first, -1)
-    return behind, ahead, shifted(behind[:half], first, 1), shifted(ahead[half:], first, -1)
+def near_of(value, first):
+    return shifted(value, first, 1), shifted(value, first, -1)
+
+
+def far_of(low, high, first):
+    return shifted(low, first, 1), shifted(high, first, -1)
 
 
 def half_sweep(item_factors, item_index, ratings, counts):
@@ -265,14 +267,23 @@
 
     who = jnp.full((1,), me, jnp.int32)
     both, own_users, other_users = (0, 1), (0,), (1,)
-    behind, ahead, far_low, far_high = ring(block, True)
-    near = jnp.stack([block, behind, ahead, jnp.concatenate([far_low, far_high])])
-    own, other = gram(who, 0, code, [near], both)
-    behind, ahead, far_low, far_high = ring(near, False)
-    own, other = gram(who, 4, code, [behind, ahead], both, (own, other))
-    (other,) = gram(who, 12, code, [far_low, far_high], other_users, (other,))
+    half = n_col // 2
+    behind, ahead = near_of(block, True)
+    alone = block[None]
+    alone_behind, alone_ahead = near_of(alone, False)
+    far = jnp.concatenate(far_of(behind[:half], ahead[half:], True))[None]
+    sides = jnp.stack([behind, ahead])
+    sides_behind, sides_ahead = near_of(sides, False)
+    far_behind, far_ahead = near_of(far, False)
+    own, other = gram(who, 0, code, [alone, sides, far], both)
+    low, high = far_of(
+        jnp.concatenate([alone_behind, sides_behind[:1]]), jnp.concatenate([sides_ahead[1:], far_ahead]), False
+    )
+    tables = [alone_behind, sides_behind, far_behind, alone_ahead, sides_ahead, far_ahead]
+    own, other = gram(who, 4, code, tables, both, (own, other))
+    (other,) = gram(who, 12, code, [low, high], other_users, (other,))
     other = lax.ppermute(other, "row", [(i, i ^ 1) for i in range(n_row)])
-    (own,) = gram(who, 12, code, [far_low, far_high], own_users, (own,))
+    (own,) = gram(who, 12, code, [low, high], own_users, (own,))
     return solve(own, other)[None]
 
 

time: 97.1 us -> 91.9 us (0.946)
  the two profiles are of different devices: /device:TPU:7 before, /device:TPU:1 now
where the time goes in v4:
time: 91.9 us; the launch traced here: 91.6 us
  starting transfers between devices  38.1 us (41%)
  Pallas kernels  35.2 us (38%)
  waiting for transfers between devices  15.1 us (16%)
  local copies, waits for them, and re-layouts  1.65 us (2%)
  other arithmetic  1.39 us (2%)
    pallas_call x4, Pallas kernels, gram(): pl.pallas_call(functools.partial(gram_kernel, counts=counts, groups=group...  28.2 us
    ppermute x12, starting transfers between devices, shifted(): return lax.ppermute(value, 'row', pairs)  14.5 us
    ppermute x4, starting transfers between devices, along_col(): lax.ppermute(value, 'col', [(i, (i + by) % size) for i in range(size)])  11.2 us
    ppermute x1, starting transfers between devices, half_sweep(): other = lax.ppermute(other, 'row', [(i, i ^ 1) for i in range(n_row)])  8.75 us
    pallas_call x1, Pallas kernels, solve(): pl.pallas_call(solve_kernel, out_shape=jax.ShapeDtypeStruct((users, rank)...  7.05 us
    ppermute x4, waiting for transfers between devices, along_col(): lax.ppermute(value, 'col', [(i, (i + by) % size) for i in range(size)])  6.18 us
    ppermute x12, waiting for transfers between devices, shifted(): return lax.ppermute(value, 'row', pairs)  5.76 us
    all_to_all x1, starting transfers between devices, half_sweep(): lax.all_to_all(code, 'row', 0, 0, tiled=True, axis_index_groups=same_core)  3.58 us
  transfers between devices with their start and end apart: 18, of which 7 were waited for; matrix products, arithmetic and copies ran while one was open for 2% of the time, Pallas kernels for 26%

profile of v4, /device:TPU:1, one launch (start us, length us, event | category | flops | bytes accessed | tf_op | source)
XLA Modules:
  0.0 91.6 jit_solution(17195455836087722220)
XLA Ops:
  0.0 0.9 copy.5
  0.9 2.5 %collective-permute-start = (bf16[128,128]{1,0:T(8,128)(2,1)S(1)}, bf16[128,128]{1,0:T(8,128)(2,1)S(1)}, u32[]{:S(2)}, u32[]{:S(2)}) collective-permute-start(bf16[128,128]{1,0:T(8,128)(2,1)S(1)} %bitcast.25), channel_id=1, source_target_pairs={{0,1},{1,2},{2,3},{3,4},{4,5},{5,6},{6,7},{7,0},{8,9},{9,10},{10,1... | collective-permute-start | bytes 98312 | tf_op jit(solution)/shard_map/ppermute | solution.py:229
  3.4 4.0 %collective-permute-start.1 = (bf16[128,128]{1,0:T(8,128)(2,1)S(1)}, bf16[128,128]{1,0:T(8,128)(2,1)S(1)}, u32[]{:S(2)}, u32[]{:S(2)}) collective-permute-start(bf16[128,128]{1,0:T(8,128)(2,1)S(1)} %bitcast.26), channel_id=1, source_target_pairs={{0,7},{1,0},{2,1},{3,2},{4,3},{5,4},{6,5},{7,6},{8,15},{9,8},{10,9... | collective-permute-start | bytes 98312 | tf_op jit(solution)/shard_map/ppermute | solution.py:229
  7.4 1.2 %collective-permute-done = bf16[128,128]{1,0:T(8,128)(2,1)S(1)} collective-permute-done((bf16[128,128]{1,0:T(8,128)(2,1)S(1)}, bf16[128,128]{1,0:T(8,128)(2,1)S(1)}, u32[]{:S(2)}, u32[]{:S(2)}) %collective-permute-start) | collective-permute-done | bytes 32800 | tf_op jit(solution)/shard_map/ppermute | solution.py:229
  8.6 0.0 collective-permute-done.1
  8.7 4.4 %collective-permute-start.2 = (bf16[3,128,128]{2,1,0:T(8,128)(2,1)S(1)}, bf16[3,128,128]{2,1,0:T(8,128)(2,1)S(1)}, u32[]{:S(2)}, u32[]{:S(2)}) collective-permute-start(bf16[3,128,128]{2,1,0:T(8,128)(2,1)S(1)} %pad_maximum_fusion.4), channel_id=1, source_target_pairs={{0,3},{1,4},{2,5},{3,6},{4,7},{5,0},{6,1},{7,2},{8,11},{9,12},{10,... | collective-permute-start | bytes 294920 | tf_op jit(solution)/shard_map/ppermute | solution.py:229
  13.0 0.0 copy-start
  13.0 0.3 collective-permute-start.3
  13.3 2.1 %collective-permute-done.2 = bf16[3,128,128]{2,1,0:T(8,128)(2,1)S(1)} collective-permute-done((bf16[3,128,128]{2,1,0:T(8,128)(2,1)S(1)}, bf16[3,128,128]{2,1,0:T(8,128)(2,1)S(1)}, u32[]{:S(2)}, u32[]{:S(2)}) %collective-permute-start.2) | collective-permute-done | bytes 98336 | tf_op jit(solution)/shard_map/ppermute | solution.py:229
  15.4 2.9 %collective-permute-done.3 = bf16[2,128,128]{2,1,0:T(8,128)(2,1)S(1)} collective-permute-done((bf16[2,128,128]{2,1,0:T(8,128)(2,1)S(1)}, bf16[2,128,128]{2,1,0:T(8,128)(2,1)S(1)}, u32[]{:S(2)}, u32[]{:S(2)}) %collective-permute-start.3) | collective-permute-done | bytes 65568 | tf_op jit(solution)/shard_map/ppermute | solution.py:229
  18.3 1.4 %collective-permute-start.5 = (bf16[8,128,128]{2,1,0:T(8,128)(2,1)S(1)}, bf16[8,128,128]{2,1,0:T(8,128)(2,1)S(1)}, u32[]{:S(2)}, u32[]{:S(2)}) collective-permute-start(bf16[8,128,128]{2,1,0:T(8,128)(2,1)S(1)} %constant_dynamic-update-slice_fusion), channel_id=1, source_target_pairs={{0,16},{8,72},{16,32},{24,88},{32,48},{40,104},{48,0},{56,120},{64... | collective-permute-start | bytes 786440 | tf_op jit(solution)/shard_map/ppermute | solution.py:240
  19.7 1.5 %collective-permute-start.6 = (bf16[8,128,128]{2,1,0:T(8,128)(2,1)S(1)}, bf16[8,128,128]{2,1,0:T(8,128)(2,1)S(1)}, u32[]{:S(2)}, u32[]{:S(2)}) collective-permute-start(bf16[8,128,128]{2,1,0:T(8,128)(2,1)S(1)} %constant_dynamic-update-slice_fusion), channel_id=1, source_target_pairs={{0,48},{8,200},{16,0},{24,216},{32,16},{40,232},{48,32},{56,248},{... | collective-permute-start | bytes 786440 | tf_op jit(solution)/shard_map/ppermute | solution.py:240
  21.2 0.0 copy-start.2
  21.2 0.0 copy-done
  21.2 0.7 copy-done.2
  21.9 0.4 fusion.4
  22.3 2.6 %collective-permute-done.5 = bf16[8,128,128]{2,1,0:T(8,128)(2,1)S(1)} collective-permute-done((bf16[8,128,128]{2,1,0:T(8,128)(2,1)S(1)}, bf16[8,128,128]{2,1,0:T(8,128)(2,1)S(1)}, u32[]{:S(2)}, u32[]{:S(2)}) %collective-permute-start.5) | collective-permute-done | bytes 262176 | tf_op jit(solution)/shard_map/ppermute | solution.py:240
  24.9 0.0 collective-permute-done.6
  24.9 0.0 copy-start.1
  24.9 0.1 pad_maximum_fusion.refs_1_
  25.0 2.6 %collective-permute-start.9 = (bf16[2,8,128,128]{3,2,1,0:T(8,128)(2,1)S(1)}, bf16[2,8,128,128]{3,2,1,0:T(8,128)(2,1)S(1)}, u32[]{:S(2)}, u32[]{:S(2)}) collective-permute-start(bf16[2,8,128,128]{3,2,1,0:T(8,128)(2,1)S(1)} %pad_maximum_fusion.refs_1_), channel_id=1, source_target_pairs={{0,192},{8,56},{16,208},{24,8},{32,224},{40,24},{48,240},{56,40},{... | collective-permute-start | bytes 1572872 | tf_op jit(solution)/shard_map/ppermute | solution.py:240
  27.6 0.0 copy-done.1
  27.6 1.4 %collective-permute-start.10 = (bf16[4,128,128]{2,1,0:T(8,128)(2,1)S(1)}, bf16[4,128,128]{2,1,0:T(8,128)(2,1)S(1)}, u32[]{:S(2)}, u32[]{:S(2)}) collective-permute-start(bf16[4,128,128]{2,1,0:T(8,128)(2,1)S(1)} %slice.20), channel_id=1, source_target_pairs={{0,16},{8,72},{16,32},{24,88},{32,48},{40,104},{48,0},{56,120},{64... | collective-permute-start | bytes 393224 | tf_op jit(solution)/shard_map/ppermute | solution.py:240
  29.0 1.5 %collective-permute-start.11 = (bf16[4,128,128]{2,1,0:T(8,128)(2,1)S(1)}, bf16[4,128,128]{2,1,0:T(8,128)(2,1)S(1)}, u32[]{:S(2)}, u32[]{:S(2)}) collective-permute-start(bf16[4,128,128]{2,1,0:T(8,128)(2,1)S(1)} %slice.21), channel_id=1, source_target_pairs={{0,48},{8,200},{16,0},{24,216},{32,16},{40,232},{48,32},{56,248},{... | collective-permute-start | bytes 393224 | tf_op jit(solution)/shard_map/ppermute | solution.py:240
  30.5 0.8 fusion.5
  31.3 3.6 %all-to-all-start = ((bf16[16,16,512]{2,1,0:T(8,128)(2,1)}), bf16[16,16,512]{2,1,0:T(8,128)(2,1)S(1)}, u32[]{:S(2)}, u32[]{:S(2)}) async-start(bf16[16,16,512]{2,1,0:T(8,128)(2,1)} %fusion.5), calls=%async_computation | async-start | bytes 524288 | tf_op jit(solution)/shard_map/all_to_all | solution.py:262
  34.9 1.4 %collective-permute-start.4 = (bf16[1,8,128,128]{3,2,1,0:T(8,128)(2,1)S(1)}, bf16[1,8,128,128]{3,2,1,0:T(8,128)(2,1)S(1)}, u32[]{:S(2)}, u32[]{:S(2)}) collective-permute-start(bf16[1,8,128,128]{3,2,1,0:T(8,128)(2,1)S(1)} %bitcast.19), channel_id=1, source_target_pairs={{0,64},{8,24},{16,80},{24,40},{32,96},{40,56},{48,112},{56,8},{64,... | collective-permute-start | bytes 786440 | tf_op jit(solution)/shard_map/ppermute | solution.py:240
  36.2 1.4 %collective-permute-start.15 = (bf16[1,8,128,128]{3,2,1,0:T(8,128)(2,1)S(1)}, bf16[1,8,128,128]{3,2,1,0:T(8,128)(2,1)S(1)}, u32[]{:S(2)}, u32[]{:S(2)}) collective-permute-start(bf16[1,8,128,128]{3,2,1,0:T(8,128)(2,1)S(1)} %bitcast.20), channel_id=1, source_target_pairs={{0,192},{8,56},{16,208},{24,8},{32,224},{40,24},{48,240},{56,40},{... | collective-permute-start | bytes 786440 | tf_op jit(solution)/shard_map/ppermute | solution.py:240
  37.6 0.0 collective-permute-done.10
  37.6 0.1 collective-permute-start.7
  37.7 0.0 collective-permute-done.11
  37.7 2.7 %collective-permute-start.12 = (bf16[1,8,128,128]{3,2,1,0:T(8,128)(2,1)S(1)}, bf16[1,8,128,128]{3,2,1,0:T(8,128)(2,1)S(1)}, u32[]{:S(2)}, u32[]{:S(2)}) collective-permute-start(bf16[1,8,128,128]{3,2,1,0:T(8,128)(2,1)S(1)} %maximum_bitcast_fusion.refs_2_), channel_id=1, source_target_pairs={{0,192},{8,56},{16,208},{24,8},{32,224},{40,24},{48,240},{56,40},{... | collective-permute-start | bytes 786440 | tf_op jit(solution)/shard_map/ppermute | solution.py:240
  40.4 0.0 collective-permute-done.9.refs_4_
  40.4 0.0 collective-permute-start.14
  40.4 3.2 %all-to-all-done.code_ref = bf16[16,16,512]{2,1,0:T(8,128)(2,1)S(1)} async-done(((bf16[16,16,512]{2,1,0:T(8,128)(2,1)}), bf16[16,16,512]{2,1,0:T(8,128)(2,1)S(1)}, u32[]{:S(2)}, u32[]{:S(2)}) %all-to-all-start) | async-done | bytes 262176 | tf_op jit(solution)/shard_map/all_to_all | solution.py:262
  43.6 6.8 %gram.4 = (f32[8,136,128]{2,1,0:T(8,128)S(1)}, f32[8,136,128]{2,1,0:T(8,128)S(1)}) custom-call(s32[1]{0:T(128)} %bitcast.me_ref, bf16[16,16,512]{2,1,0:T(8,128)(2,1)S(1)} %all-to-all-done.code_ref, bf16[1,8,128,128]{3,2,1,0:T(8,128)(2,1)S(1)} %bitcast.21, bf16[2,8,128,128]{3,2,1,0:T(8,128)(2,1)S(1)} %pad_maximum_fusion.refs_1_, ...), custom_call_target="tpu_custom_call" | custom-call | flops 4831838208 | bytes 65536 | tf_op jit(solution)/shard_map/gram/pallas_call | solution.py:111
  50.4 0.0 collective-permute-done.12.refs_5_
  50.4 0.1 pad_maximum_fusion.2
  50.5 0.1 collective-permute-start.13
  50.6 1.0 %collective-permute-done.7.refs_1_ = bf16[2,8,128,128]{3,2,1,0:T(8,128)(2,1)S(1)} collective-permute-done((bf16[2,8,128,128]{3,2,1,0:T(8,128)(2,1)S(1)}, bf16[2,8,128,128]{3,2,1,0:T(8,128)(2,1)S(1)}, u32[]{:S(2)}, u32[]{:S(2)}) %collective-permute-start.7) | collective-permute-done | bytes 524320 | tf_op jit(solution)/shard_map/ppermute | solution.py:240
  51.6 0.0 collective-permute-done.4.refs_0_
  51.6 0.1 pad_maximum_fusion.1
  51.6 0.5 collective-permute-start.8
  52.2 0.0 collective-permute-done.15.refs_3_
  52.2 2.2 %collective-permute-done.14.refs_2_ = bf16[1,8,128,128]{3,2,1,0:T(8,128)(2,1)S(1)} collective-permute-done((bf16[1,8,128,128]{3,2,1,0:T(8,128)(2,1)S(1)}, bf16[1,8,128,128]{3,2,1,0:T(8,128)(2,1)S(1)}, u32[]{:S(2)}, u32[]{:S(2)}) %collective-permute-start.14) | collective-permute-done | bytes 262176 | tf_op jit(solution)/shard_map/ppermute | solution.py:240
  54.4 13.6 %gram.5 = (f32[8,136,128]{2,1,0:T(8,128)S(1)}, f32[8,136,128]{2,1,0:T(8,128)S(1)}) custom-call(s32[1]{0:T(128)} %bitcast.me_ref, bf16[16,16,512]{2,1,0:T(8,128)(2,1)S(1)} %all-to-all-done.code_ref, bf16[1,8,128,128]{3,2,1,0:T(8,128)(2,1)S(1)} %collective-permute-done.4.refs_0_, bf16[2,8,128,128]{3,2,1,0:T(8,128)(2,1)S(1)} %collective-permute-done.7.refs_1_, ...), custom_call_target="tpu_custom_call" | custom-call | flops 9663676416 | bytes 131072 | tf_op jit(solution)/shard_map/gram/pallas_call | solution.py:111
  68.0 0.0 collective-permute-done.13.refs_1_
  68.0 0.0 collective-permute-done.8.refs_0_
  68.0 3.9 %gram.7 = f32[8,136,128]{2,1,0:T(8,128)S(1)} custom-call(s32[1]{0:T(128)} %bitcast.me_ref, bf16[16,16,512]{2,1,0:T(8,128)(2,1)S(1)} %all-to-all-done.code_ref, bf16[2,8,128,128]{3,2,1,0:T(8,128)(2,1)S(1)} %collective-permute-done.8.refs_0_, bf16[2,8,128,128]{3,2,1,0:T(8,128)(2,1)S(1)} %collective-permute-done.13.refs_1_, ...), custom_call_target="tpu_custom_call" | custom-call | flops 2415919104 | bytes 32768 | tf_op jit(solution)/shard_map/gram/pallas_call | solution.py:111
  71.9 8.7 %collective-permute-start.16 = (f32[8,136,128]{2,1,0:T(8,128)S(1)}, f32[8,136,128]{2,1,0:T(8,128)S(1)}, u32[]{:S(2)}, u32[]{:S(2)}) collective-permute-start(f32[8,136,128]{2,1,0:T(8,128)S(1)} %gram.7), channel_id=1, source_target_pairs={{0,8},{8,0},{16,24},{24,16},{32,40},{40,32},{48,56},{56,48},{64,72... | collective-permute-start | bytes 1671176 | tf_op jit(solution)/shard_map/ppermute | solution.py:285
  80.7 3.9 %gram.6.own_ref = f32[8,136,128]{2,1,0:T(8,128)S(1)} custom-call(s32[1]{0:T(128)} %bitcast.me_ref, bf16[16,16,512]{2,1,0:T(8,128)(2,1)S(1)} %all-to-all-done.code_ref, bf16[2,8,128,128]{3,2,1,0:T(8,128)(2,1)S(1)} %collective-permute-done.8.refs_0_, bf16[2,8,128,128]{3,2,1,0:T(8,128)(2,1)S(1)} %collective-permute-done.13.refs_1_, ...), custom_call_target="tpu_custom_call" | custom-call | flops 2415919104 | bytes 32768 | tf_op jit(solution)/shard_map/gram/pallas_call | solution.py:111
  84.5 0.0 collective-permute-done.16.other_ref
  84.5 7.0 %solve.1 = f32[8,128]{1,0:T(8,128)} custom-call(f32[8,136,128]{2,1,0:T(8,128)S(1)} %gram.6.own_ref, f32[8,136,128]{2,1,0:T(8,128)S(1)} %collective-permute-done.16.other_ref), custom_call_target="tpu_custom_call" | custom-call | tf_op jit(solution)/shard_map/solve/pallas_call | solution.py:206
  (13 shorter events, 0.2 us)
Async XLA Ops:
  0.9 7.8 %collective-permute-start = (bf16[128,128]{1,0:T(8,128)(2,1)S(1)}, bf16[128,128]{1,0:T(8,128)(2,1)S(1)}, u32[]{:S(2)}, u32[]{:S(2)}) collective-permute-start(bf16[128,128]{1,0:T(8,128)(2,1)S(1)} %bitcast.25), channel_id=1, source_target_pairs={{0,1},{1,2},{2,3},{3,4},{4,5},{5,6},{6,7},{7,0},{8,9},{9,10},{10,1... | collective-permute-start | bytes 98312 | tf_op jit(solution)/shard_map/ppermute | solution.py:229
  3.4 5.2 %collective-permute-start.1 = (bf16[128,128]{1,0:T(8,128)(2,1)S(1)}, bf16[128,128]{1,0:T(8,128)(2,1)S(1)}, u32[]{:S(2)}, u32[]{:S(2)}) collective-permute-start(bf16[128,128]{1,0:T(8,128)(2,1)S(1)} %bitcast.26), channel_id=1, source_target_pairs={{0,7},{1,0},{2,1},{3,2},{4,3},{5,4},{6,5},{7,6},{8,15},{9,8},{10,9... | collective-permute-start | bytes 98312 | tf_op jit(solution)/shard_map/ppermute | solution.py:229
  8.7 6.7 %collective-permute-start.2 = (bf16[3,128,128]{2,1,0:T(8,128)(2,1)S(1)}, bf16[3,128,128]{2,1,0:T(8,128)(2,1)S(1)}, u32[]{:S(2)}, u32[]{:S(2)}) collective-permute-start(bf16[3,128,128]{2,1,0:T(8,128)(2,1)S(1)} %pad_maximum_fusion.4), channel_id=1, source_target_pairs={{0,3},{1,4},{2,5},{3,6},{4,7},{5,0},{6,1},{7,2},{8,11},{9,12},{10,... | collective-permute-start | bytes 294920 | tf_op jit(solution)/shard_map/ppermute | solution.py:229
  13.0 8.2 %copy-start = (s32[256,256]{1,0:T(8,128)S(1)}, s32[256,256]{1,0:T(8,128)}, u32[]{:S(2)}) copy-start(s32[256,256]{1,0:T(8,128)} %param.5) | copy-start | bytes 786436
  13.0 5.3 %collective-permute-start.3 = (bf16[2,128,128]{2,1,0:T(8,128)(2,1)S(1)}, bf16[2,128,128]{2,1,0:T(8,128)(2,1)S(1)}, u32[]{:S(2)}, u32[]{:S(2)}) collective-permute-start(bf16[2,128,128]{2,1,0:T(8,128)(2,1)S(1)} %pad_maximum_fusion.5), channel_id=1, source_target_pairs={{0,5},{1,6},{2,7},{3,0},{4,1},{5,2},{6,3},{7,4},{8,13},{9,14},{10,... | collective-permute-start | bytes 196616 | tf_op jit(solution)/shard_map/ppermute | solution.py:229
  18.3 6.6 %collective-permute-start.5 = (bf16[8,128,128]{2,1,0:T(8,128)(2,1)S(1)}, bf16[8,128,128]{2,1,0:T(8,128)(2,1)S(1)}, u32[]{:S(2)}, u32[]{:S(2)}) collective-permute-start(bf16[8,128,128]{2,1,0:T(8,128)(2,1)S(1)} %constant_dynamic-update-slice_fusion), channel_id=1, source_target_pairs={{0,16},{8,72},{16,32},{24,88},{32,48},{40,104},{48,0},{56,120},{64... | collective-permute-start | bytes 786440 | tf_op jit(solution)/shard_map/ppermute | solution.py:240
  19.7 5.2 %collective-permute-start.6 = (bf16[8,128,128]{2,1,0:T(8,128)(2,1)S(1)}, bf16[8,128,128]{2,1,0:T(8,128)(2,1)S(1)}, u32[]{:S(2)}, u32[]{:S(2)}) collective-permute-start(bf16[8,128,128]{2,1,0:T(8,128)(2,1)S(1)} %constant_dynamic-update-slice_fusion), channel_id=1, source_target_pairs={{0,48},{8,200},{16,0},{24,216},{32,16},{40,232},{48,32},{56,248},{... | collective-permute-start | bytes 786440 | tf_op jit(solution)/shard_map/ppermute | solution.py:240
  21.2 0.7 copy-start.2
  24.9 2.6 %copy-start.1 = (bf16[256,256]{1,0:T(8,128)(2,1)S(1)}, bf16[256,256]{1,0:T(8,128)(2,1)}, u32[]{:S(2)}) copy-start(bf16[256,256]{1,0:T(8,128)(2,1)} %param.6) | copy-start | bytes 393220
  25.0 15.4 %collective-permute-start.9 = (bf16[2,8,128,128]{3,2,1,0:T(8,128)(2,1)S(1)}, bf16[2,8,128,128]{3,2,1,0:T(8,128)(2,1)S(1)}, u32[]{:S(2)}, u32[]{:S(2)}) collective-permute-start(bf16[2,8,128,128]{3,2,1,0:T(8,128)(2,1)S(1)} %pad_maximum_fusion.refs_1_), channel_id=1, source_target_pairs={{0,192},{8,56},{16,208},{24,8},{32,224},{40,24},{48,240},{56,40},{... | collective-permute-start | bytes 1572872 | tf_op jit(solution)/shard_map/ppermute | solution.py:240
  27.6 10.0 %collective-permute-start.10 = (bf16[4,128,128]{2,1,0:T(8,128)(2,1)S(1)}, bf16[4,128,128]{2,1,0:T(8,128)(2,1)S(1)}, u32[]{:S(2)}, u32[]{:S(2)}) collective-permute-start(bf16[4,128,128]{2,1,0:T(8,128)(2,1)S(1)} %slice.20), channel_id=1, source_target_pairs={{0,16},{8,72},{16,32},{24,88},{32,48},{40,104},{48,0},{56,120},{64... | collective-permute-start | bytes 393224 | tf_op jit(solution)/shard_map/ppermute | solution.py:240
  29.0 8.7 %collective-permute-start.11 = (bf16[4,128,128]{2,1,0:T(8,128)(2,1)S(1)}, bf16[4,128,128]{2,1,0:T(8,128)(2,1)S(1)}, u32[]{:S(2)}, u32[]{:S(2)}) collective-permute-start(bf16[4,128,128]{2,1,0:T(8,128)(2,1)S(1)} %slice.21), channel_id=1, source_target_pairs={{0,48},{8,200},{16,0},{24,216},{32,16},{40,232},{48,32},{56,248},{... | collective-permute-start | bytes 393224 | tf_op jit(solution)/shard_map/ppermute | solution.py:240
  31.3 12.3 %all-to-all-start = ((bf16[16,16,512]{2,1,0:T(8,128)(2,1)}), bf16[16,16,512]{2,1,0:T(8,128)(2,1)S(1)}, u32[]{:S(2)}, u32[]{:S(2)}) async-start(bf16[16,16,512]{2,1,0:T(8,128)(2,1)} %fusion.5), calls=%async_computation | async-start | bytes 524288 | tf_op jit(solution)/shard_map/all_to_all | solution.py:262
  34.9 16.7 %collective-permute-start.4 = (bf16[1,8,128,128]{3,2,1,0:T(8,128)(2,1)S(1)}, bf16[1,8,128,128]{3,2,1,0:T(8,128)(2,1)S(1)}, u32[]{:S(2)}, u32[]{:S(2)}) collective-permute-start(bf16[1,8,128,128]{3,2,1,0:T(8,128)(2,1)S(1)} %bitcast.19), channel_id=1, source_target_pairs={{0,64},{8,24},{16,80},{24,40},{32,96},{40,56},{48,112},{56,8},{64,... | collective-permute-start | bytes 786440 | tf_op jit(solution)/shard_map/ppermute | solution.py:240
  36.2 15.9 %collective-permute-start.15 = (bf16[1,8,128,128]{3,2,1,0:T(8,128)(2,1)S(1)}, bf16[1,8,128,128]{3,2,1,0:T(8,128)(2,1)S(1)}, u32[]{:S(2)}, u32[]{:S(2)}) collective-permute-start(bf16[1,8,128,128]{3,2,1,0:T(8,128)(2,1)S(1)} %bitcast.20), channel_id=1, source_target_pairs={{0,192},{8,56},{16,208},{24,8},{32,224},{40,24},{48,240},{56,40},{... | collective-permute-start | bytes 786440 | tf_op jit(solution)/shard_map/ppermute | solution.py:240
  37.6 13.9 %collective-permute-start.7 = (bf16[2,8,128,128]{3,2,1,0:T(8,128)(2,1)S(1)}, bf16[2,8,128,128]{3,2,1,0:T(8,128)(2,1)S(1)}, u32[]{:S(2)}, u32[]{:S(2)}) collective-permute-start(bf16[2,8,128,128]{3,2,1,0:T(8,128)(2,1)S(1)} %pad_maximum_fusion.refs_1_), channel_id=1, source_target_pairs={{0,64},{8,24},{16,80},{24,40},{32,96},{40,56},{48,112},{56,8},{64,... | collective-permute-start | bytes 1572872 | tf_op jit(solution)/shard_map/ppermute | solution.py:240
  37.7 12.7 %collective-permute-start.12 = (bf16[1,8,128,128]{3,2,1,0:T(8,128)(2,1)S(1)}, bf16[1,8,128,128]{3,2,1,0:T(8,128)(2,1)S(1)}, u32[]{:S(2)}, u32[]{:S(2)}) collective-permute-start(bf16[1,8,128,128]{3,2,1,0:T(8,128)(2,1)S(1)} %maximum_bitcast_fusion.refs_2_), channel_id=1, source_target_pairs={{0,192},{8,56},{16,208},{24,8},{32,224},{40,24},{48,240},{56,40},{... | collective-permute-start | bytes 786440 | tf_op jit(solution)/shard_map/ppermute | solution.py:240
  40.4 13.9 %collective-permute-start.14 = (bf16[1,8,128,128]{3,2,1,0:T(8,128)(2,1)S(1)}, bf16[1,8,128,128]{3,2,1,0:T(8,128)(2,1)S(1)}, u32[]{:S(2)}, u32[]{:S(2)}) collective-permute-start(bf16[1,8,128,128]{3,2,1,0:T(8,128)(2,1)S(1)} %maximum_bitcast_fusion.refs_2_), channel_id=1, source_target_pairs={{0,64},{8,24},{16,80},{24,40},{32,96},{40,56},{48,112},{56,8},{64,... | collective-permute-start | bytes 786440 | tf_op jit(solution)/shard_map/ppermute | solution.py:240
  50.5 17.5 %collective-permute-start.13 = (bf16[2,8,128,128]{3,2,1,0:T(8,128)(2,1)S(1)}, bf16[2,8,128,128]{3,2,1,0:T(8,128)(2,1)S(1)}, u32[]{:S(2)}, u32[]{:S(2)}) collective-permute-start(bf16[2,8,128,128]{3,2,1,0:T(8,128)(2,1)S(1)} %pad_maximum_fusion.2), channel_id=1, source_target_pairs={{0,192},{8,56},{16,208},{24,8},{32,224},{40,24},{48,240},{56,40},{... | collective-permute-start | bytes 1572872 | tf_op jit(solution)/shard_map/ppermute | solution.py:240
  51.6 16.4 %collective-permute-start.8 = (bf16[2,8,128,128]{3,2,1,0:T(8,128)(2,1)S(1)}, bf16[2,8,128,128]{3,2,1,0:T(8,128)(2,1)S(1)}, u32[]{:S(2)}, u32[]{:S(2)}) collective-permute-start(bf16[2,8,128,128]{3,2,1,0:T(8,128)(2,1)S(1)} %pad_maximum_fusion.1), channel_id=1, source_target_pairs={{0,64},{8,24},{16,80},{24,40},{32,96},{40,56},{48,112},{56,8},{64,... | collective-permute-start | bytes 1572872 | tf_op jit(solution)/shard_map/ppermute | solution.py:240
  71.9 12.6 %collective-permute-start.16 = (f32[8,136,128]{2,1,0:T(8,128)S(1)}, f32[8,136,128]{2,1,0:T(8,128)S(1)}, u32[]{:S(2)}, u32[]{:S(2)}) collective-permute-start(f32[8,136,128]{2,1,0:T(8,128)S(1)} %gram.7), channel_id=1, source_target_pairs={{0,8},{8,0},{16,24},{24,16},{32,40},{40,32},{48,56},{56,48},{64,72... | collective-permute-start | bytes 1671176 | tf_op jit(solution)/shard_map/ppermute | solution.py:285

commit v5 on v4

--- a/solution.py
+++ b/solution.py
@@ -269,17 +269,14 @@
     both, own_users, other_users = (0, 1), (0,), (1,)
     half = n_col // 2
     behind, ahead = near_of(block, True)
-    alone = block[None]
-    alone_behind, alone_ahead = near_of(alone, False)
+    three = jnp.stack([block, behind, ahead])
+    three_behind, three_ahead = near_of(three, False)
     far = jnp.concatenate(far_of(behind[:half], ahead[half:], True))[None]
-    sides = jnp.stack([behind, ahead])
-    sides_behind, sides_ahead = near_of(sides, False)
+    own, other = gram(who, 0, code, [three], both)
     far_behind, far_ahead = near_of(far, False)
-    own, other = gram(who, 0, code, [alone, sides, far], both)
-    low, high = far_of(
-        jnp.concatenate([alone_behind, sides_behind[:1]]), jnp.concatenate([sides_ahead[1:], far_ahead]), False
-    )
-    tables = [alone_behind, sides_behind, far_behind, alone_ahead, sides_ahead, far_ahead]
+    own, other = gram(who, 3, code, [far], both, (own, other))
+    low, high = far_of(three_behind[:2], jnp.concatenate([three_ahead[2:], far_ahead]), False)
+    tables = [three_behind, far_behind, three_ahead, far_ahead]
     own, other = gram(who, 4, code, tables, both, (own, other))
     (other,) = gram(who, 12, code, [low, high], other_users, (other,))
     other = lax.ppermute(other, "row", [(i, i ^ 1) for i in range(n_row)])

time: 91.9 us -> 90.4 us (0.984)
  waiting for transfers between devices: 15.1 us -> 13.8 us
    ppermute x12 -> x10, waiting for transfers between devices: 5.76 us -> 2.79 us  [shifted(): return lax.ppermute(value, 'row', pairs)]
    all_to_all x1, waiting for transfers between devices: 3.16 us -> 4.88 us  [half_sweep(): lax.all_to_all(code, 'row', 0, 0, tiled=True, axis_index_groups=same_core)]
    ppermute x1, starting transfers between devices: 8.75 us -> 7.29 us  [half_sweep(): other = lax.ppermute(other, 'row', [(i, i ^ 1) for i in range(n_row)])]
    ppermute x12 -> x10, starting transfers between devices: 14.5 us -> 15.4 us  [shifted(): return lax.ppermute(value, 'row', pairs)]
    pallas_call x4 -> x5, Pallas kernels: 28.2 us -> 28 us  [gram(): pl.pallas_call(functools.partial(gram_kernel, counts=counts, groups=group...]
  transfers between devices with their start and end apart: 18 -> 16, of which waited for: 7 -> 5; matrix products, arithmetic and copies ran while one was open for 2% -> 2% of each run, Pallas kernels for 26% -> 27%
where the time goes in v5:
time: 90.4 us; the launch traced here: 90.2 us
  starting transfers between devices  38.2 us (42%)
  Pallas kernels  35.1 us (39%)
  waiting for transfers between devices  13.8 us (15%)
  local copies, waits for them, and re-layouts  1.49 us (2%)
  other arithmetic  1.37 us (2%)
    pallas_call x5, Pallas kernels, gram(): pl.pallas_call(functools.partial(gram_kernel, counts=counts, groups=group...  28 us
    ppermute x10, starting transfers between devices, shifted(): return lax.ppermute(value, 'row', pairs)  15.4 us
    ppermute x4, starting transfers between devices, along_col(): lax.ppermute(value, 'col', [(i, (i + by) % size) for i in range(size)])  11.2 us
    ppermute x1, starting transfers between devices, half_sweep(): other = lax.ppermute(other, 'row', [(i, i ^ 1) for i in range(n_row)])  7.29 us
    pallas_call x1, Pallas kernels, solve(): pl.pallas_call(solve_kernel, out_shape=jax.ShapeDtypeStruct((users, rank)...  7.05 us
    ppermute x4, waiting for transfers between devices, along_col(): lax.ppermute(value, 'col', [(i, (i + by) % size) for i in range(size)])  6.18 us
    all_to_all x1, waiting for transfers between devices, half_sweep(): lax.all_to_all(code, 'row', 0, 0, tiled=True, axis_index_groups=same_core)  4.88 us
    all_to_all x1, starting transfers between devices, half_sweep(): lax.all_to_all(code, 'row', 0, 0, tiled=True, axis_index_groups=same_core)  4.3 us
  transfers between devices with their start and end apart: 16, of which 5 were waited for; matrix products, arithmetic and copies ran while one was open for 2% of the time, Pallas kernels for 27%

profile of v5, /device:TPU:1, one launch (start us, length us, event | category | flops | bytes accessed | tf_op | source)
XLA Modules:
  0.0 90.2 jit_solution(10672201037932659127)
XLA Ops:
  0.0 0.9 copy.5
  0.9 2.5 %collective-permute-start = (bf16[128,128]{1,0:T(8,128)(2,1)S(1)}, bf16[128,128]{1,0:T(8,128)(2,1)S(1)}, u32[]{:S(2)}, u32[]{:S(2)}) collective-permute-start(bf16[128,128]{1,0:T(8,128)(2,1)S(1)} %bitcast.22), channel_id=1, source_target_pairs={{0,1},{1,2},{2,3},{3,4},{4,5},{5,6},{6,7},{7,0},{8,9},{9,10},{10,1... | collective-permute-start | bytes 98312 | tf_op jit(solution)/shard_map/ppermute | solution.py:229
  3.4 4.0 %collective-permute-start.1 = (bf16[128,128]{1,0:T(8,128)(2,1)S(1)}, bf16[128,128]{1,0:T(8,128)(2,1)S(1)}, u32[]{:S(2)}, u32[]{:S(2)}) collective-permute-start(bf16[128,128]{1,0:T(8,128)(2,1)S(1)} %bitcast.23), channel_id=1, source_target_pairs={{0,7},{1,0},{2,1},{3,2},{4,3},{5,4},{6,5},{7,6},{8,15},{9,8},{10,9... | collective-permute-start | bytes 98312 | tf_op jit(solution)/shard_map/ppermute | solution.py:229
  7.4 1.2 %collective-permute-done = bf16[128,128]{1,0:T(8,128)(2,1)S(1)} collective-permute-done((bf16[128,128]{1,0:T(8,128)(2,1)S(1)}, bf16[128,128]{1,0:T(8,128)(2,1)S(1)}, u32[]{:S(2)}, u32[]{:S(2)}) %collective-permute-start) | collective-permute-done | bytes 32800 | tf_op jit(solution)/shard_map/ppermute | solution.py:229
  8.6 0.0 collective-permute-done.1
  8.7 4.4 %collective-permute-start.2 = (bf16[3,128,128]{2,1,0:T(8,128)(2,1)S(1)}, bf16[3,128,128]{2,1,0:T(8,128)(2,1)S(1)}, u32[]{:S(2)}, u32[]{:S(2)}) collective-permute-start(bf16[3,128,128]{2,1,0:T(8,128)(2,1)S(1)} %pad_maximum_fusion.3), channel_id=1, source_target_pairs={{0,3},{1,4},{2,5},{3,6},{4,7},{5,0},{6,1},{7,2},{8,11},{9,12},{10,... | collective-permute-start | bytes 294920 | tf_op jit(solution)/shard_map/ppermute | solution.py:229
  13.0 0.0 copy-start
  13.0 0.3 collective-permute-start.3
  13.3 2.1 %collective-permute-done.2 = bf16[3,128,128]{2,1,0:T(8,128)(2,1)S(1)} collective-permute-done((bf16[3,128,128]{2,1,0:T(8,128)(2,1)S(1)}, bf16[3,128,128]{2,1,0:T(8,128)(2,1)S(1)}, u32[]{:S(2)}, u32[]{:S(2)}) %collective-permute-start.2) | collective-permute-done | bytes 98336 | tf_op jit(solution)/shard_map/ppermute | solution.py:229
  15.4 2.9 %collective-permute-done.3 = bf16[2,128,128]{2,1,0:T(8,128)(2,1)S(1)} collective-permute-done((bf16[2,128,128]{2,1,0:T(8,128)(2,1)S(1)}, bf16[2,128,128]{2,1,0:T(8,128)(2,1)S(1)}, u32[]{:S(2)}, u32[]{:S(2)}) %collective-permute-start.3) | collective-permute-done | bytes 65568 | tf_op jit(solution)/shard_map/ppermute | solution.py:229
  18.3 0.0 copy-start.2
  18.4 1.4 %collective-permute-start.4 = (bf16[8,128,128]{2,1,0:T(8,128)(2,1)S(1)}, bf16[8,128,128]{2,1,0:T(8,128)(2,1)S(1)}, u32[]{:S(2)}, u32[]{:S(2)}) collective-permute-start(bf16[8,128,128]{2,1,0:T(8,128)(2,1)S(1)} %constant_dynamic-update-slice_fusion), channel_id=1, source_target_pairs={{0,16},{8,72},{16,32},{24,88},{32,48},{40,104},{48,0},{56,120},{64... | collective-permute-start | bytes 786440 | tf_op jit(solution)/shard_map/ppermute | solution.py:240
  19.7 1.5 %collective-permute-start.5 = (bf16[8,128,128]{2,1,0:T(8,128)(2,1)S(1)}, bf16[8,128,128]{2,1,0:T(8,128)(2,1)S(1)}, u32[]{:S(2)}, u32[]{:S(2)}) collective-permute-start(bf16[8,128,128]{2,1,0:T(8,128)(2,1)S(1)} %constant_dynamic-update-slice_fusion), channel_id=1, source_target_pairs={{0,48},{8,200},{16,0},{24,216},{32,16},{40,232},{48,32},{56,248},{... | collective-permute-start | bytes 786440 | tf_op jit(solution)/shard_map/ppermute | solution.py:240
  21.3 0.0 copy-done
  21.3 0.0 copy-done.2
  21.3 0.0 copy-start.1
  21.3 0.4 fusion.4
  21.7 0.5 copy-done.1
  22.2 2.8 %collective-permute-done.5 = bf16[8,128,128]{2,1,0:T(8,128)(2,1)S(1)} collective-permute-done((bf16[8,128,128]{2,1,0:T(8,128)(2,1)S(1)}, bf16[8,128,128]{2,1,0:T(8,128)(2,1)S(1)}, u32[]{:S(2)}, u32[]{:S(2)}) %collective-permute-start.5) | collective-permute-done | bytes 262176 | tf_op jit(solution)/shard_map/ppermute | solution.py:240
  25.0 2.8 %collective-permute-start.10 = (bf16[4,128,128]{2,1,0:T(8,128)(2,1)S(1)}, bf16[4,128,128]{2,1,0:T(8,128)(2,1)S(1)}, u32[]{:S(2)}, u32[]{:S(2)}) collective-permute-start(bf16[4,128,128]{2,1,0:T(8,128)(2,1)S(1)} %slice.21), channel_id=1, source_target_pairs={{0,48},{8,200},{16,0},{24,216},{32,16},{40,232},{48,32},{56,248},{... | collective-permute-start | bytes 393224 | tf_op jit(solution)/shard_map/ppermute | solution.py:240
  27.8 0.0 collective-permute-done.4
  27.8 0.1 collective-permute-start.9
  27.9 0.1 pad_maximum_fusion.refs_0_
  28.0 2.6 %collective-permute-start.8 = (bf16[3,8,128,128]{3,2,1,0:T(8,128)(2,1)S(1)}, bf16[3,8,128,128]{3,2,1,0:T(8,128)(2,1)S(1)}, u32[]{:S(2)}, u32[]{:S(2)}) collective-permute-start(bf16[3,8,128,128]{3,2,1,0:T(8,128)(2,1)S(1)} %pad_maximum_fusion.refs_0_), channel_id=1, source_target_pairs={{0,192},{8,56},{16,208},{24,8},{32,224},{40,24},{48,240},{56,40},{... | collective-permute-start | bytes 2359304 | tf_op jit(solution)/shard_map/ppermute | solution.py:240
  30.5 0.8 fusion.5
  31.3 4.3 %all-to-all-start = ((bf16[16,16,512]{2,1,0:T(8,128)(2,1)}), bf16[16,16,512]{2,1,0:T(8,128)(2,1)S(1)}, u32[]{:S(2)}, u32[]{:S(2)}) async-start(bf16[16,16,512]{2,1,0:T(8,128)(2,1)} %fusion.5), calls=%async_computation | async-start | bytes 524288 | tf_op jit(solution)/shard_map/all_to_all | solution.py:262
  35.6 1.4 %collective-permute-start.6 = (bf16[3,8,128,128]{3,2,1,0:T(8,128)(2,1)S(1)}, bf16[3,8,128,128]{3,2,1,0:T(8,128)(2,1)S(1)}, u32[]{:S(2)}, u32[]{:S(2)}) collective-permute-start(bf16[3,8,128,128]{3,2,1,0:T(8,128)(2,1)S(1)} %pad_maximum_fusion.refs_0_), channel_id=1, source_target_pairs={{0,64},{8,24},{16,80},{24,40},{32,96},{40,56},{48,112},{56,8},{64,... | collective-permute-start | bytes 2359304 | tf_op jit(solution)/shard_map/ppermute | solution.py:240
  37.0 0.0 collective-permute-done.10
  37.0 0.0 collective-permute-done.9
  37.0 1.5 %collective-permute-start.11 = (bf16[1,8,128,128]{3,2,1,0:T(8,128)(2,1)S(1)}, bf16[1,8,128,128]{3,2,1,0:T(8,128)(2,1)S(1)}, u32[]{:S(2)}, u32[]{:S(2)}) collective-permute-start(bf16[1,8,128,128]{3,2,1,0:T(8,128)(2,1)S(1)} %maximum_bitcast_fusion.refs_0_), channel_id=1, source_target_pairs={{0,192},{8,56},{16,208},{24,8},{32,224},{40,24},{48,240},{56,40},{... | collective-permute-start | bytes 786440 | tf_op jit(solution)/shard_map/ppermute | solution.py:240
  38.5 0.1 collective-permute-start.13
  38.6 4.9 %all-to-all-done.code_ref = bf16[16,16,512]{2,1,0:T(8,128)(2,1)S(1)} async-done(((bf16[16,16,512]{2,1,0:T(8,128)(2,1)}), bf16[16,16,512]{2,1,0:T(8,128)(2,1)S(1)}, u32[]{:S(2)}, u32[]{:S(2)}) %all-to-all-start) | async-done | bytes 262176 | tf_op jit(solution)/shard_map/all_to_all | solution.py:262
  43.4 5.1 %gram.5 = (f32[8,136,128]{2,1,0:T(8,128)S(1)}, f32[8,136,128]{2,1,0:T(8,128)S(1)}) custom-call(s32[1]{0:T(128)} %bitcast.me_ref, bf16[16,16,512]{2,1,0:T(8,128)(2,1)S(1)} %all-to-all-done.code_ref, bf16[3,8,128,128]{3,2,1,0:T(8,128)(2,1)S(1)} %pad_maximum_fusion.refs_0_), custom_call_target="tpu_custom_call" | custom-call | flops 3623878656 | bytes 49152 | tf_op jit(solution)/shard_map/gram/pallas_call | solution.py:111
  48.5 1.6 %gram.6 = (f32[8,136,128]{2,1,0:T(8,128)S(1)}, f32[8,136,128]{2,1,0:T(8,128)S(1)}) custom-call(s32[1]{0:T(128)} %bitcast.me_ref, bf16[16,16,512]{2,1,0:T(8,128)(2,1)S(1)} %all-to-all-done.code_ref, bf16[1,8,128,128]{3,2,1,0:T(8,128)(2,1)S(1)} %maximum_bitcast_fusion.refs_0_, f32[8,136,128]{2,1,0:T(8,128)S(1)} %get-tuple-element.11.refs_1_, ...), custom_call_target="tpu_custom_call" | custom-call | flops 1207959552 | bytes 16384 | tf_op jit(solution)/shard_map/gram/pallas_call | solution.py:111
  50.1 0.0 collective-permute-done.8.refs_2_
  50.2 0.0 collective-permute-done.11.refs_3_
  50.2 0.1 pad_maximum_fusion.1
  50.2 4.1 %collective-permute-start.12 = (bf16[2,8,128,128]{3,2,1,0:T(8,128)(2,1)S(1)}, bf16[2,8,128,128]{3,2,1,0:T(8,128)(2,1)S(1)}, u32[]{:S(2)}, u32[]{:S(2)}) collective-permute-start(bf16[2,8,128,128]{3,2,1,0:T(8,128)(2,1)S(1)} %pad_maximum_fusion.1), channel_id=1, source_target_pairs={{0,192},{8,56},{16,208},{24,8},{32,224},{40,24},{48,240},{56,40},{... | collective-permute-start | bytes 1572872 | tf_op jit(solution)/shard_map/ppermute | solution.py:240
  54.3 0.0 collective-permute-done.6.refs_0_
  54.3 0.1 collective-permute-start.7
  54.4 0.0 collective-permute-done.13.refs_1_
  54.4 13.6 %gram.7 = (f32[8,136,128]{2,1,0:T(8,128)S(1)}, f32[8,136,128]{2,1,0:T(8,128)S(1)}) custom-call(s32[1]{0:T(128)} %bitcast.me_ref, bf16[16,16,512]{2,1,0:T(8,128)(2,1)S(1)} %all-to-all-done.code_ref, bf16[3,8,128,128]{3,2,1,0:T(8,128)(2,1)S(1)} %collective-permute-done.6.refs_0_, bf16[1,8,128,128]{3,2,1,0:T(8,128)(2,1)S(1)} %collective-permute-done.13.refs_1_, ...), custom_call_target="tpu_custom_call" | custom-call | flops 9663676416 | bytes 131072 | tf_op jit(solution)/shard_map/gram/pallas_call | solution.py:111
  68.0 0.0 collective-permute-done.12.refs_1_
  68.0 0.0 collective-permute-done.7.refs_0_
  68.0 3.9 %gram.9 = f32[8,136,128]{2,1,0:T(8,128)S(1)} custom-call(s32[1]{0:T(128)} %bitcast.me_ref, bf16[16,16,512]{2,1,0:T(8,128)(2,1)S(1)} %all-to-all-done.code_ref, bf16[2,8,128,128]{3,2,1,0:T(8,128)(2,1)S(1)} %collective-permute-done.7.refs_0_, bf16[2,8,128,128]{3,2,1,0:T(8,128)(2,1)S(1)} %collective-permute-done.12.refs_1_, ...), custom_call_target="tpu_custom_call" | custom-call | flops 2415919104 | bytes 32768 | tf_op jit(solution)/shard_map/gram/pallas_call | solution.py:111
  71.9 7.3 %collective-permute-start.14 = (f32[8,136,128]{2,1,0:T(8,128)S(1)}, f32[8,136,128]{2,1,0:T(8,128)S(1)}, u32[]{:S(2)}, u32[]{:S(2)}) collective-permute-start(f32[8,136,128]{2,1,0:T(8,128)S(1)} %gram.9), channel_id=1, source_target_pairs={{0,8},{8,0},{16,24},{24,16},{32,40},{40,32},{48,56},{56,48},{64,72... | collective-permute-start | bytes 1671176 | tf_op jit(solution)/shard_map/ppermute | solution.py:282
  79.2 3.9 %gram.8.own_ref = f32[8,136,128]{2,1,0:T(8,128)S(1)} custom-call(s32[1]{0:T(128)} %bitcast.me_ref, bf16[16,16,512]{2,1,0:T(8,128)(2,1)S(1)} %all-to-all-done.code_ref, bf16[2,8,128,128]{3,2,1,0:T(8,128)(2,1)S(1)} %collective-permute-done.7.refs_0_, bf16[2,8,128,128]{3,2,1,0:T(8,128)(2,1)S(1)} %collective-permute-done.12.refs_1_, ...), custom_call_target="tpu_custom_call" | custom-call | flops 2415919104 | bytes 32768 | tf_op jit(solution)/shard_map/gram/pallas_call | solution.py:111
  83.1 0.0 collective-permute-done.14.other_ref
  83.1 7.0 %solve.1 = f32[8,128]{1,0:T(8,128)} custom-call(f32[8,136,128]{2,1,0:T(8,128)S(1)} %gram.8.own_ref, f32[8,136,128]{2,1,0:T(8,128)S(1)} %collective-permute-done.14.other_ref), custom_call_target="tpu_custom_call" | custom-call | tf_op jit(solution)/shard_map/solve/pallas_call | solution.py:206
  (13 shorter events, 0.2 us)
Async XLA Ops:
  0.9 7.8 %collective-permute-start = (bf16[128,128]{1,0:T(8,128)(2,1)S(1)}, bf16[128,128]{1,0:T(8,128)(2,1)S(1)}, u32[]{:S(2)}, u32[]{:S(2)}) collective-permute-start(bf16[128,128]{1,0:T(8,128)(2,1)S(1)} %bitcast.22), channel_id=1, source_target_pairs={{0,1},{1,2},{2,3},{3,4},{4,5},{5,6},{6,7},{7,0},{8,9},{9,10},{10,1... | collective-permute-start | bytes 98312 | tf_op jit(solution)/shard_map/ppermute | solution.py:229
  3.4 5.2 %collective-permute-start.1 = (bf16[128,128]{1,0:T(8,128)(2,1)S(1)}, bf16[128,128]{1,0:T(8,128)(2,1)S(1)}, u32[]{:S(2)}, u32[]{:S(2)}) collective-permute-start(bf16[128,128]{1,0:T(8,128)(2,1)S(1)} %bitcast.23), channel_id=1, source_target_pairs={{0,7},{1,0},{2,1},{3,2},{4,3},{5,4},{6,5},{7,6},{8,15},{9,8},{10,9... | collective-permute-start | bytes 98312 | tf_op jit(solution)/shard_map/ppermute | solution.py:229
  8.7 6.7 %collective-permute-start.2 = (bf16[3,128,128]{2,1,0:T(8,128)(2,1)S(1)}, bf16[3,128,128]{2,1,0:T(8,128)(2,1)S(1)}, u32[]{:S(2)}, u32[]{:S(2)}) collective-permute-start(bf16[3,128,128]{2,1,0:T(8,128)(2,1)S(1)} %pad_maximum_fusion.3), channel_id=1, source_target_pairs={{0,3},{1,4},{2,5},{3,6},{4,7},{5,0},{6,1},{7,2},{8,11},{9,12},{10,... | collective-permute-start | bytes 294920 | tf_op jit(solution)/shard_map/ppermute | solution.py:229
  13.0 8.2 %copy-start = (s32[256,256]{1,0:T(8,128)S(1)}, s32[256,256]{1,0:T(8,128)}, u32[]{:S(2)}) copy-start(s32[256,256]{1,0:T(8,128)} %param.5) | copy-start | bytes 786436
  13.0 5.3 %collective-permute-start.3 = (bf16[2,128,128]{2,1,0:T(8,128)(2,1)S(1)}, bf16[2,128,128]{2,1,0:T(8,128)(2,1)S(1)}, u32[]{:S(2)}, u32[]{:S(2)}) collective-permute-start(bf16[2,128,128]{2,1,0:T(8,128)(2,1)S(1)} %pad_maximum_fusion.4), channel_id=1, source_target_pairs={{0,5},{1,6},{2,7},{3,0},{4,1},{5,2},{6,3},{7,4},{8,13},{9,14},{10,... | collective-permute-start | bytes 196616 | tf_op jit(solution)/shard_map/ppermute | solution.py:229
  18.3 2.9 %copy-start.2 = (s32[256,1]{0,1:T(1,128)S(1)}, s32[256,1]{0,1:T(1,128)}, u32[]{:S(2)}) copy-start(s32[256,1]{0,1:T(1,128)} %param.7) | copy-start | bytes 3076
  18.4 9.4 %collective-permute-start.4 = (bf16[8,128,128]{2,1,0:T(8,128)(2,1)S(1)}, bf16[8,128,128]{2,1,0:T(8,128)(2,1)S(1)}, u32[]{:S(2)}, u32[]{:S(2)}) collective-permute-start(bf16[8,128,128]{2,1,0:T(8,128)(2,1)S(1)} %constant_dynamic-update-slice_fusion), channel_id=1, source_target_pairs={{0,16},{8,72},{16,32},{24,88},{32,48},{40,104},{48,0},{56,120},{64... | collective-permute-start | bytes 786440 | tf_op jit(solution)/shard_map/ppermute | solution.py:240
  19.7 5.2 %collective-permute-start.5 = (bf16[8,128,128]{2,1,0:T(8,128)(2,1)S(1)}, bf16[8,128,128]{2,1,0:T(8,128)(2,1)S(1)}, u32[]{:S(2)}, u32[]{:S(2)}) collective-permute-start(bf16[8,128,128]{2,1,0:T(8,128)(2,1)S(1)} %constant_dynamic-update-slice_fusion), channel_id=1, source_target_pairs={{0,48},{8,200},{16,0},{24,216},{32,16},{40,232},{48,32},{56,248},{... | collective-permute-start | bytes 786440 | tf_op jit(solution)/shard_map/ppermute | solution.py:240
  21.3 0.9 %copy-start.1 = (bf16[256,256]{1,0:T(8,128)(2,1)S(1)}, bf16[256,256]{1,0:T(8,128)(2,1)}, u32[]{:S(2)}) copy-start(bf16[256,256]{1,0:T(8,128)(2,1)} %param.6) | copy-start | bytes 393220
  25.0 12.0 %collective-permute-start.10 = (bf16[4,128,128]{2,1,0:T(8,128)(2,1)S(1)}, bf16[4,128,128]{2,1,0:T(8,128)(2,1)S(1)}, u32[]{:S(2)}, u32[]{:S(2)}) collective-permute-start(bf16[4,128,128]{2,1,0:T(8,128)(2,1)S(1)} %slice.21), channel_id=1, source_target_pairs={{0,48},{8,200},{16,0},{24,216},{32,16},{40,232},{48,32},{56,248},{... | collective-permute-start | bytes 393224 | tf_op jit(solution)/shard_map/ppermute | solution.py:240
  27.8 9.2 %collective-permute-start.9 = (bf16[4,128,128]{2,1,0:T(8,128)(2,1)S(1)}, bf16[4,128,128]{2,1,0:T(8,128)(2,1)S(1)}, u32[]{:S(2)}, u32[]{:S(2)}) collective-permute-start(bf16[4,128,128]{2,1,0:T(8,128)(2,1)S(1)} %slice.20), channel_id=1, source_target_pairs={{0,16},{8,72},{16,32},{24,88},{32,48},{40,104},{48,0},{56,120},{64... | collective-permute-start | bytes 393224 | tf_op jit(solution)/shard_map/ppermute | solution.py:240
  28.0 22.1 %collective-permute-start.8 = (bf16[3,8,128,128]{3,2,1,0:T(8,128)(2,1)S(1)}, bf16[3,8,128,128]{3,2,1,0:T(8,128)(2,1)S(1)}, u32[]{:S(2)}, u32[]{:S(2)}) collective-permute-start(bf16[3,8,128,128]{3,2,1,0:T(8,128)(2,1)S(1)} %pad_maximum_fusion.refs_0_), channel_id=1, source_target_pairs={{0,192},{8,56},{16,208},{24,8},{32,224},{40,24},{48,240},{56,40},{... | collective-permute-start | bytes 2359304 | tf_op jit(solution)/shard_map/ppermute | solution.py:240
  31.3 12.1 %all-to-all-start = ((bf16[16,16,512]{2,1,0:T(8,128)(2,1)}), bf16[16,16,512]{2,1,0:T(8,128)(2,1)S(1)}, u32[]{:S(2)}, u32[]{:S(2)}) async-start(bf16[16,16,512]{2,1,0:T(8,128)(2,1)} %fusion.5), calls=%async_computation | async-start | bytes 524288 | tf_op jit(solution)/shard_map/all_to_all | solution.py:262
  35.6 18.7 %collective-permute-start.6 = (bf16[3,8,128,128]{3,2,1,0:T(8,128)(2,1)S(1)}, bf16[3,8,128,128]{3,2,1,0:T(8,128)(2,1)S(1)}, u32[]{:S(2)}, u32[]{:S(2)}) collective-permute-start(bf16[3,8,128,128]{3,2,1,0:T(8,128)(2,1)S(1)} %pad_maximum_fusion.refs_0_), channel_id=1, source_target_pairs={{0,64},{8,24},{16,80},{24,40},{32,96},{40,56},{48,112},{56,8},{64,... | collective-permute-start | bytes 2359304 | tf_op jit(solution)/shard_map/ppermute | solution.py:240
  37.0 13.2 %collective-permute-start.11 = (bf16[1,8,128,128]{3,2,1,0:T(8,128)(2,1)S(1)}, bf16[1,8,128,128]{3,2,1,0:T(8,128)(2,1)S(1)}, u32[]{:S(2)}, u32[]{:S(2)}) collective-permute-start(bf16[1,8,128,128]{3,2,1,0:T(8,128)(2,1)S(1)} %maximum_bitcast_fusion.refs_0_), channel_id=1, source_target_pairs={{0,192},{8,56},{16,208},{24,8},{32,224},{40,24},{48,240},{56,40},{... | collective-permute-start | bytes 786440 | tf_op jit(solution)/shard_map/ppermute | solution.py:240
  38.5 16.0 %collective-permute-start.13 = (bf16[1,8,128,128]{3,2,1,0:T(8,128)(2,1)S(1)}, bf16[1,8,128,128]{3,2,1,0:T(8,128)(2,1)S(1)}, u32[]{:S(2)}, u32[]{:S(2)}) collective-permute-start(bf16[1,8,128,128]{3,2,1,0:T(8,128)(2,1)S(1)} %maximum_bitcast_fusion.refs_0_), channel_id=1, source_target_pairs={{0,64},{8,24},{16,80},{24,40},{32,96},{40,56},{48,112},{56,8},{64,... | collective-permute-start | bytes 786440 | tf_op jit(solution)/shard_map/ppermute | solution.py:240
  50.2 17.8 %collective-permute-start.12 = (bf16[2,8,128,128]{3,2,1,0:T(8,128)(2,1)S(1)}, bf16[2,8,128,128]{3,2,1,0:T(8,128)(2,1)S(1)}, u32[]{:S(2)}, u32[]{:S(2)}) collective-permute-start(bf16[2,8,128,128]{3,2,1,0:T(8,128)(2,1)S(1)} %pad_maximum_fusion.1), channel_id=1, source_target_pairs={{0,192},{8,56},{16,208},{24,8},{32,224},{40,24},{48,240},{56,40},{... | collective-permute-start | bytes 1572872 | tf_op jit(solution)/shard_map/ppermute | solution.py:240
  54.3 13.7 %collective-permute-start.7 = (bf16[2,8,128,128]{3,2,1,0:T(8,128)(2,1)S(1)}, bf16[2,8,128,128]{3,2,1,0:T(8,128)(2,1)S(1)}, u32[]{:S(2)}, u32[]{:S(2)}) collective-permute-start(bf16[2,8,128,128]{3,2,1,0:T(8,128)(2,1)S(1)} %slice.18), channel_id=1, source_target_pairs={{0,64},{8,24},{16,80},{24,40},{32,96},{40,56},{48,112},{56,8},{64,... | collective-permute-start | bytes 1572872 | tf_op jit(solution)/shard_map/ppermute | solution.py:240
  71.9 11.2 %collective-permute-start.14 = (f32[8,136,128]{2,1,0:T(8,128)S(1)}, f32[8,136,128]{2,1,0:T(8,128)S(1)}, u32[]{:S(2)}, u32[]{:S(2)}) collective-permute-start(f32[8,136,128]{2,1,0:T(8,128)S(1)} %gram.9), channel_id=1, source_target_pairs={{0,8},{8,0},{16,24},{24,16},{32,40},{40,32},{48,56},{56,48},{64,72... | collective-permute-start | bytes 1671176 | tf_op jit(solution)/shard_map/ppermute | solution.py:282

commit v6 on v4

--- a/solution.py
+++ b/solution.py
@@ -213,9 +213,9 @@
 
 
 def coded(item_index, counts, begin, items):
-    item_index = (item_index + (items - begin)) % items
-    low = item_index % LOW
-    value = jnp.where(low < HALF, low + HALF, -low) * (1 << (item_index // LOW))
+    item_index = (item_index + (items - begin)) & (items - 1)
+    low = item_index & (LOW - 1)
+    value = jnp.where(low < HALF, low + HALF, -low) << (item_index >> 8)
     position = lax.broadcasted_iota(jnp.int32, item_index.shape, 1)
     return jnp.where(position < counts, value, 0).astype(BF16)
 
@@ -272,10 +272,11 @@
     alone = block[None]
     alone_behind, alone_ahead = near_of(alone, False)
     far = jnp.concatenate(far_of(behind[:half], ahead[half:], True))[None]
+    own, other = gram(who, 0, code, [alone], both)
     sides = jnp.stack([behind, ahead])
     sides_behind, sides_ahead = near_of(sides, False)
     far_behind, far_ahead = near_of(far, False)
-    own, other = gram(who, 0, code, [alone, sides, far], both)
+    own, other = gram(who, 1, code, [sides, far], both, (own, other))
     low, high = far_of(
         jnp.concatenate([alone_behind, sides_behind[:1]]), jnp.concatenate([sides_ahead[1:], far_ahead]), False
     )

time: 91.9 us -> 94.9 us (1.033)
  starting transfers between devices: 38.1 us -> 42.2 us
    ppermute x12, starting transfers between devices: 14.5 us -> 16.7 us  [shifted(): return lax.ppermute(value, 'row', pairs)]
    all_to_all x1, waiting for transfers between devices: 3.16 us -> 2 us  [half_sweep(): lax.all_to_all(code, 'row', 0, 0, tiled=True, axis_index_groups=same_core)]
    ppermute x1, starting transfers between devices: 8.75 us -> 9.87 us  [half_sweep(): other = lax.ppermute(other, 'row', [(i, i ^ 1) for i in range(n_row)])]
    pallas_call x4 -> x5, Pallas kernels: 28.2 us -> 28.1 us  [gram(): pl.pallas_call(functools.partial(gram_kernel, counts=counts, groups=group...]
  transfers between devices with their start and end apart: 18 -> 18, of which waited for: 7 -> 7; matrix products, arithmetic and copies ran while one was open for 2% -> 1% of each run, Pallas kernels for 26% -> 26%
where the time goes in v6:
time: 94.9 us; the launch traced here: 94.7 us
  starting transfers between devices  42.2 us (44%)
  Pallas kernels  35.1 us (37%)
  waiting for transfers between devices  14.3 us (15%)
  local copies, waits for them, and re-layouts  1.77 us (2%)
  other arithmetic  1.1 us (1%)
    pallas_call x5, Pallas kernels, gram(): pl.pallas_call(functools.partial(gram_kernel, counts=counts, groups=group...  28.1 us
    ppermute x12, starting transfers between devices, shifted(): return lax.ppermute(value, 'row', pairs)  16.7 us
    ppermute x4, starting transfers between devices, along_col(): lax.ppermute(value, 'col', [(i, (i + by) % size) for i in range(size)])  11.2 us
    ppermute x1, starting transfers between devices, half_sweep(): other = lax.ppermute(other, 'row', [(i, i ^ 1) for i in range(n_row)])  9.87 us
    pallas_call x1, Pallas kernels, solve(): pl.pallas_call(solve_kernel, out_shape=jax.ShapeDtypeStruct((users, rank)...  7.05 us
    ppermute x4, waiting for transfers between devices, along_col(): lax.ppermute(value, 'col', [(i, (i + by) % size) for i in range(size)])  6.18 us
    ppermute x12, waiting for transfers between devices, shifted(): return lax.ppermute(value, 'row', pairs)  6.15 us
    all_to_all x1, starting transfers between devices, half_sweep(): lax.all_to_all(code, 'row', 0, 0, tiled=True, axis_index_groups=same_core)  4.38 us
  transfers between devices with their start and end apart: 18, of which 7 were waited for; matrix products, arithmetic and copies ran while one was open for 1% of the time, Pallas kernels for 26%

profile of v6, /device:TPU:1, one launch (start us, length us, event | category | flops | bytes accessed | tf_op | source)
XLA Modules:
  0.0 94.7 jit_solution(12730424255023578440)
XLA Ops:
  0.0 0.9 copy.5
  0.9 2.5 %collective-permute-start = (bf16[128,128]{1,0:T(8,128)(2,1)S(1)}, bf16[128,128]{1,0:T(8,128)(2,1)S(1)}, u32[]{:S(2)}, u32[]{:S(2)}) collective-permute-start(bf16[128,128]{1,0:T(8,128)(2,1)S(1)} %bitcast.25), channel_id=1, source_target_pairs={{0,1},{1,2},{2,3},{3,4},{4,5},{5,6},{6,7},{7,0},{8,9},{9,10},{10,1... | collective-permute-start | bytes 98312 | tf_op jit(solution)/shard_map/ppermute | solution.py:229
  3.4 4.0 %collective-permute-start.1 = (bf16[128,128]{1,0:T(8,128)(2,1)S(1)}, bf16[128,128]{1,0:T(8,128)(2,1)S(1)}, u32[]{:S(2)}, u32[]{:S(2)}) collective-permute-start(bf16[128,128]{1,0:T(8,128)(2,1)S(1)} %bitcast.26), channel_id=1, source_target_pairs={{0,7},{1,0},{2,1},{3,2},{4,3},{5,4},{6,5},{7,6},{8,15},{9,8},{10,9... | collective-permute-start | bytes 98312 | tf_op jit(solution)/shard_map/ppermute | solution.py:229
  7.4 1.2 %collective-permute-done = bf16[128,128]{1,0:T(8,128)(2,1)S(1)} collective-permute-done((bf16[128,128]{1,0:T(8,128)(2,1)S(1)}, bf16[128,128]{1,0:T(8,128)(2,1)S(1)}, u32[]{:S(2)}, u32[]{:S(2)}) %collective-permute-start) | collective-permute-done | bytes 32800 | tf_op jit(solution)/shard_map/ppermute | solution.py:229
  8.6 0.0 collective-permute-done.1
  8.7 4.4 %collective-permute-start.2 = (bf16[3,128,128]{2,1,0:T(8,128)(2,1)S(1)}, bf16[3,128,128]{2,1,0:T(8,128)(2,1)S(1)}, u32[]{:S(2)}, u32[]{:S(2)}) collective-permute-start(bf16[3,128,128]{2,1,0:T(8,128)(2,1)S(1)} %pad_maximum_fusion.4), channel_id=1, source_target_pairs={{0,3},{1,4},{2,5},{3,6},{4,7},{5,0},{6,1},{7,2},{8,11},{9,12},{10,... | collective-permute-start | bytes 294920 | tf_op jit(solution)/shard_map/ppermute | solution.py:229
  13.0 0.0 copy-start
  13.0 0.3 collective-permute-start.3
  13.3 2.1 %collective-permute-done.2 = bf16[3,128,128]{2,1,0:T(8,128)(2,1)S(1)} collective-permute-done((bf16[3,128,128]{2,1,0:T(8,128)(2,1)S(1)}, bf16[3,128,128]{2,1,0:T(8,128)(2,1)S(1)}, u32[]{:S(2)}, u32[]{:S(2)}) %collective-permute-start.2) | collective-permute-done | bytes 98336 | tf_op jit(solution)/shard_map/ppermute | solution.py:229
  15.4 2.9 %collective-permute-done.3 = bf16[2,128,128]{2,1,0:T(8,128)(2,1)S(1)} collective-permute-done((bf16[2,128,128]{2,1,0:T(8,128)(2,1)S(1)}, bf16[2,128,128]{2,1,0:T(8,128)(2,1)S(1)}, u32[]{:S(2)}, u32[]{:S(2)}) %collective-permute-start.3) | collective-permute-done | bytes 65568 | tf_op jit(solution)/shard_map/ppermute | solution.py:229
  18.3 0.0 copy-start.2
  18.4 1.4 %collective-permute-start.5 = (bf16[8,128,128]{2,1,0:T(8,128)(2,1)S(1)}, bf16[8,128,128]{2,1,0:T(8,128)(2,1)S(1)}, u32[]{:S(2)}, u32[]{:S(2)}) collective-permute-start(bf16[8,128,128]{2,1,0:T(8,128)(2,1)S(1)} %constant_dynamic-update-slice_fusion), channel_id=1, source_target_pairs={{0,16},{8,72},{16,32},{24,88},{32,48},{40,104},{48,0},{56,120},{64... | collective-permute-start | bytes 786440 | tf_op jit(solution)/shard_map/ppermute | solution.py:240
  19.7 1.5 %collective-permute-start.6 = (bf16[8,128,128]{2,1,0:T(8,128)(2,1)S(1)}, bf16[8,128,128]{2,1,0:T(8,128)(2,1)S(1)}, u32[]{:S(2)}, u32[]{:S(2)}) collective-permute-start(bf16[8,128,128]{2,1,0:T(8,128)(2,1)S(1)} %constant_dynamic-update-slice_fusion), channel_id=1, source_target_pairs={{0,48},{8,200},{16,0},{24,216},{32,16},{40,232},{48,32},{56,248},{... | collective-permute-start | bytes 786440 | tf_op jit(solution)/shard_map/ppermute | solution.py:240
  21.3 0.0 copy-done
  21.3 0.0 copy-done.2
  21.3 0.0 copy-start.1
  21.3 0.1 select_convert_fusion
  21.4 0.8 copy-done.1
  22.2 2.7 %collective-permute-done.5 = bf16[8,128,128]{2,1,0:T(8,128)(2,1)S(1)} collective-permute-done((bf16[8,128,128]{2,1,0:T(8,128)(2,1)S(1)}, bf16[8,128,128]{2,1,0:T(8,128)(2,1)S(1)}, u32[]{:S(2)}, u32[]{:S(2)}) %collective-permute-start.5) | collective-permute-done | bytes 262176 | tf_op jit(solution)/shard_map/ppermute | solution.py:240
  24.9 0.0 collective-permute-done.6
  25.0 0.1 pad_maximum_fusion.refs_0_
  25.0 2.6 %collective-permute-start.9 = (bf16[2,8,128,128]{3,2,1,0:T(8,128)(2,1)S(1)}, bf16[2,8,128,128]{3,2,1,0:T(8,128)(2,1)S(1)}, u32[]{:S(2)}, u32[]{:S(2)}) collective-permute-start(bf16[2,8,128,128]{3,2,1,0:T(8,128)(2,1)S(1)} %pad_maximum_fusion.refs_0_), channel_id=1, source_target_pairs={{0,192},{8,56},{16,208},{24,8},{32,224},{40,24},{48,240},{56,40},{... | collective-permute-start | bytes 1572872 | tf_op jit(solution)/shard_map/ppermute | solution.py:240
  27.6 0.8 fusion
  28.3 4.4 %all-to-all-start = ((bf16[16,16,512]{2,1,0:T(8,128)(2,1)}), bf16[16,16,512]{2,1,0:T(8,128)(2,1)S(1)}, u32[]{:S(2)}, u32[]{:S(2)}) async-start(bf16[16,16,512]{2,1,0:T(8,128)(2,1)} %fusion), calls=%async_computation | async-start | bytes 524288 | tf_op jit(solution)/shard_map/all_to_all | solution.py:262
  32.7 1.4 %collective-permute-start.10 = (bf16[4,128,128]{2,1,0:T(8,128)(2,1)S(1)}, bf16[4,128,128]{2,1,0:T(8,128)(2,1)S(1)}, u32[]{:S(2)}, u32[]{:S(2)}) collective-permute-start(bf16[4,128,128]{2,1,0:T(8,128)(2,1)S(1)} %slice.20), channel_id=1, source_target_pairs={{0,16},{8,72},{16,32},{24,88},{32,48},{40,104},{48,0},{56,120},{64... | collective-permute-start | bytes 393224 | tf_op jit(solution)/shard_map/ppermute | solution.py:240
  34.2 1.4 %collective-permute-start.11 = (bf16[4,128,128]{2,1,0:T(8,128)(2,1)S(1)}, bf16[4,128,128]{2,1,0:T(8,128)(2,1)S(1)}, u32[]{:S(2)}, u32[]{:S(2)}) collective-permute-start(bf16[4,128,128]{2,1,0:T(8,128)(2,1)S(1)} %slice.21), channel_id=1, source_target_pairs={{0,48},{8,200},{16,0},{24,216},{32,16},{40,232},{48,32},{56,248},{... | collective-permute-start | bytes 393224 | tf_op jit(solution)/shard_map/ppermute | solution.py:240
  35.6 1.4 %collective-permute-start.4 = (bf16[1,8,128,128]{3,2,1,0:T(8,128)(2,1)S(1)}, bf16[1,8,128,128]{3,2,1,0:T(8,128)(2,1)S(1)}, u32[]{:S(2)}, u32[]{:S(2)}) collective-permute-start(bf16[1,8,128,128]{3,2,1,0:T(8,128)(2,1)S(1)} %bitcast.19), channel_id=1, source_target_pairs={{0,64},{8,24},{16,80},{24,40},{32,96},{40,56},{48,112},{56,8},{64,... | collective-permute-start | bytes 786440 | tf_op jit(solution)/shard_map/ppermute | solution.py:240
  37.0 1.3 %collective-permute-start.15 = (bf16[1,8,128,128]{3,2,1,0:T(8,128)(2,1)S(1)}, bf16[1,8,128,128]{3,2,1,0:T(8,128)(2,1)S(1)}, u32[]{:S(2)}, u32[]{:S(2)}) collective-permute-start(bf16[1,8,128,128]{3,2,1,0:T(8,128)(2,1)S(1)} %bitcast.20), channel_id=1, source_target_pairs={{0,192},{8,56},{16,208},{24,8},{32,224},{40,24},{48,240},{56,40},{... | collective-permute-start | bytes 786440 | tf_op jit(solution)/shard_map/ppermute | solution.py:240
  38.3 2.0 %all-to-all-done.code_ref = bf16[16,16,512]{2,1,0:T(8,128)(2,1)S(1)} async-done(((bf16[16,16,512]{2,1,0:T(8,128)(2,1)}), bf16[16,16,512]{2,1,0:T(8,128)(2,1)S(1)}, u32[]{:S(2)}, u32[]{:S(2)}) %all-to-all-start) | async-done | bytes 262176 | tf_op jit(solution)/shard_map/all_to_all | solution.py:262
  40.3 1.6 %gram.5 = (f32[8,136,128]{2,1,0:T(8,128)S(1)}, f32[8,136,128]{2,1,0:T(8,128)S(1)}) custom-call(s32[1]{0:T(128)} %bitcast.me_ref, bf16[16,16,512]{2,1,0:T(8,128)(2,1)S(1)} %all-to-all-done.code_ref, bf16[1,8,128,128]{3,2,1,0:T(8,128)(2,1)S(1)} %bitcast.21), custom_call_target="tpu_custom_call" | custom-call | flops 1207959552 | bytes 16384 | tf_op jit(solution)/shard_map/gram/pallas_call | solution.py:111
  41.9 0.0 collective-permute-done.10
  41.9 0.9 collective-permute-start.7
  42.8 0.0 collective-permute-done.11
  42.8 2.0 %collective-permute-start.12 = (bf16[1,8,128,128]{3,2,1,0:T(8,128)(2,1)S(1)}, bf16[1,8,128,128]{3,2,1,0:T(8,128)(2,1)S(1)}, u32[]{:S(2)}, u32[]{:S(2)}) collective-permute-start(bf16[1,8,128,128]{3,2,1,0:T(8,128)(2,1)S(1)} %maximum_bitcast_fusion.refs_1_), channel_id=1, source_target_pairs={{0,192},{8,56},{16,208},{24,8},{32,224},{40,24},{48,240},{56,40},{... | collective-permute-start | bytes 786440 | tf_op jit(solution)/shard_map/ppermute | solution.py:240
  44.7 0.0 collective-permute-done.9.refs_4_
  44.8 0.0 collective-permute-start.14
  44.8 5.1 %gram.6 = (f32[8,136,128]{2,1,0:T(8,128)S(1)}, f32[8,136,128]{2,1,0:T(8,128)S(1)}) custom-call(s32[1]{0:T(128)} %bitcast.me_ref, bf16[16,16,512]{2,1,0:T(8,128)(2,1)S(1)} %all-to-all-done.code_ref, bf16[2,8,128,128]{3,2,1,0:T(8,128)(2,1)S(1)} %pad_maximum_fusion.refs_0_, bf16[1,8,128,128]{3,2,1,0:T(8,128)(2,1)S(1)} %maximum_bitcast_fusion.refs_1_, ...), custom_call_target="tpu_custom_call" | custom-call | flops 3623878656 | bytes 49152 | tf_op jit(solution)/shard_map/gram/pallas_call | solution.py:111
  49.9 0.0 collective-permute-done.12.refs_5_
  49.9 0.1 pad_maximum_fusion.2
  49.9 2.8 %collective-permute-start.13 = (bf16[2,8,128,128]{3,2,1,0:T(8,128)(2,1)S(1)}, bf16[2,8,128,128]{3,2,1,0:T(8,128)(2,1)S(1)}, u32[]{:S(2)}, u32[]{:S(2)}) collective-permute-start(bf16[2,8,128,128]{3,2,1,0:T(8,128)(2,1)S(1)} %pad_maximum_fusion.2), channel_id=1, source_target_pairs={{0,192},{8,56},{16,208},{24,8},{32,224},{40,24},{48,240},{56,40},{... | collective-permute-start | bytes 1572872 | tf_op jit(solution)/shard_map/ppermute | solution.py:240
  52.8 0.8 collective-permute-done.7.refs_1_
  53.5 0.0 collective-permute-done.4.refs_0_
  53.6 0.1 pad_maximum_fusion.1
  53.6 0.1 collective-permute-start.8
  53.7 0.0 collective-permute-done.15.refs_3_
  53.7 2.6 %collective-permute-done.14.refs_2_ = bf16[1,8,128,128]{3,2,1,0:T(8,128)(2,1)S(1)} collective-permute-done((bf16[1,8,128,128]{3,2,1,0:T(8,128)(2,1)S(1)}, bf16[1,8,128,128]{3,2,1,0:T(8,128)(2,1)S(1)}, u32[]{:S(2)}, u32[]{:S(2)}) %collective-permute-start.14) | collective-permute-done | bytes 262176 | tf_op jit(solution)/shard_map/ppermute | solution.py:240
  56.3 13.6 %gram.7 = (f32[8,136,128]{2,1,0:T(8,128)S(1)}, f32[8,136,128]{2,1,0:T(8,128)S(1)}) custom-call(s32[1]{0:T(128)} %bitcast.me_ref, bf16[16,16,512]{2,1,0:T(8,128)(2,1)S(1)} %all-to-all-done.code_ref, bf16[1,8,128,128]{3,2,1,0:T(8,128)(2,1)S(1)} %collective-permute-done.4.refs_0_, bf16[2,8,128,128]{3,2,1,0:T(8,128)(2,1)S(1)} %collective-permute-done.7.refs_1_, ...), custom_call_target="tpu_custom_call" | custom-call | flops 9663676416 | bytes 131072 | tf_op jit(solution)/shard_map/gram/pallas_call | solution.py:111
  70.0 0.0 collective-permute-done.13.refs_1_
  70.0 0.0 collective-permute-done.8.refs_0_
  70.0 3.9 %gram.9 = f32[8,136,128]{2,1,0:T(8,128)S(1)} custom-call(s32[1]{0:T(128)} %bitcast.me_ref, bf16[16,16,512]{2,1,0:T(8,128)(2,1)S(1)} %all-to-all-done.code_ref, bf16[2,8,128,128]{3,2,1,0:T(8,128)(2,1)S(1)} %collective-permute-done.8.refs_0_, bf16[2,8,128,128]{3,2,1,0:T(8,128)(2,1)S(1)} %collective-permute-done.13.refs_1_, ...), custom_call_target="tpu_custom_call" | custom-call | flops 2415919104 | bytes 32768 | tf_op jit(solution)/shard_map/gram/pallas_call | solution.py:111
  73.9 9.9 %collective-permute-start.16 = (f32[8,136,128]{2,1,0:T(8,128)S(1)}, f32[8,136,128]{2,1,0:T(8,128)S(1)}, u32[]{:S(2)}, u32[]{:S(2)}) collective-permute-start(f32[8,136,128]{2,1,0:T(8,128)S(1)} %gram.9), channel_id=1, source_target_pairs={{0,8},{8,0},{16,24},{24,16},{32,40},{40,32},{48,56},{56,48},{64,72... | collective-permute-start | bytes 1671176 | tf_op jit(solution)/shard_map/ppermute | solution.py:286
  83.8 3.9 %gram.8.own_ref = f32[8,136,128]{2,1,0:T(8,128)S(1)} custom-call(s32[1]{0:T(128)} %bitcast.me_ref, bf16[16,16,512]{2,1,0:T(8,128)(2,1)S(1)} %all-to-all-done.code_ref, bf16[2,8,128,128]{3,2,1,0:T(8,128)(2,1)S(1)} %collective-permute-done.8.refs_0_, bf16[2,8,128,128]{3,2,1,0:T(8,128)(2,1)S(1)} %collective-permute-done.13.refs_1_, ...), custom_call_target="tpu_custom_call" | custom-call | flops 2415919104 | bytes 32768 | tf_op jit(solution)/shard_map/gram/pallas_call | solution.py:111
  87.6 0.0 collective-permute-done.16.other_ref
  87.7 7.0 %solve.1 = f32[8,128]{1,0:T(8,128)} custom-call(f32[8,136,128]{2,1,0:T(8,128)S(1)} %gram.8.own_ref, f32[8,136,128]{2,1,0:T(8,128)S(1)} %collective-permute-done.16.other_ref), custom_call_target="tpu_custom_call" | custom-call | tf_op jit(solution)/shard_map/solve/pallas_call | solution.py:206
  (13 shorter events, 0.2 us)
Async XLA Ops:
  0.9 7.8 %collective-permute-start = (bf16[128,128]{1,0:T(8,128)(2,1)S(1)}, bf16[128,128]{1,0:T(8,128)(2,1)S(1)}, u32[]{:S(2)}, u32[]{:S(2)}) collective-permute-start(bf16[128,128]{1,0:T(8,128)(2,1)S(1)} %bitcast.25), channel_id=1, source_target_pairs={{0,1},{1,2},{2,3},{3,4},{4,5},{5,6},{6,7},{7,0},{8,9},{9,10},{10,1... | collective-permute-start | bytes 98312 | tf_op jit(solution)/shard_map/ppermute | solution.py:229
  3.4 5.2 %collective-permute-start.1 = (bf16[128,128]{1,0:T(8,128)(2,1)S(1)}, bf16[128,128]{1,0:T(8,128)(2,1)S(1)}, u32[]{:S(2)}, u32[]{:S(2)}) collective-permute-start(bf16[128,128]{1,0:T(8,128)(2,1)S(1)} %bitcast.26), channel_id=1, source_target_pairs={{0,7},{1,0},{2,1},{3,2},{4,3},{5,4},{6,5},{7,6},{8,15},{9,8},{10,9... | collective-permute-start | bytes 98312 | tf_op jit(solution)/shard_map/ppermute | solution.py:229
  8.7 6.7 %collective-permute-start.2 = (bf16[3,128,128]{2,1,0:T(8,128)(2,1)S(1)}, bf16[3,128,128]{2,1,0:T(8,128)(2,1)S(1)}, u32[]{:S(2)}, u32[]{:S(2)}) collective-permute-start(bf16[3,128,128]{2,1,0:T(8,128)(2,1)S(1)} %pad_maximum_fusion.4), channel_id=1, source_target_pairs={{0,3},{1,4},{2,5},{3,6},{4,7},{5,0},{6,1},{7,2},{8,11},{9,12},{10,... | collective-permute-start | bytes 294920 | tf_op jit(solution)/shard_map/ppermute | solution.py:229
  13.0 8.2 %copy-start = (s32[256,256]{1,0:T(8,128)S(1)}, s32[256,256]{1,0:T(8,128)}, u32[]{:S(2)}) copy-start(s32[256,256]{1,0:T(8,128)} %param.5) | copy-start | bytes 786436
  13.0 5.3 %collective-permute-start.3 = (bf16[2,128,128]{2,1,0:T(8,128)(2,1)S(1)}, bf16[2,128,128]{2,1,0:T(8,128)(2,1)S(1)}, u32[]{:S(2)}, u32[]{:S(2)}) collective-permute-start(bf16[2,128,128]{2,1,0:T(8,128)(2,1)S(1)} %pad_maximum_fusion.5), channel_id=1, source_target_pairs={{0,5},{1,6},{2,7},{3,0},{4,1},{5,2},{6,3},{7,4},{8,13},{9,14},{10,... | collective-permute-start | bytes 196616 | tf_op jit(solution)/shard_map/ppermute | solution.py:229
  18.3 2.9 %copy-start.2 = (s32[256,1]{0,1:T(1,128)S(1)}, s32[256,1]{0,1:T(1,128)}, u32[]{:S(2)}) copy-start(s32[256,1]{0,1:T(1,128)} %param.7) | copy-start | bytes 3076
  18.4 6.6 %collective-permute-start.5 = (bf16[8,128,128]{2,1,0:T(8,128)(2,1)S(1)}, bf16[8,128,128]{2,1,0:T(8,128)(2,1)S(1)}, u32[]{:S(2)}, u32[]{:S(2)}) collective-permute-start(bf16[8,128,128]{2,1,0:T(8,128)(2,1)S(1)} %constant_dynamic-update-slice_fusion), channel_id=1, source_target_pairs={{0,16},{8,72},{16,32},{24,88},{32,48},{40,104},{48,0},{56,120},{64... | collective-permute-start | bytes 786440 | tf_op jit(solution)/shard_map/ppermute | solution.py:240
  19.7 5.2 %collective-permute-start.6 = (bf16[8,128,128]{2,1,0:T(8,128)(2,1)S(1)}, bf16[8,128,128]{2,1,0:T(8,128)(2,1)S(1)}, u32[]{:S(2)}, u32[]{:S(2)}) collective-permute-start(bf16[8,128,128]{2,1,0:T(8,128)(2,1)S(1)} %constant_dynamic-update-slice_fusion), channel_id=1, source_target_pairs={{0,48},{8,200},{16,0},{24,216},{32,16},{40,232},{48,32},{56,248},{... | collective-permute-start | bytes 786440 | tf_op jit(solution)/shard_map/ppermute | solution.py:240
  21.3 0.9 copy-start.1
  25.0 19.7 %collective-permute-start.9 = (bf16[2,8,128,128]{3,2,1,0:T(8,128)(2,1)S(1)}, bf16[2,8,128,128]{3,2,1,0:T(8,128)(2,1)S(1)}, u32[]{:S(2)}, u32[]{:S(2)}) collective-permute-start(bf16[2,8,128,128]{3,2,1,0:T(8,128)(2,1)S(1)} %pad_maximum_fusion.refs_0_), channel_id=1, source_target_pairs={{0,192},{8,56},{16,208},{24,8},{32,224},{40,24},{48,240},{56,40},{... | collective-permute-start | bytes 1572872 | tf_op jit(solution)/shard_map/ppermute | solution.py:240
  28.3 11.9 %all-to-all-start = ((bf16[16,16,512]{2,1,0:T(8,128)(2,1)}), bf16[16,16,512]{2,1,0:T(8,128)(2,1)S(1)}, u32[]{:S(2)}, u32[]{:S(2)}) async-start(bf16[16,16,512]{2,1,0:T(8,128)(2,1)} %fusion), calls=%async_computation | async-start | bytes 524288 | tf_op jit(solution)/shard_map/all_to_all | solution.py:262
  32.7 9.1 %collective-permute-start.10 = (bf16[4,128,128]{2,1,0:T(8,128)(2,1)S(1)}, bf16[4,128,128]{2,1,0:T(8,128)(2,1)S(1)}, u32[]{:S(2)}, u32[]{:S(2)}) collective-permute-start(bf16[4,128,128]{2,1,0:T(8,128)(2,1)S(1)} %slice.20), channel_id=1, source_target_pairs={{0,16},{8,72},{16,32},{24,88},{32,48},{40,104},{48,0},{56,120},{64... | collective-permute-start | bytes 393224 | tf_op jit(solution)/shard_map/ppermute | solution.py:240
  34.2 8.6 %collective-permute-start.11 = (bf16[4,128,128]{2,1,0:T(8,128)(2,1)S(1)}, bf16[4,128,128]{2,1,0:T(8,128)(2,1)S(1)}, u32[]{:S(2)}, u32[]{:S(2)}) collective-permute-start(bf16[4,128,128]{2,1,0:T(8,128)(2,1)S(1)} %slice.21), channel_id=1, source_target_pairs={{0,48},{8,200},{16,0},{24,216},{32,16},{40,232},{48,32},{56,248},{... | collective-permute-start | bytes 393224 | tf_op jit(solution)/shard_map/ppermute | solution.py:240
  35.6 18.0 %collective-permute-start.4 = (bf16[1,8,128,128]{3,2,1,0:T(8,128)(2,1)S(1)}, bf16[1,8,128,128]{3,2,1,0:T(8,128)(2,1)S(1)}, u32[]{:S(2)}, u32[]{:S(2)}) collective-permute-start(bf16[1,8,128,128]{3,2,1,0:T(8,128)(2,1)S(1)} %bitcast.19), channel_id=1, source_target_pairs={{0,64},{8,24},{16,80},{24,40},{32,96},{40,56},{48,112},{56,8},{64,... | collective-permute-start | bytes 786440 | tf_op jit(solution)/shard_map/ppermute | solution.py:240
  37.0 16.8 %collective-permute-start.15 = (bf16[1,8,128,128]{3,2,1,0:T(8,128)(2,1)S(1)}, bf16[1,8,128,128]{3,2,1,0:T(8,128)(2,1)S(1)}, u32[]{:S(2)}, u32[]{:S(2)}) collective-permute-start(bf16[1,8,128,128]{3,2,1,0:T(8,128)(2,1)S(1)} %bitcast.20), channel_id=1, source_target_pairs={{0,192},{8,56},{16,208},{24,8},{32,224},{40,24},{48,240},{56,40},{... | collective-permute-start | bytes 786440 | tf_op jit(solution)/shard_map/ppermute | solution.py:240
  41.9 11.6 %collective-permute-start.7 = (bf16[2,8,128,128]{3,2,1,0:T(8,128)(2,1)S(1)}, bf16[2,8,128,128]{3,2,1,0:T(8,128)(2,1)S(1)}, u32[]{:S(2)}, u32[]{:S(2)}) collective-permute-start(bf16[2,8,128,128]{3,2,1,0:T(8,128)(2,1)S(1)} %pad_maximum_fusion.refs_0_), channel_id=1, source_target_pairs={{0,64},{8,24},{16,80},{24,40},{32,96},{40,56},{48,112},{56,8},{64,... | collective-permute-start | bytes 1572872 | tf_op jit(solution)/shard_map/ppermute | solution.py:240
  42.8 7.1 %collective-permute-start.12 = (bf16[1,8,128,128]{3,2,1,0:T(8,128)(2,1)S(1)}, bf16[1,8,128,128]{3,2,1,0:T(8,128)(2,1)S(1)}, u32[]{:S(2)}, u32[]{:S(2)}) collective-permute-start(bf16[1,8,128,128]{3,2,1,0:T(8,128)(2,1)S(1)} %maximum_bitcast_fusion.refs_1_), channel_id=1, source_target_pairs={{0,192},{8,56},{16,208},{24,8},{32,224},{40,24},{48,240},{56,40},{... | collective-permute-start | bytes 786440 | tf_op jit(solution)/shard_map/ppermute | solution.py:240
  44.8 11.6 %collective-permute-start.14 = (bf16[1,8,128,128]{3,2,1,0:T(8,128)(2,1)S(1)}, bf16[1,8,128,128]{3,2,1,0:T(8,128)(2,1)S(1)}, u32[]{:S(2)}, u32[]{:S(2)}) collective-permute-start(bf16[1,8,128,128]{3,2,1,0:T(8,128)(2,1)S(1)} %maximum_bitcast_fusion.refs_1_), channel_id=1, source_target_pairs={{0,64},{8,24},{16,80},{24,40},{32,96},{40,56},{48,112},{56,8},{64,... | collective-permute-start | bytes 786440 | tf_op jit(solution)/shard_map/ppermute | solution.py:240
  49.9 20.0 %collective-permute-start.13 = (bf16[2,8,128,128]{3,2,1,0:T(8,128)(2,1)S(1)}, bf16[2,8,128,128]{3,2,1,0:T(8,128)(2,1)S(1)}, u32[]{:S(2)}, u32[]{:S(2)}) collective-permute-start(bf16[2,8,128,128]{3,2,1,0:T(8,128)(2,1)S(1)} %pad_maximum_fusion.2), channel_id=1, source_target_pairs={{0,192},{8,56},{16,208},{24,8},{32,224},{40,24},{48,240},{56,40},{... | collective-permute-start | bytes 1572872 | tf_op jit(solution)/shard_map/ppermute | solution.py:240
  53.6 16.4 %collective-permute-start.8 = (bf16[2,8,128,128]{3,2,1,0:T(8,128)(2,1)S(1)}, bf16[2,8,128,128]{3,2,1,0:T(8,128)(2,1)S(1)}, u32[]{:S(2)}, u32[]{:S(2)}) collective-permute-start(bf16[2,8,128,128]{3,2,1,0:T(8,128)(2,1)S(1)} %pad_maximum_fusion.1), channel_id=1, source_target_pairs={{0,64},{8,24},{16,80},{24,40},{32,96},{40,56},{48,112},{56,8},{64,... | collective-permute-start | bytes 1572872 | tf_op jit(solution)/shard_map/ppermute | solution.py:240
  73.9 13.8 %collective-permute-start.16 = (f32[8,136,128]{2,1,0:T(8,128)S(1)}, f32[8,136,128]{2,1,0:T(8,128)S(1)}, u32[]{:S(2)}, u32[]{:S(2)}) collective-permute-start(f32[8,136,128]{2,1,0:T(8,128)S(1)} %gram.9), channel_id=1, source_target_pairs={{0,8},{8,0},{16,24},{24,16},{32,40},{40,32},{48,56},{56,48},{64,72... | collective-permute-start | bytes 1671176 | tf_op jit(solution)/shard_map/ppermute | solution.py:286

commit v7 on v5

--- a/solution.py
+++ b/solution.py
@@ -213,9 +213,9 @@
 
 
 def coded(item_index, counts, begin, items):
-    item_index = (item_index + (items - begin)) % items
-    low = item_index % LOW
-    value = jnp.where(low < HALF, low + HALF, -low) * (1 << (item_index // LOW))
+    item_index = (item_index + (items - begin)) & (items - 1)
+    low = item_index & (LOW - 1)
+    value = jnp.where(low < HALF, low + HALF, -low) << (item_index >> 8)
     position = lax.broadcasted_iota(jnp.int32, item_index.shape, 1)
     return jnp.where(position < counts, value, 0).astype(BF16)
 
@@ -272,9 +272,8 @@
     three = jnp.stack([block, behind, ahead])
     three_behind, three_ahead = near_of(three, False)
     far = jnp.concatenate(far_of(behind[:half], ahead[half:], True))[None]
-    own, other = gram(who, 0, code, [three], both)
     far_behind, far_ahead = near_of(far, False)
-    own, other = gram(who, 3, code, [far], both, (own, other))
+    own, other = gram(who, 0, code, [three, far], both)
     low, high = far_of(three_behind[:2], jnp.concatenate([three_ahead[2:], far_ahead]), False)
     tables = [three_behind, far_behind, three_ahead, far_ahead]
     own, other = gram(who, 4, code, tables, both, (own, other))

time: 90.4 us -> 90.4 us (level)
    pallas_call x5 -> x4, Pallas kernels: 28 us -> 28.1 us  [gram(): pl.pallas_call(functools.partial(gram_kernel, counts=counts, groups=group...]
  transfers between devices with their start and end apart: 16 -> 16, of which waited for: 5 -> 5; matrix products, arithmetic and copies ran while one was open for 2% -> 1% of each run, Pallas kernels for 27% -> 27%
where the time goes in v7:
time: 90.4 us; the launch traced here: 90.2 us
  starting transfers between devices  38.2 us (42%)
  Pallas kernels  35.1 us (39%)
  waiting for transfers between devices  13.8 us (15%)
  local copies, waits for them, and re-layouts  1.78 us (2%)
  other arithmetic  1.07 us (1%)
    pallas_call x4, Pallas kernels, gram(): pl.pallas_call(functools.partial(gram_kernel, counts=counts, groups=group...  28.1 us
    ppermute x10, starting transfers between devices, shifted(): return lax.ppermute(value, 'row', pairs)  15.6 us
    ppermute x4, starting transfers between devices, along_col(): lax.ppermute(value, 'col', [(i, (i + by) % size) for i in range(size)])  11.2 us
    ppermute x1, starting transfers between devices, half_sweep(): other = lax.ppermute(other, 'row', [(i, i ^ 1) for i in range(n_row)])  7.07 us
    pallas_call x1, Pallas kernels, solve(): pl.pallas_call(solve_kernel, out_shape=jax.ShapeDtypeStruct((users, rank)...  7.05 us
    ppermute x4, waiting for transfers between devices, along_col(): lax.ppermute(value, 'col', [(i, (i + by) % size) for i in range(size)])  6.18 us
    all_to_all x1, waiting for transfers between devices, half_sweep(): lax.all_to_all(code, 'row', 0, 0, tiled=True, axis_index_groups=same_core)  4.88 us
    all_to_all x1, starting transfers between devices, half_sweep(): lax.all_to_all(code, 'row', 0, 0, tiled=True, axis_index_groups=same_core)  4.3 us
  transfers between devices with their start and end apart: 16, of which 5 were waited for; matrix products, arithmetic and copies ran while one was open for 1% of the time, Pallas kernels for 27%

profile of v7, /device:TPU:1, one launch (start us, length us, event | category | flops | bytes accessed | tf_op | source)
XLA Modules:
  0.0 90.2 jit_solution(10195406538071549276)
XLA Ops:
  0.0 0.9 copy.5
  0.9 2.5 %collective-permute-start = (bf16[128,128]{1,0:T(8,128)(2,1)S(1)}, bf16[128,128]{1,0:T(8,128)(2,1)S(1)}, u32[]{:S(2)}, u32[]{:S(2)}) collective-permute-start(bf16[128,128]{1,0:T(8,128)(2,1)S(1)} %bitcast.22), channel_id=1, source_target_pairs={{0,1},{1,2},{2,3},{3,4},{4,5},{5,6},{6,7},{7,0},{8,9},{9,10},{10,1... | collective-permute-start | bytes 98312 | tf_op jit(solution)/shard_map/ppermute | solution.py:229
  3.4 4.0 %collective-permute-start.1 = (bf16[128,128]{1,0:T(8,128)(2,1)S(1)}, bf16[128,128]{1,0:T(8,128)(2,1)S(1)}, u32[]{:S(2)}, u32[]{:S(2)}) collective-permute-start(bf16[128,128]{1,0:T(8,128)(2,1)S(1)} %bitcast.23), channel_id=1, source_target_pairs={{0,7},{1,0},{2,1},{3,2},{4,3},{5,4},{6,5},{7,6},{8,15},{9,8},{10,9... | collective-permute-start | bytes 98312 | tf_op jit(solution)/shard_map/ppermute | solution.py:229
  7.4 1.2 %collective-permute-done = bf16[128,128]{1,0:T(8,128)(2,1)S(1)} collective-permute-done((bf16[128,128]{1,0:T(8,128)(2,1)S(1)}, bf16[128,128]{1,0:T(8,128)(2,1)S(1)}, u32[]{:S(2)}, u32[]{:S(2)}) %collective-permute-start) | collective-permute-done | bytes 32800 | tf_op jit(solution)/shard_map/ppermute | solution.py:229
  8.6 0.0 collective-permute-done.1
  8.7 4.4 %collective-permute-start.2 = (bf16[3,128,128]{2,1,0:T(8,128)(2,1)S(1)}, bf16[3,128,128]{2,1,0:T(8,128)(2,1)S(1)}, u32[]{:S(2)}, u32[]{:S(2)}) collective-permute-start(bf16[3,128,128]{2,1,0:T(8,128)(2,1)S(1)} %pad_maximum_fusion.3), channel_id=1, source_target_pairs={{0,3},{1,4},{2,5},{3,6},{4,7},{5,0},{6,1},{7,2},{8,11},{9,12},{10,... | collective-permute-start | bytes 294920 | tf_op jit(solution)/shard_map/ppermute | solution.py:229
  13.0 0.0 copy-start
  13.0 0.3 collective-permute-start.3
  13.3 2.1 %collective-permute-done.2 = bf16[3,128,128]{2,1,0:T(8,128)(2,1)S(1)} collective-permute-done((bf16[3,128,128]{2,1,0:T(8,128)(2,1)S(1)}, bf16[3,128,128]{2,1,0:T(8,128)(2,1)S(1)}, u32[]{:S(2)}, u32[]{:S(2)}) %collective-permute-start.2) | collective-permute-done | bytes 98336 | tf_op jit(solution)/shard_map/ppermute | solution.py:229
  15.4 2.9 %collective-permute-done.3 = bf16[2,128,128]{2,1,0:T(8,128)(2,1)S(1)} collective-permute-done((bf16[2,128,128]{2,1,0:T(8,128)(2,1)S(1)}, bf16[2,128,128]{2,1,0:T(8,128)(2,1)S(1)}, u32[]{:S(2)}, u32[]{:S(2)}) %collective-permute-start.3) | collective-permute-done | bytes 65568 | tf_op jit(solution)/shard_map/ppermute | solution.py:229
  18.3 0.0 copy-start.2
  18.4 1.4 %collective-permute-start.4 = (bf16[8,128,128]{2,1,0:T(8,128)(2,1)S(1)}, bf16[8,128,128]{2,1,0:T(8,128)(2,1)S(1)}, u32[]{:S(2)}, u32[]{:S(2)}) collective-permute-start(bf16[8,128,128]{2,1,0:T(8,128)(2,1)S(1)} %constant_dynamic-update-slice_fusion), channel_id=1, source_target_pairs={{0,16},{8,72},{16,32},{24,88},{32,48},{40,104},{48,0},{56,120},{64... | collective-permute-start | bytes 786440 | tf_op jit(solution)/shard_map/ppermute | solution.py:240
  19.7 1.5 %collective-permute-start.5 = (bf16[8,128,128]{2,1,0:T(8,128)(2,1)S(1)}, bf16[8,128,128]{2,1,0:T(8,128)(2,1)S(1)}, u32[]{:S(2)}, u32[]{:S(2)}) collective-permute-start(bf16[8,128,128]{2,1,0:T(8,128)(2,1)S(1)} %constant_dynamic-update-slice_fusion), channel_id=1, source_target_pairs={{0,48},{8,200},{16,0},{24,216},{32,16},{40,232},{48,32},{56,248},{... | collective-permute-start | bytes 786440 | tf_op jit(solution)/shard_map/ppermute | solution.py:240
  21.3 0.0 copy-done
  21.3 0.0 copy-done.2
  21.3 0.0 copy-start.1
  21.3 0.1 select_convert_fusion
  21.4 0.8 copy-done.1
  22.2 2.8 %collective-permute-done.5 = bf16[8,128,128]{2,1,0:T(8,128)(2,1)S(1)} collective-permute-done((bf16[8,128,128]{2,1,0:T(8,128)(2,1)S(1)}, bf16[8,128,128]{2,1,0:T(8,128)(2,1)S(1)}, u32[]{:S(2)}, u32[]{:S(2)}) %collective-permute-start.5) | collective-permute-done | bytes 262176 | tf_op jit(solution)/shard_map/ppermute | solution.py:240
  25.0 2.8 %collective-permute-start.10 = (bf16[4,128,128]{2,1,0:T(8,128)(2,1)S(1)}, bf16[4,128,128]{2,1,0:T(8,128)(2,1)S(1)}, u32[]{:S(2)}, u32[]{:S(2)}) collective-permute-start(bf16[4,128,128]{2,1,0:T(8,128)(2,1)S(1)} %slice.21), channel_id=1, source_target_pairs={{0,48},{8,200},{16,0},{24,216},{32,16},{40,232},{48,32},{56,248},{... | collective-permute-start | bytes 393224 | tf_op jit(solution)/shard_map/ppermute | solution.py:240
  27.8 0.0 collective-permute-done.4
  27.8 0.1 collective-permute-start.9
  27.9 0.1 pad_maximum_fusion.refs_0_
  28.0 2.6 %collective-permute-start.8 = (bf16[3,8,128,128]{3,2,1,0:T(8,128)(2,1)S(1)}, bf16[3,8,128,128]{3,2,1,0:T(8,128)(2,1)S(1)}, u32[]{:S(2)}, u32[]{:S(2)}) collective-permute-start(bf16[3,8,128,128]{3,2,1,0:T(8,128)(2,1)S(1)} %pad_maximum_fusion.refs_0_), channel_id=1, source_target_pairs={{0,192},{8,56},{16,208},{24,8},{32,224},{40,24},{48,240},{56,40},{... | collective-permute-start | bytes 2359304 | tf_op jit(solution)/shard_map/ppermute | solution.py:240
  30.5 0.8 fusion
  31.3 4.3 %all-to-all-start = ((bf16[16,16,512]{2,1,0:T(8,128)(2,1)}), bf16[16,16,512]{2,1,0:T(8,128)(2,1)S(1)}, u32[]{:S(2)}, u32[]{:S(2)}) async-start(bf16[16,16,512]{2,1,0:T(8,128)(2,1)} %fusion), calls=%async_computation | async-start | bytes 524288 | tf_op jit(solution)/shard_map/all_to_all | solution.py:262
  35.6 1.4 %collective-permute-start.6 = (bf16[3,8,128,128]{3,2,1,0:T(8,128)(2,1)S(1)}, bf16[3,8,128,128]{3,2,1,0:T(8,128)(2,1)S(1)}, u32[]{:S(2)}, u32[]{:S(2)}) collective-permute-start(bf16[3,8,128,128]{3,2,1,0:T(8,128)(2,1)S(1)} %pad_maximum_fusion.refs_0_), channel_id=1, source_target_pairs={{0,64},{8,24},{16,80},{24,40},{32,96},{40,56},{48,112},{56,8},{64,... | collective-permute-start | bytes 2359304 | tf_op jit(solution)/shard_map/ppermute | solution.py:240
  37.0 0.0 collective-permute-done.10
  37.0 0.0 collective-permute-done.9
  37.0 1.5 %collective-permute-start.11 = (bf16[1,8,128,128]{3,2,1,0:T(8,128)(2,1)S(1)}, bf16[1,8,128,128]{3,2,1,0:T(8,128)(2,1)S(1)}, u32[]{:S(2)}, u32[]{:S(2)}) collective-permute-start(bf16[1,8,128,128]{3,2,1,0:T(8,128)(2,1)S(1)} %maximum_bitcast_fusion.refs_1_), channel_id=1, source_target_pairs={{0,192},{8,56},{16,208},{24,8},{32,224},{40,24},{48,240},{56,40},{... | collective-permute-start | bytes 786440 | tf_op jit(solution)/shard_map/ppermute | solution.py:240
  38.5 0.1 collective-permute-start.13
  38.6 4.9 %all-to-all-done.code_ref = bf16[16,16,512]{2,1,0:T(8,128)(2,1)S(1)} async-done(((bf16[16,16,512]{2,1,0:T(8,128)(2,1)}), bf16[16,16,512]{2,1,0:T(8,128)(2,1)S(1)}, u32[]{:S(2)}, u32[]{:S(2)}) %all-to-all-start) | async-done | bytes 262176 | tf_op jit(solution)/shard_map/all_to_all | solution.py:262
  43.4 6.8 %gram.4 = (f32[8,136,128]{2,1,0:T(8,128)S(1)}, f32[8,136,128]{2,1,0:T(8,128)S(1)}) custom-call(s32[1]{0:T(128)} %bitcast.me_ref, bf16[16,16,512]{2,1,0:T(8,128)(2,1)S(1)} %all-to-all-done.code_ref, bf16[3,8,128,128]{3,2,1,0:T(8,128)(2,1)S(1)} %pad_maximum_fusion.refs_0_, bf16[1,8,128,128]{3,2,1,0:T(8,128)(2,1)S(1)} %maximum_bitcast_fusion.refs_1_), custom_call_target="tpu_custom_call" | custom-call | flops 4831838208 | bytes 65536 | tf_op jit(solution)/shard_map/gram/pallas_call | solution.py:111
  50.2 0.0 collective-permute-done.8.refs_2_
  50.2 0.0 collective-permute-done.11.refs_3_
  50.2 0.1 pad_maximum_fusion.1
  50.3 4.2 %collective-permute-start.12 = (bf16[2,8,128,128]{3,2,1,0:T(8,128)(2,1)S(1)}, bf16[2,8,128,128]{3,2,1,0:T(8,128)(2,1)S(1)}, u32[]{:S(2)}, u32[]{:S(2)}) collective-permute-start(bf16[2,8,128,128]{3,2,1,0:T(8,128)(2,1)S(1)} %pad_maximum_fusion.1), channel_id=1, source_target_pairs={{0,192},{8,56},{16,208},{24,8},{32,224},{40,24},{48,240},{56,40},{... | collective-permute-start | bytes 1572872 | tf_op jit(solution)/shard_map/ppermute | solution.py:240
  54.5 0.0 collective-permute-done.6.refs_0_
  54.6 0.1 collective-permute-start.7
  54.7 0.0 collective-permute-done.13.refs_1_
  54.7 13.6 %gram.5 = (f32[8,136,128]{2,1,0:T(8,128)S(1)}, f32[8,136,128]{2,1,0:T(8,128)S(1)}) custom-call(s32[1]{0:T(128)} %bitcast.me_ref, bf16[16,16,512]{2,1,0:T(8,128)(2,1)S(1)} %all-to-all-done.code_ref, bf16[3,8,128,128]{3,2,1,0:T(8,128)(2,1)S(1)} %collective-permute-done.6.refs_0_, bf16[1,8,128,128]{3,2,1,0:T(8,128)(2,1)S(1)} %collective-permute-done.13.refs_1_, ...), custom_call_target="tpu_custom_call" | custom-call | flops 9663676416 | bytes 131072 | tf_op jit(solution)/shard_map/gram/pallas_call | solution.py:111
  68.3 0.0 collective-permute-done.12.refs_1_
  68.3 0.0 collective-permute-done.7.refs_0_
  68.3 3.9 %gram.7 = f32[8,136,128]{2,1,0:T(8,128)S(1)} custom-call(s32[1]{0:T(128)} %bitcast.me_ref, bf16[16,16,512]{2,1,0:T(8,128)(2,1)S(1)} %all-to-all-done.code_ref, bf16[2,8,128,128]{3,2,1,0:T(8,128)(2,1)S(1)} %collective-permute-done.7.refs_0_, bf16[2,8,128,128]{3,2,1,0:T(8,128)(2,1)S(1)} %collective-permute-done.12.refs_1_, ...), custom_call_target="tpu_custom_call" | custom-call | flops 2415919104 | bytes 32768 | tf_op jit(solution)/shard_map/gram/pallas_call | solution.py:111
  72.2 7.1 %collective-permute-start.14 = (f32[8,136,128]{2,1,0:T(8,128)S(1)}, f32[8,136,128]{2,1,0:T(8,128)S(1)}, u32[]{:S(2)}, u32[]{:S(2)}) collective-permute-start(f32[8,136,128]{2,1,0:T(8,128)S(1)} %gram.7), channel_id=1, source_target_pairs={{0,8},{8,0},{16,24},{24,16},{32,40},{40,32},{48,56},{56,48},{64,72... | collective-permute-start | bytes 1671176 | tf_op jit(solution)/shard_map/ppermute | solution.py:281
  79.3 3.9 %gram.6.own_ref = f32[8,136,128]{2,1,0:T(8,128)S(1)} custom-call(s32[1]{0:T(128)} %bitcast.me_ref, bf16[16,16,512]{2,1,0:T(8,128)(2,1)S(1)} %all-to-all-done.code_ref, bf16[2,8,128,128]{3,2,1,0:T(8,128)(2,1)S(1)} %collective-permute-done.7.refs_0_, bf16[2,8,128,128]{3,2,1,0:T(8,128)(2,1)S(1)} %collective-permute-done.12.refs_1_, ...), custom_call_target="tpu_custom_call" | custom-call | flops 2415919104 | bytes 32768 | tf_op jit(solution)/shard_map/gram/pallas_call | solution.py:111
  83.1 0.0 collective-permute-done.14.other_ref
  83.1 7.0 %solve.1 = f32[8,128]{1,0:T(8,128)} custom-call(f32[8,136,128]{2,1,0:T(8,128)S(1)} %gram.6.own_ref, f32[8,136,128]{2,1,0:T(8,128)S(1)} %collective-permute-done.14.other_ref), custom_call_target="tpu_custom_call" | custom-call | tf_op jit(solution)/shard_map/solve/pallas_call | solution.py:206
  (13 shorter events, 0.2 us)
Async XLA Ops:
  0.9 7.8 %collective-permute-start = (bf16[128,128]{1,0:T(8,128)(2,1)S(1)}, bf16[128,128]{1,0:T(8,128)(2,1)S(1)}, u32[]{:S(2)}, u32[]{:S(2)}) collective-permute-start(bf16[128,128]{1,0:T(8,128)(2,1)S(1)} %bitcast.22), channel_id=1, source_target_pairs={{0,1},{1,2},{2,3},{3,4},{4,5},{5,6},{6,7},{7,0},{8,9},{9,10},{10,1... | collective-permute-start | bytes 98312 | tf_op jit(solution)/shard_map/ppermute | solution.py:229
  3.4 5.2 %collective-permute-start.1 = (bf16[128,128]{1,0:T(8,128)(2,1)S(1)}, bf16[128,128]{1,0:T(8,128)(2,1)S(1)}, u32[]{:S(2)}, u32[]{:S(2)}) collective-permute-start(bf16[128,128]{1,0:T(8,128)(2,1)S(1)} %bitcast.23), channel_id=1, source_target_pairs={{0,7},{1,0},{2,1},{3,2},{4,3},{5,4},{6,5},{7,6},{8,15},{9,8},{10,9... | collective-permute-start | bytes 98312 | tf_op jit(solution)/shard_map/ppermute | solution.py:229
  8.7 6.7 %collective-permute-start.2 = (bf16[3,128,128]{2,1,0:T(8,128)(2,1)S(1)}, bf16[3,128,128]{2,1,0:T(8,128)(2,1)S(1)}, u32[]{:S(2)}, u32[]{:S(2)}) collective-permute-start(bf16[3,128,128]{2,1,0:T(8,128)(2,1)S(1)} %pad_maximum_fusion.3), channel_id=1, source_target_pairs={{0,3},{1,4},{2,5},{3,6},{4,7},{5,0},{6,1},{7,2},{8,11},{9,12},{10,... | collective-permute-start | bytes 294920 | tf_op jit(solution)/shard_map/ppermute | solution.py:229
  13.0 8.2 %copy-start = (s32[256,256]{1,0:T(8,128)S(1)}, s32[256,256]{1,0:T(8,128)}, u32[]{:S(2)}) copy-start(s32[256,256]{1,0:T(8,128)} %param.5) | copy-start | bytes 786436
  13.0 5.3 %collective-permute-start.3 = (bf16[2,128,128]{2,1,0:T(8,128)(2,1)S(1)}, bf16[2,128,128]{2,1,0:T(8,128)(2,1)S(1)}, u32[]{:S(2)}, u32[]{:S(2)}) collective-permute-start(bf16[2,128,128]{2,1,0:T(8,128)(2,1)S(1)} %pad_maximum_fusion.4), channel_id=1, source_target_pairs={{0,5},{1,6},{2,7},{3,0},{4,1},{5,2},{6,3},{7,4},{8,13},{9,14},{10,... | collective-permute-start | bytes 196616 | tf_op jit(solution)/shard_map/ppermute | solution.py:229
  18.3 2.9 %copy-start.2 = (s32[256,1]{0,1:T(1,128)S(1)}, s32[256,1]{0,1:T(1,128)}, u32[]{:S(2)}) copy-start(s32[256,1]{0,1:T(1,128)} %param.7) | copy-start | bytes 3076
  18.4 9.4 %collective-permute-start.4 = (bf16[8,128,128]{2,1,0:T(8,128)(2,1)S(1)}, bf16[8,128,128]{2,1,0:T(8,128)(2,1)S(1)}, u32[]{:S(2)}, u32[]{:S(2)}) collective-permute-start(bf16[8,128,128]{2,1,0:T(8,128)(2,1)S(1)} %constant_dynamic-update-slice_fusion), channel_id=1, source_target_pairs={{0,16},{8,72},{16,32},{24,88},{32,48},{40,104},{48,0},{56,120},{64... | collective-permute-start | bytes 786440 | tf_op jit(solution)/shard_map/ppermute | solution.py:240
  19.7 5.2 %collective-permute-start.5 = (bf16[8,128,128]{2,1,0:T(8,128)(2,1)S(1)}, bf16[8,128,128]{2,1,0:T(8,128)(2,1)S(1)}, u32[]{:S(2)}, u32[]{:S(2)}) collective-permute-start(bf16[8,128,128]{2,1,0:T(8,128)(2,1)S(1)} %constant_dynamic-update-slice_fusion), channel_id=1, source_target_pairs={{0,48},{8,200},{16,0},{24,216},{32,16},{40,232},{48,32},{56,248},{... | collective-permute-start | bytes 786440 | tf_op jit(solution)/shard_map/ppermute | solution.py:240
  21.3 0.9 %copy-start.1 = (bf16[256,256]{1,0:T(8,128)(2,1)S(1)}, bf16[256,256]{1,0:T(8,128)(2,1)}, u32[]{:S(2)}) copy-start(bf16[256,256]{1,0:T(8,128)(2,1)} %param.6) | copy-start | bytes 393220
  25.0 12.0 %collective-permute-start.10 = (bf16[4,128,128]{2,1,0:T(8,128)(2,1)S(1)}, bf16[4,128,128]{2,1,0:T(8,128)(2,1)S(1)}, u32[]{:S(2)}, u32[]{:S(2)}) collective-permute-start(bf16[4,128,128]{2,1,0:T(8,128)(2,1)S(1)} %slice.21), channel_id=1, source_target_pairs={{0,48},{8,200},{16,0},{24,216},{32,16},{40,232},{48,32},{56,248},{... | collective-permute-start | bytes 393224 | tf_op jit(solution)/shard_map/ppermute | solution.py:240
  27.8 9.2 %collective-permute-start.9 = (bf16[4,128,128]{2,1,0:T(8,128)(2,1)S(1)}, bf16[4,128,128]{2,1,0:T(8,128)(2,1)S(1)}, u32[]{:S(2)}, u32[]{:S(2)}) collective-permute-start(bf16[4,128,128]{2,1,0:T(8,128)(2,1)S(1)} %slice.20), channel_id=1, source_target_pairs={{0,16},{8,72},{16,32},{24,88},{32,48},{40,104},{48,0},{56,120},{64... | collective-permute-start | bytes 393224 | tf_op jit(solution)/shard_map/ppermute | solution.py:240
  28.0 22.2 %collective-permute-start.8 = (bf16[3,8,128,128]{3,2,1,0:T(8,128)(2,1)S(1)}, bf16[3,8,128,128]{3,2,1,0:T(8,128)(2,1)S(1)}, u32[]{:S(2)}, u32[]{:S(2)}) collective-permute-start(bf16[3,8,128,128]{3,2,1,0:T(8,128)(2,1)S(1)} %pad_maximum_fusion.refs_0_), channel_id=1, source_target_pairs={{0,192},{8,56},{16,208},{24,8},{32,224},{40,24},{48,240},{56,40},{... | collective-permute-start | bytes 2359304 | tf_op jit(solution)/shard_map/ppermute | solution.py:240
  31.3 12.1 %all-to-all-start = ((bf16[16,16,512]{2,1,0:T(8,128)(2,1)}), bf16[16,16,512]{2,1,0:T(8,128)(2,1)S(1)}, u32[]{:S(2)}, u32[]{:S(2)}) async-start(bf16[16,16,512]{2,1,0:T(8,128)(2,1)} %fusion), calls=%async_computation | async-start | bytes 524288 | tf_op jit(solution)/shard_map/all_to_all | solution.py:262
  35.6 18.9 %collective-permute-start.6 = (bf16[3,8,128,128]{3,2,1,0:T(8,128)(2,1)S(1)}, bf16[3,8,128,128]{3,2,1,0:T(8,128)(2,1)S(1)}, u32[]{:S(2)}, u32[]{:S(2)}) collective-permute-start(bf16[3,8,128,128]{3,2,1,0:T(8,128)(2,1)S(1)} %pad_maximum_fusion.refs_0_), channel_id=1, source_target_pairs={{0,64},{8,24},{16,80},{24,40},{32,96},{40,56},{48,112},{56,8},{64,... | collective-permute-start | bytes 2359304 | tf_op jit(solution)/shard_map/ppermute | solution.py:240
  37.0 13.2 %collective-permute-start.11 = (bf16[1,8,128,128]{3,2,1,0:T(8,128)(2,1)S(1)}, bf16[1,8,128,128]{3,2,1,0:T(8,128)(2,1)S(1)}, u32[]{:S(2)}, u32[]{:S(2)}) collective-permute-start(bf16[1,8,128,128]{3,2,1,0:T(8,128)(2,1)S(1)} %maximum_bitcast_fusion.refs_1_), channel_id=1, source_target_pairs={{0,192},{8,56},{16,208},{24,8},{32,224},{40,24},{48,240},{56,40},{... | collective-permute-start | bytes 786440 | tf_op jit(solution)/shard_map/ppermute | solution.py:240
  38.5 16.2 %collective-permute-start.13 = (bf16[1,8,128,128]{3,2,1,0:T(8,128)(2,1)S(1)}, bf16[1,8,128,128]{3,2,1,0:T(8,128)(2,1)S(1)}, u32[]{:S(2)}, u32[]{:S(2)}) collective-permute-start(bf16[1,8,128,128]{3,2,1,0:T(8,128)(2,1)S(1)} %maximum_bitcast_fusion.refs_1_), channel_id=1, source_target_pairs={{0,64},{8,24},{16,80},{24,40},{32,96},{40,56},{48,112},{56,8},{64,... | collective-permute-start | bytes 786440 | tf_op jit(solution)/shard_map/ppermute | solution.py:240
  50.3 18.0 %collective-permute-start.12 = (bf16[2,8,128,128]{3,2,1,0:T(8,128)(2,1)S(1)}, bf16[2,8,128,128]{3,2,1,0:T(8,128)(2,1)S(1)}, u32[]{:S(2)}, u32[]{:S(2)}) collective-permute-start(bf16[2,8,128,128]{3,2,1,0:T(8,128)(2,1)S(1)} %pad_maximum_fusion.1), channel_id=1, source_target_pairs={{0,192},{8,56},{16,208},{24,8},{32,224},{40,24},{48,240},{56,40},{... | collective-permute-start | bytes 1572872 | tf_op jit(solution)/shard_map/ppermute | solution.py:240
  54.6 13.7 %collective-permute-start.7 = (bf16[2,8,128,128]{3,2,1,0:T(8,128)(2,1)S(1)}, bf16[2,8,128,128]{3,2,1,0:T(8,128)(2,1)S(1)}, u32[]{:S(2)}, u32[]{:S(2)}) collective-permute-start(bf16[2,8,128,128]{3,2,1,0:T(8,128)(2,1)S(1)} %slice.18), channel_id=1, source_target_pairs={{0,64},{8,24},{16,80},{24,40},{32,96},{40,56},{48,112},{56,8},{64,... | collective-permute-start | bytes 1572872 | tf_op jit(solution)/shard_map/ppermute | solution.py:240
  72.2 11.0 %collective-permute-start.14 = (f32[8,136,128]{2,1,0:T(8,128)S(1)}, f32[8,136,128]{2,1,0:T(8,128)S(1)}, u32[]{:S(2)}, u32[]{:S(2)}) collective-permute-start(f32[8,136,128]{2,1,0:T(8,128)S(1)} %gram.7), channel_id=1, source_target_pairs={{0,8},{8,0},{16,24},{24,16},{32,40},{40,32},{48,56},{56,48},{64,72... | collective-permute-start | bytes 1671176 | tf_op jit(solution)/shard_map/ppermute | solution.py:281
